TPU v7x, 512 devices: a 4x2x32 block of a 4x16x32 slice. The times are simulated.
512 devices in a mesh: groups: 2 (over y), expert: 64 (over z, core), hidden: 4 (over x).
Axes of the slice: x: 4, y: 2, z: 32, core: 2. Of those that a mesh axis runs over, the one named last changes fastest.
The devices are a block of a 4x16x32 slice.
Arguments:
- tokens: bfloat16 [2048, 4096], P(('groups', 'expert')), parts along dimension 0, may hold values from -6 to 6
- expert_ids: int32 [2048, 8], P(('groups', 'expert')), parts along dimension 0, may hold values from 0 to 31, all different within a row; in each aligned block of 16 rows (0 to 15, 16 to 31, ...) at most 8 rows name the same one
- router_scores: float32 [2048, 8], P(('groups', 'expert')), parts along dimension 0, may hold values from 0.05 to 1
- gate_weight: bfloat16 [64, 4096, 512], P('expert', None, 'hidden'), may hold values from -0.09375 to 0.09375
- up_weight: bfloat16 [64, 4096, 512], P('expert', None, 'hidden'), may hold values from -0.09375 to 0.09375
- down_weight: bfloat16 [64, 512, 4096], P('expert', 'hidden'), may hold values from -0.1875 to 0.1875
Outputs:
- moe_out: bfloat16 [2048, 4096], P(('groups', 'expert'), 'hidden'), parts along dimension 0
There are 2 independent parts, one for each index of `groups`. A program takes and returns all parts, laid end to end along the dimension named above; an argument that names none is the same for every part. Nothing has to cross between parts.
Inputs may be any that keep to these rules, and one draw needn't show every extreme that they name: `expert_ids`: each row names 8 different experts. In each aligned block of 16 rows no expert is named by more than 8 rows, a bound that some block reaches.
All inputs are finite; a program needn't handle non-finite values.
Results may differ from a plain program's by a relative error of at most 0.012.
Values may be sent and summed in bfloat16 or wider, within the bound.
No kernel may reach another device: no remote copies, remote signals or barrier semaphores. Data moves between devices by JAX's collectives and lax.ppermute only.
A program may use at most 64 MiB of HBM per device.

v0:
```python
import jax
import jax.numpy as jnp
from jax import lax
from jax.experimental import pallas as pl
from jax.experimental.pallas import tpu as pltpu
from jax.sharding import PartitionSpec as P


SPAN = 2
CAP = 8
F32 = jnp.float32
BF = jnp.bfloat16
VM = pltpu.MemorySpace.VMEM


def pack_kernel(x_ref, ids_ref, scores_ref, tok_ref, out_ref, weight_ref):
    top, count = ids_ref.shape
    experts, cap, part = out_ref.shape
    pairs = experts * cap
    scores = scores_ref[...]
    routed = 2.5 * scores / jnp.sum(scores, axis=0, keepdims=True)
    row = lax.broadcasted_iota(jnp.int32, (pairs, count), 0)
    expert = row // cap
    member = jnp.zeros((pairs, count), F32)
    weight = jnp.zeros((pairs, count), F32)
    for k in range(top):
        hit = ids_ref[k : k + 1, :] == expert
        member = jnp.where(hit, 1.0, member)
        weight = jnp.where(hit, routed[k : k + 1, :], weight)
    earlier = lax.broadcasted_iota(jnp.int32, (count, count), 0) < lax.broadcasted_iota(
        jnp.int32, (count, count), 1
    )
    place = jnp.dot(
        member.astype(BF), jnp.where(earlier, 1.0, 0.0).astype(BF), preferred_element_type=F32
    )
    mine = (member > 0.5) & (place == (row - expert * cap).astype(F32))
    weight_ref[...] = jnp.where(mine, weight, 0.0)
    chosen = jnp.where(mine, 1.0, 0.0).astype(BF)
    col = pl.multiple_of(x_ref[0] * part, part)
    rows = jnp.dot(chosen, tok_ref[:, pl.ds(col, part)], preferred_element_type=F32)
    for e in range(experts):
        out_ref[e] = rows[e * cap : (e + 1) * cap].astype(BF)


def pack(x, ids, scores, tokens, experts, part):
    count = tokens.shape[0]
    return pl.pallas_call(
        pack_kernel,
        out_shape=(
            jax.ShapeDtypeStruct((experts, CAP, part), BF),
            jax.ShapeDtypeStruct((experts * CAP, count), F32),
        ),
        in_specs=[pl.BlockSpec(memory_space=pltpu.MemorySpace.SMEM)] + [pl.BlockSpec(memory_space=VM)] * 3,
        out_specs=[pl.BlockSpec(memory_space=VM)] * 2,
        compiler_params=pltpu.CompilerParams(vmem_limit_bytes=24 << 20),
        name="pack",
    )(x, ids, scores, tokens)


def act_kernel(at_ref, own_ref, left_ref, right_ref, top_ref, low_ref, gate_ref, up_ref, gate2_ref, up2_ref, out_ref):
    part = own_ref.shape[1]
    width = gate_ref.shape[1]
    far = jnp.concatenate([top_ref[...], low_ref[...]], axis=0)
    val = None
    for d, rows in enumerate((own_ref[...], left_ref[...], right_ref[...], far)):
        at = pl.ds(pl.multiple_of(at_ref[d] * part, part), part)
        weights = jnp.concatenate([r[at, :] for r in (gate_ref, up_ref, gate2_ref, up2_ref)], axis=1)
        more = jnp.dot(rows, weights, preferred_element_type=F32)
        val = more if val is None else val + more
    for i in range(SPAN):
        gate = val[:, 2 * i * width : (2 * i + 1) * width]
        up = val[:, (2 * i + 1) * width : (2 * i + 2) * width]
        out_ref[i] = (gate / (1.0 + jnp.exp(-gate)) * up).astype(BF)


def act_of(at, pieces, weights):
    return pl.pallas_call(
        act_kernel,
        out_shape=jax.ShapeDtypeStruct((SPAN, pieces[0].shape[0], weights[0].shape[1]), BF),
        in_specs=[pl.BlockSpec(memory_space=pltpu.MemorySpace.SMEM)] + [pl.BlockSpec(memory_space=VM)] * 9,
        out_specs=pl.BlockSpec(memory_space=VM),
        compiler_params=pltpu.CompilerParams(vmem_limit_bytes=24 << 20),
        name="act",
    )(at, *pieces, *weights)


def down_kernel(at_ref, act_ref, own_ref, other_ref, out_ref):
    blocks, width, part = own_ref.shape
    val = None
    for slot, weights_ref in enumerate((own_ref, other_ref)):
        rows = jnp.concatenate([act_ref[at_ref[i], slot] for i in range(blocks)], axis=1)
        more = jnp.dot(rows, weights_ref[...].reshape(blocks * width, part), preferred_element_type=F32)
        val = more if val is None else val + more
    out_ref[...] = val.astype(BF)


def down_of(at, act, own, other):
    return pl.pallas_call(
        down_kernel,
        out_shape=jax.ShapeDtypeStruct((act.shape[2], own.shape[2]), BF),
        in_specs=[pl.BlockSpec(memory_space=pltpu.MemorySpace.SMEM)] + [pl.BlockSpec(memory_space=VM)] * 3,
        out_specs=pl.BlockSpec(memory_space=VM),
        compiler_params=pltpu.CompilerParams(vmem_limit_bytes=24 << 20),
        name="down",
    )(at, act, own, other)


def combine_kernel(back_ref, weight_ref, out_ref):
    experts = back_ref.shape[0]
    weight = weight_ref[...]
    high = weight.astype(BF)
    rest = weight - high.astype(F32)
    middle = rest.astype(BF)
    low = (rest - middle.astype(F32)).astype(BF)
    over_rows = (((0,), (0,)), ((), ()))
    rows = jnp.concatenate([back_ref[e].astype(F32) for e in range(experts)], axis=0).astype(BF)
    val = None
    for term in (low, middle, high):
        more = lax.dot_general(term, rows, over_rows, preferred_element_type=F32)
        val = more if val is None else val + more
    out_ref[...] = val.astype(BF)


def combine(back, weight):
    return pl.pallas_call(
        combine_kernel,
        out_shape=jax.ShapeDtypeStruct((weight.shape[1], back.shape[2]), BF),
        in_specs=[pl.BlockSpec(memory_space=VM)] * 2,
        out_specs=pl.BlockSpec(memory_space=VM),
        compiler_params=pltpu.CompilerParams(vmem_limit_bytes=24 << 20),
        name="combine",
    )(back, weight)


def body(tokens, expert_ids, router_scores, gate_weight, up_weight, down_weight):
    slots, columns = lax.axis_size("expert"), lax.axis_size("hidden")
    experts = slots // SPAN
    part = tokens.shape[1] // columns
    x = lax.axis_index("hidden").astype(jnp.int32)
    same_core = [[SPAN * z + core for z in range(experts)] for core in range(SPAN)]
    swap = [(i, i ^ 1) for i in range(slots)]

    def turned(v, s):
        return lax.ppermute(v, "hidden", [(i, (i + s) % columns) for i in range(columns)])

    def swapped(v):
        return lax.ppermute(v, "expert", swap)

    def exchanged(v):
        return lax.all_to_all(
            v, "expert", split_axis=0, concat_axis=0, tiled=True, axis_index_groups=same_core
        )

    arrived = []
    for s in range(columns):
        share = lax.dynamic_slice_in_dim(down_weight[0], (x + s) % columns * part, part, 1)
        arrived.append(turned(share, s) if s else share)
    outgoing, weight = pack(x.reshape(1), expert_ids.T, router_scores.T, tokens, experts, part)
    own = exchanged(outgoing).reshape(experts * CAP, part)
    half = experts * CAP // 2
    left, right = turned(own, 1), turned(own, columns - 1)
    gate_other, up_other = swapped(gate_weight[0]), swapped(up_weight[0])
    far_top, far_low = turned(left[:half], 1), turned(right[half:], columns - 1)
    down = jnp.stack(arrived)
    down_other = swapped(down)
    at = (x + jnp.array([0, columns - 1, 1, 2], jnp.int32)) % columns
    act = act_of(
        at, (own, left, right, far_top, far_low), (gate_weight[0], up_weight[0], gate_other, up_other)
    )
    act_all = lax.all_gather(act, "hidden", axis=0, tiled=False)
    source = (x - jnp.arange(columns, dtype=jnp.int32)) % columns
    val = down_of(source, act_all, down, down_other)
    back = exchanged(val.reshape(experts, CAP, part))
    return combine(back, weight)


def solution(mesh):
    return jax.shard_map(
        body,
        mesh=mesh,
        in_specs=(
            P(("groups", "expert"), None),
            P(("groups", "expert"), None),
            P(("groups", "expert"), None),
            P("expert", None, "hidden"),
            P("expert", None, "hidden"),
            P("expert", "hidden", None),
        ),
        out_specs=P(("groups", "expert"), "hidden"),
        check_vma=False,
    )
```

profile of v0, /device:TPU:40, one launch (start us, length us, event | category | flops | bytes accessed | tf_op | source)
XLA Modules:
  0.0 223.8 jit_solution(16174371853215996948)
XLA Ops:
  0.0 0.0 copy-start.4
  0.0 0.0 copy-start.3
  0.0 0.7 copy-done.4
  0.7 0.0 copy-done.3
  0.7 0.0 copy-start.2
  0.7 0.9 copy-done.2
  1.6 1.2 pack.1
  2.8 45.8 %all-to-all-start = ((bf16[32,8,1024]{2,1,0:T(8,128)(2,1)}), bf16[32,8,1024]{2,1,0:T(8,128)(2,1)S(1)}, u32[]{:S(2)}, u32[]{:S(2)}) async-start(bf16[32,8,1024]{2,1,0:T(8,128)(2,1)} %get-tuple-element.7), calls=%async_computation | async-start | bytes 1048576 | tf_op jit(solution)/shard_map/all_to_all | solution.py:150
  48.7 0.0 copy-start
  48.7 0.0 copy-start.1
  48.7 1.4 constant_dynamic-slice_fusion
  50.1 5.1 %collective-permute-start.8 = (bf16[128,1024]{1,0:T(8,128)(2,1)S(1)}, bf16[128,1024]{1,0:T(8,128)(2,1)}, u32[]{:S(2)}, u32[]{:S(2)}) collective-permute-start(bf16[128,1024]{1,0:T(8,128)(2,1)S(1)} %get-tuple-element.11), channel_id=1, source_target_pairs={{0,3},{1,0},{2,1},{3,2},{4,7},{5,4},{6,5},{7,6},{8,11},{9,8},{10,9... | collective-permute-start | bytes 786440 | tf_op jit(solution)/shard_map/ppermute | solution.py:144
  55.3 2.5 %collective-permute-start.7 = (bf16[128,1024]{1,0:T(8,128)(2,1)S(1)}, bf16[128,1024]{1,0:T(8,128)(2,1)}, u32[]{:S(2)}, u32[]{:S(2)}) collective-permute-start(bf16[128,1024]{1,0:T(8,128)(2,1)S(1)} %get-tuple-element.12), channel_id=1, source_target_pairs={{0,2},{1,3},{2,0},{3,1},{4,6},{5,7},{6,4},{7,5},{8,10},{9,11},{10,... | collective-permute-start | bytes 786440 | tf_op jit(solution)/shard_map/ppermute | solution.py:144
  57.7 3.0 %collective-permute-start.6 = (bf16[128,1024]{1,0:T(8,128)(2,1)S(1)}, bf16[128,1024]{1,0:T(8,128)(2,1)}, u32[]{:S(2)}, u32[]{:S(2)}) collective-permute-start(bf16[128,1024]{1,0:T(8,128)(2,1)S(1)} %get-tuple-element.10), channel_id=1, source_target_pairs={{0,1},{1,2},{2,3},{3,0},{4,5},{5,6},{6,7},{7,4},{8,9},{9,10},{10,1... | collective-permute-start | bytes 786440 | tf_op jit(solution)/shard_map/ppermute | solution.py:144
  60.7 0.0 copy-done
  60.7 2.0 collective-permute-start.4
  62.7 0.0 copy-done.1
  62.7 2.4 %collective-permute-start.5 = (bf16[4096,128]{1,0:T(8,128)(2,1)S(1)}, bf16[4096,128]{1,0:T(8,128)(2,1)}, u32[]{:S(2)}, u32[]{:S(2)}) collective-permute-start(bf16[4096,128]{1,0:T(8,128)(2,1)S(1)} %bitcast.24), channel_id=1, source_target_pairs={{0,4},{4,0},{8,12},{12,8},{16,20},{20,16},{24,28},{28,24},{32,36},... | collective-permute-start | bytes 3145736 | tf_op jit(solution)/shard_map/ppermute | solution.py:147
  65.1 1.1 collective-permute-done.8
  66.2 46.8 %all-to-all-done = bf16[32,8,1024]{2,1,0:T(8,128)(2,1)S(1)} async-done(((bf16[32,8,1024]{2,1,0:T(8,128)(2,1)}), bf16[32,8,1024]{2,1,0:T(8,128)(2,1)S(1)}, u32[]{:S(2)}, u32[]{:S(2)}) %all-to-all-start) | async-done | bytes 524320 | tf_op jit(solution)/shard_map/all_to_all | solution.py:150
  113.0 3.6 %collective-permute-start = (bf16[256,1024]{1,0:T(8,128)(2,1)S(1)}, bf16[256,1024]{1,0:T(8,128)(2,1)S(1)}, u32[]{:S(2)}, u32[]{:S(2)}) collective-permute-start(bf16[256,1024]{1,0:T(8,128)(2,1)S(1)} %bitcast.17), channel_id=1, source_target_pairs={{0,1},{1,2},{2,3},{3,0},{4,5},{5,6},{6,7},{7,4},{8,9},{9,10},{10,1... | collective-permute-start | bytes 1572872 | tf_op jit(solution)/shard_map/ppermute | solution.py:144
  116.6 0.0 collective-permute-done.7
  116.6 3.5 %collective-permute-start.1 = (bf16[256,1024]{1,0:T(8,128)(2,1)S(1)}, bf16[256,1024]{1,0:T(8,128)(2,1)S(1)}, u32[]{:S(2)}, u32[]{:S(2)}) collective-permute-start(bf16[256,1024]{1,0:T(8,128)(2,1)S(1)} %bitcast.18), channel_id=1, source_target_pairs={{0,3},{1,0},{2,1},{3,2},{4,7},{5,4},{6,5},{7,6},{8,11},{9,8},{10,9... | collective-permute-start | bytes 1572872 | tf_op jit(solution)/shard_map/ppermute | solution.py:144
  120.1 0.0 collective-permute-done.6
  120.2 1.2 pad_maximum_fusion.own_ref
  121.4 2.0 collective-permute-start.9
  123.4 5.9 %collective-permute-done.left_ref = bf16[256,1024]{1,0:T(8,128)(2,1)S(1)} collective-permute-done((bf16[256,1024]{1,0:T(8,128)(2,1)S(1)}, bf16[256,1024]{1,0:T(8,128)(2,1)S(1)}, u32[]{:S(2)}, u32[]{:S(2)}) %collective-permute-start) | collective-permute-done | bytes 524320 | tf_op jit(solution)/shard_map/ppermute | solution.py:144
  129.3 2.1 collective-permute-start.2
  131.5 0.0 collective-permute-done.1.right_ref
  131.5 0.0 copy-start.5
  131.5 5.0 %collective-permute-start.3 = (bf16[128,1024]{1,0:T(8,128)(2,1)S(1)}, bf16[128,1024]{1,0:T(8,128)(2,1)S(1)}, u32[]{:S(2)}, u32[]{:S(2)}) collective-permute-start(bf16[128,1024]{1,0:T(8,128)(2,1)S(1)} %slice.9), channel_id=1, source_target_pairs={{0,3},{1,0},{2,1},{3,2},{4,7},{5,4},{6,5},{7,6},{8,11},{9,8},{10,9... | collective-permute-start | bytes 786440 | tf_op jit(solution)/shard_map/ppermute | solution.py:144
  136.5 0.0 copy-done.5
  136.5 0.0 collective-permute-done.4.gate2_ref
  136.6 0.0 collective-permute-done.5.up2_ref
  136.6 2.6 %collective-permute-done.2.top_ref = bf16[128,1024]{1,0:T(8,128)(2,1)S(1)} collective-permute-done((bf16[128,1024]{1,0:T(8,128)(2,1)S(1)}, bf16[128,1024]{1,0:T(8,128)(2,1)S(1)}, u32[]{:S(2)}, u32[]{:S(2)}) %collective-permute-start.2) | collective-permute-done | bytes 262176 | tf_op jit(solution)/shard_map/ppermute | solution.py:144
  139.2 1.3 collective-permute-done.3.low_ref
  140.4 2.8 %act.1 = bf16[2,256,128]{2,1,0:T(8,128)(2,1)S(1)} custom-call(s32[4]{0:T(128)S(1)} %and_select_fusion.at_ref, bf16[256,1024]{1,0:T(8,128)(2,1)S(1)} %bitcast.19, bf16[256,1024]{1,0:T(8,128)(2,1)S(1)} %collective-permute-done.left_ref, bf16[256,1024]{1,0:T(8,128)(2,1)S(1)} %collective-permute-done.1.right_ref, ...), custom_call_target="tpu_custom_call" | custom-call | tf_op jit(solution)/shard_map/act/pallas_call | solution.py:77
  143.2 14.0 %all-gather = bf16[8,256,128]{2,1,0:T(8,128)(2,1)S(1)} all-gather(bf16[2,256,128]{2,1,0:T(8,128)(2,1)S(1)} %act.1), channel_id=2, replica_groups=mesh['groups'=2,'expert'=64,'hidden'=4] {'hidden'}, dimensions={0}, use_global_device_ids=true | all-gather | bytes 655360 | tf_op jit(solution)/shard_map/all_gather | solution.py:170
  157.3 0.0 collective-permute-done.9.other_ref
  157.3 1.2 down.1
  158.5 64.3 %all_to_all.10.back_ref = bf16[32,8,1024]{2,1,0:T(8,128)(2,1)S(1)} all-to-all(bf16[32,8,1024]{2,1,0:T(8,128)(2,1)S(1)} %bitcast.21), channel_id=1, replica_groups={{0,8,16,24,32,40,48,56,64,72,80,88,96,104,112,120,128,136,144,152,160,1..., dimensions={0} | all-to-all | bytes 1048576 | tf_op jit(solution)/shard_map/all_to_all | solution.py:150
  222.8 1.0 combine.1
  (4 shorter events, 0.1 us)
Async XLA Ops:
  0.0 0.7 copy-start.4
  0.0 0.7 copy-start.3
  0.7 0.9 copy-start.2
  2.8 110.2 %all-to-all-start = ((bf16[32,8,1024]{2,1,0:T(8,128)(2,1)}), bf16[32,8,1024]{2,1,0:T(8,128)(2,1)S(1)}, u32[]{:S(2)}, u32[]{:S(2)}) async-start(bf16[32,8,1024]{2,1,0:T(8,128)(2,1)} %get-tuple-element.7), calls=%async_computation | async-start | bytes 1048576 | tf_op jit(solution)/shard_map/all_to_all | solution.py:150
  48.7 12.0 %copy-start = (bf16[1,4096,128]{2,1,0:T(8,128)(2,1)S(1)}, bf16[1,4096,128]{2,1,0:T(8,128)(2,1)}, u32[]{:S(2)}) copy-start(bf16[1,4096,128]{2,1,0:T(8,128)(2,1)} %param.10) | copy-start | bytes 3145732
  48.7 14.0 %copy-start.1 = (bf16[1,4096,128]{2,1,0:T(8,128)(2,1)S(1)}, bf16[1,4096,128]{2,1,0:T(8,128)(2,1)}, u32[]{:S(2)}) copy-start(bf16[1,4096,128]{2,1,0:T(8,128)(2,1)} %param.11) | copy-start | bytes 3145732
  50.1 16.1 %collective-permute-start.8 = (bf16[128,1024]{1,0:T(8,128)(2,1)S(1)}, bf16[128,1024]{1,0:T(8,128)(2,1)}, u32[]{:S(2)}, u32[]{:S(2)}) collective-permute-start(bf16[128,1024]{1,0:T(8,128)(2,1)S(1)} %get-tuple-element.11), channel_id=1, source_target_pairs={{0,3},{1,0},{2,1},{3,2},{4,7},{5,4},{6,5},{7,6},{8,11},{9,8},{10,9... | collective-permute-start | bytes 786440 | tf_op jit(solution)/shard_map/ppermute | solution.py:144
  55.3 61.3 %collective-permute-start.7 = (bf16[128,1024]{1,0:T(8,128)(2,1)S(1)}, bf16[128,1024]{1,0:T(8,128)(2,1)}, u32[]{:S(2)}, u32[]{:S(2)}) collective-permute-start(bf16[128,1024]{1,0:T(8,128)(2,1)S(1)} %get-tuple-element.12), channel_id=1, source_target_pairs={{0,2},{1,3},{2,0},{3,1},{4,6},{5,7},{6,4},{7,5},{8,10},{9,11},{10,... | collective-permute-start | bytes 786440 | tf_op jit(solution)/shard_map/ppermute | solution.py:144
  57.7 62.4 %collective-permute-start.6 = (bf16[128,1024]{1,0:T(8,128)(2,1)S(1)}, bf16[128,1024]{1,0:T(8,128)(2,1)}, u32[]{:S(2)}, u32[]{:S(2)}) collective-permute-start(bf16[128,1024]{1,0:T(8,128)(2,1)S(1)} %get-tuple-element.10), channel_id=1, source_target_pairs={{0,1},{1,2},{2,3},{3,0},{4,5},{5,6},{6,7},{7,4},{8,9},{9,10},{10,1... | collective-permute-start | bytes 786440 | tf_op jit(solution)/shard_map/ppermute | solution.py:144
  60.7 75.8 %collective-permute-start.4 = (bf16[4096,128]{1,0:T(8,128)(2,1)S(1)}, bf16[4096,128]{1,0:T(8,128)(2,1)}, u32[]{:S(2)}, u32[]{:S(2)}) collective-permute-start(bf16[4096,128]{1,0:T(8,128)(2,1)S(1)} %bitcast.22), channel_id=1, source_target_pairs={{0,4},{4,0},{8,12},{12,8},{16,20},{20,16},{24,28},{28,24},{32,36},... | collective-permute-start | bytes 3145736 | tf_op jit(solution)/shard_map/ppermute | solution.py:147
  62.7 73.9 %collective-permute-start.5 = (bf16[4096,128]{1,0:T(8,128)(2,1)S(1)}, bf16[4096,128]{1,0:T(8,128)(2,1)}, u32[]{:S(2)}, u32[]{:S(2)}) collective-permute-start(bf16[4096,128]{1,0:T(8,128)(2,1)S(1)} %bitcast.24), channel_id=1, source_target_pairs={{0,4},{4,0},{8,12},{12,8},{16,20},{20,16},{24,28},{28,24},{32,36},... | collective-permute-start | bytes 3145736 | tf_op jit(solution)/shard_map/ppermute | solution.py:147
  113.0 16.3 %collective-permute-start = (bf16[256,1024]{1,0:T(8,128)(2,1)S(1)}, bf16[256,1024]{1,0:T(8,128)(2,1)S(1)}, u32[]{:S(2)}, u32[]{:S(2)}) collective-permute-start(bf16[256,1024]{1,0:T(8,128)(2,1)S(1)} %bitcast.17), channel_id=1, source_target_pairs={{0,1},{1,2},{2,3},{3,0},{4,5},{5,6},{6,7},{7,4},{8,9},{9,10},{10,1... | collective-permute-start | bytes 1572872 | tf_op jit(solution)/shard_map/ppermute | solution.py:144
  116.6 14.9 %collective-permute-start.1 = (bf16[256,1024]{1,0:T(8,128)(2,1)S(1)}, bf16[256,1024]{1,0:T(8,128)(2,1)S(1)}, u32[]{:S(2)}, u32[]{:S(2)}) collective-permute-start(bf16[256,1024]{1,0:T(8,128)(2,1)S(1)} %bitcast.18), channel_id=1, source_target_pairs={{0,3},{1,0},{2,1},{3,2},{4,7},{5,4},{6,5},{7,6},{8,11},{9,8},{10,9... | collective-permute-start | bytes 1572872 | tf_op jit(solution)/shard_map/ppermute | solution.py:144
  121.4 35.9 %collective-permute-start.9 = (bf16[4,128,1024]{2,1,0:T(8,128)(2,1)S(1)}, bf16[4,128,1024]{2,1,0:T(8,128)(2,1)S(1)}, u32[]{:S(2)}, u32[]{:S(2)}) collective-permute-start(bf16[4,128,1024]{2,1,0:T(8,128)(2,1)S(1)} %pad_maximum_fusion.own_ref), channel_id=1, source_target_pairs={{0,4},{4,0},{8,12},{12,8},{16,20},{20,16},{24,28},{28,24},{32,36},... | collective-permute-start | bytes 3145736 | tf_op jit(solution)/shard_map/ppermute | solution.py:147
  129.3 9.8 %collective-permute-start.2 = (bf16[128,1024]{1,0:T(8,128)(2,1)S(1)}, bf16[128,1024]{1,0:T(8,128)(2,1)S(1)}, u32[]{:S(2)}, u32[]{:S(2)}) collective-permute-start(bf16[128,1024]{1,0:T(8,128)(2,1)S(1)} %slice.8), channel_id=1, source_target_pairs={{0,1},{1,2},{2,3},{3,0},{4,5},{5,6},{6,7},{7,4},{8,9},{9,10},{10,1... | collective-permute-start | bytes 786440 | tf_op jit(solution)/shard_map/ppermute | solution.py:144
  131.5 5.0 %copy-start.5 = (s32[4]{0:T(128)S(1)}, s32[4]{0:T(128)}, u32[]{:S(2)}) copy-start(s32[4]{0:T(128)} %constant.58.clone) | copy-start | bytes 52
  131.5 8.9 %collective-permute-start.3 = (bf16[128,1024]{1,0:T(8,128)(2,1)S(1)}, bf16[128,1024]{1,0:T(8,128)(2,1)S(1)}, u32[]{:S(2)}, u32[]{:S(2)}) collective-permute-start(bf16[128,1024]{1,0:T(8,128)(2,1)S(1)} %slice.9), channel_id=1, source_target_pairs={{0,3},{1,0},{2,1},{3,2},{4,7},{5,4},{6,5},{7,6},{8,11},{9,8},{10,9... | collective-permute-start | bytes 786440 | tf_op jit(solution)/shard_map/ppermute | solution.py:144
where the time goes:
time: 225 us; the launch traced here: 224 us
  blocking collectives  78.3 us (35%)
  starting transfers between devices  76.9 us (34%)
  waiting for transfers between devices  57.7 us (26%)
  Pallas kernels  6.26 us (3%)
  local copies, waits for them, and re-layouts  3.1 us (1%)
    all_to_all x1, blocking collectives, exchanged(): lax.all_to_all(v, 'expert', split_axis=0, concat_axis=0, tiled=True, axis...  64.3 us
    all_to_all x1, waiting for transfers between devices, exchanged(): lax.all_to_all(v, 'expert', split_axis=0, concat_axis=0, tiled=True, axis...  46.8 us
    all_to_all x1, starting transfers between devices, exchanged(): lax.all_to_all(v, 'expert', split_axis=0, concat_axis=0, tiled=True, axis...  45.8 us
    ppermute x7, starting transfers between devices, turned(): lax.ppermute(v, 'hidden', [(i, (i + s) % columns) for i in range(columns)])  24.8 us
    all_gather x1, blocking collectives, body(): act_all = lax.all_gather(act, 'hidden', axis=0, tiled=False)  14 us
    ppermute x7, waiting for transfers between devices, turned(): lax.ppermute(v, 'hidden', [(i, (i + s) % columns) for i in range(columns)])  10.9 us
    ppermute x3, starting transfers between devices, swapped(): return lax.ppermute(v, 'expert', swap)  6.34 us
  transfers between devices with their start and end apart: 11, of which 5 were waited for; matrix products, arithmetic and copies ran while one was open for 1% of the time, Pallas kernels for 1%

commit v1 on v0

v1 whole, which is shorter than its diff:
```python
import jax
import jax.numpy as jnp
from jax import lax
from jax.experimental import pallas as pl
from jax.experimental.pallas import tpu as pltpu
from jax.sharding import PartitionSpec as P


SPAN = 2
CAP = 8
CHUNKS = 2
F32 = jnp.float32
BF = jnp.bfloat16
VM = pltpu.MemorySpace.VMEM


def params():
    return pltpu.CompilerParams(vmem_limit_bytes=24 << 20)


def specs(count):
    return [pl.BlockSpec(memory_space=VM)] * count


def pack_kernel(x_ref, ids_ref, scores_ref, tok_ref, *out_refs):
    top, count = ids_ref.shape
    experts, cap, part = out_refs[0].shape
    pairs, quad = experts * cap, cap // CHUNKS
    scores = scores_ref[...]
    routed = 2.5 * scores / jnp.sum(scores, axis=0, keepdims=True)
    row = lax.broadcasted_iota(jnp.int32, (pairs, count), 0)
    expert = row // cap
    member = jnp.zeros((pairs, count), F32)
    weight = jnp.zeros((pairs, count), F32)
    for k in range(top):
        hit = ids_ref[k : k + 1, :] == expert
        member = jnp.where(hit, 1.0, member)
        weight = jnp.where(hit, routed[k : k + 1, :], weight)
    earlier = lax.broadcasted_iota(jnp.int32, (count, count), 0) < lax.broadcasted_iota(
        jnp.int32, (count, count), 1
    )
    place = jnp.dot(
        member.astype(BF), jnp.where(earlier, 1.0, 0.0).astype(BF), preferred_element_type=F32
    )
    first = lax.broadcasted_iota(jnp.int32, (pairs, part), 0) % cap < quad
    tokens = [
        tok_ref[:, pl.ds(pl.multiple_of(x_ref[0] * (2 * part) + h * part, part), part)] for h in range(2)
    ]
    for q in range(CHUNKS):
        mine = (member > 0.5) & (place == (row % quad + q * quad).astype(F32))
        out_refs[CHUNKS + q][...] = jnp.where(mine, weight, 0.0)
        chosen = jnp.where(mine, 1.0, 0.0).astype(BF)
        low, high = (jnp.dot(chosen, t, preferred_element_type=F32) for t in tokens)
        rows = jnp.where(first, low, high)
        for e in range(experts):
            out_refs[q][e] = rows[e * cap : (e + 1) * cap].astype(BF)


def pack(x, ids, scores, tokens, experts, part):
    count = tokens.shape[0]
    return pl.pallas_call(
        pack_kernel,
        out_shape=[jax.ShapeDtypeStruct((experts, CAP, part), BF)] * CHUNKS
        + [jax.ShapeDtypeStruct((experts * CAP, count), F32)] * CHUNKS,
        in_specs=[pl.BlockSpec(memory_space=pltpu.MemorySpace.SMEM)] + specs(3),
        out_specs=specs(2 * CHUNKS),
        compiler_params=params(),
        name="pack",
    )(x, ids, scores, tokens)


def picker(rows, half, across):
    quad = CAP // CHUNKS
    shape = (2 * rows, rows) if across else (rows, 2 * rows)
    i = lax.broadcasted_iota(jnp.int32, shape, 1 if across else 0)
    j = lax.broadcasted_iota(jnp.int32, shape, 0 if across else 1)
    return jnp.where(j == i // quad * CAP + half * quad + i % quad, 1.0, 0.0).astype(BF)


def act_kernel(at_ref, own_ref, left_ref, right_ref, top_ref, low_ref, gate_ref, up_ref, gate2_ref, up2_ref, out_ref):
    part = own_ref.shape[1]
    width = gate_ref.shape[1]
    far = jnp.concatenate([top_ref[...], low_ref[...]], axis=0)
    pick = [picker(own_ref.shape[0] // 2, h, False) for h in range(2)]
    val = None
    for d, rows in enumerate((own_ref[...], left_ref[...], right_ref[...], far)):
        for h in range(2):
            at = pl.ds(pl.multiple_of(at_ref[d] * (2 * part) + h * part, part), part)
            weights = jnp.concatenate([r[at, :] for r in (gate_ref, up_ref, gate2_ref, up2_ref)], axis=1)
            compact = jnp.dot(pick[h], rows, preferred_element_type=F32).astype(BF)
            more = jnp.dot(compact, weights, preferred_element_type=F32)
            val = more if val is None else val + more
    for i in range(SPAN):
        gate = val[:, 2 * i * width : (2 * i + 1) * width]
        up = val[:, (2 * i + 1) * width : (2 * i + 2) * width]
        out_ref[i] = (gate / (1.0 + jnp.exp(-gate)) * up).astype(BF)


def act_of(at, pieces, weights):
    return pl.pallas_call(
        act_kernel,
        out_shape=jax.ShapeDtypeStruct((SPAN, pieces[0].shape[0] // 2, weights[0].shape[1]), BF),
        in_specs=[pl.BlockSpec(memory_space=pltpu.MemorySpace.SMEM)] + specs(9),
        out_specs=pl.BlockSpec(memory_space=VM),
        compiler_params=params(),
        name="act",
    )(at, *pieces, *weights)


def down_kernel(at_ref, act_ref, own_ref, other_ref, out_ref):
    blocks, width, part = own_ref.shape
    count, half = act_ref.shape[2], part // 2
    val = None
    for slot, weights_ref in enumerate((own_ref, other_ref)):
        rows = jnp.concatenate([act_ref[at_ref[i], slot] for i in range(blocks)], axis=1)
        more = jnp.dot(rows, weights_ref[...].reshape(blocks * width, part), preferred_element_type=F32)
        val = more if val is None else val + more
    val = val.astype(BF)
    out = jnp.dot(picker(count, 0, True), val[:, :half], preferred_element_type=F32)
    out = out + jnp.dot(picker(count, 1, True), val[:, half:], preferred_element_type=F32)
    out_ref[...] = out.astype(BF)


def down_of(at, act, own, other):
    return pl.pallas_call(
        down_kernel,
        out_shape=jax.ShapeDtypeStruct((2 * act.shape[2], own.shape[2] // 2), BF),
        in_specs=[pl.BlockSpec(memory_space=pltpu.MemorySpace.SMEM)] + specs(3),
        out_specs=pl.BlockSpec(memory_space=VM),
        compiler_params=params(),
        name="down",
    )(at, act, own, other)


def combine_kernel(*refs):
    back_refs, weight_refs, out_ref = refs[:CHUNKS], refs[CHUNKS : 2 * CHUNKS], refs[2 * CHUNKS]
    experts, cap, part = back_refs[0].shape
    quad = cap // CHUNKS
    over_rows = (((0,), (0,)), ((), ()))
    val = [None, None]
    for back_ref, weight_ref in zip(back_refs, weight_refs):
        rows = jnp.concatenate([back_ref[e].astype(F32) for e in range(experts)], axis=0).astype(BF)
        weight = weight_ref[...]
        first = lax.broadcasted_iota(jnp.int32, weight.shape, 0) % cap < quad
        for h in range(2):
            part_weight = jnp.where(first == (h == 0), weight, 0.0)
            high = part_weight.astype(BF)
            rest = part_weight - high.astype(F32)
            middle = rest.astype(BF)
            low = (rest - middle.astype(F32)).astype(BF)
            for term in (low, middle, high):
                more = lax.dot_general(term, rows, over_rows, preferred_element_type=F32)
                val[h] = more if val[h] is None else val[h] + more
    for h in range(2):
        out_ref[:, h * part : (h + 1) * part] = val[h].astype(BF)


def combine(backs, weights):
    return pl.pallas_call(
        combine_kernel,
        out_shape=jax.ShapeDtypeStruct((weights[0].shape[1], 2 * backs[0].shape[2]), BF),
        in_specs=specs(2 * CHUNKS),
        out_specs=pl.BlockSpec(memory_space=VM),
        compiler_params=params(),
        name="combine",
    )(*backs, *weights)


def body(tokens, expert_ids, router_scores, gate_weight, up_weight, down_weight):
    slots, columns = lax.axis_size("expert"), lax.axis_size("hidden")
    experts = slots // SPAN
    width = tokens.shape[1] // columns
    part = width // 2
    x = lax.axis_index("hidden").astype(jnp.int32)
    same_core = [[SPAN * z + core for z in range(experts)] for core in range(SPAN)]
    swap = [(i, i ^ 1) for i in range(slots)]

    def turned(v, s):
        return lax.ppermute(v, "hidden", [(i, (i + s) % columns) for i in range(columns)])

    def swapped(v):
        return lax.ppermute(v, "expert", swap)

    def exchanged(v):
        return lax.all_to_all(
            v, "expert", split_axis=0, concat_axis=0, tiled=True, axis_index_groups=same_core
        )

    packed = pack(x.reshape(1), expert_ids.T, router_scores.T, tokens, experts, part)
    outgoing, weights = packed[:CHUNKS], packed[CHUNKS:]
    arrived = []
    for s in range(columns):
        share = lax.dynamic_slice_in_dim(down_weight[0], (x + s) % columns * width, width, 1)
        arrived.append(turned(share, s) if s else share)
    gate_other, up_other = swapped(gate_weight[0]), swapped(up_weight[0])
    down = jnp.stack(arrived)
    down_other = swapped(down)
    at = (x + jnp.array([0, columns - 1, 1, 2], jnp.int32)) % columns
    source = (x - jnp.arange(columns, dtype=jnp.int32)) % columns
    mine = []
    for q in range(CHUNKS):
        mine.append(exchanged(outgoing[q]).reshape(experts * CAP, part))
    half = experts * CAP // 2
    backs = []
    for q in range(CHUNKS):
        own = mine[q]
        left, right = turned(own, 1), turned(own, columns - 1)
        far_top, far_low = turned(left[:half], 1), turned(right[half:], columns - 1)
        act = act_of(
            at, (own, left, right, far_top, far_low), (gate_weight[0], up_weight[0], gate_other, up_other)
        )
        act_all = lax.all_gather(act, "hidden", axis=0, tiled=False)
        val = down_of(source, act_all, down, down_other)
        backs.append(exchanged(val.reshape(experts, CAP, part)))
    return combine(backs, weights)


def solution(mesh):
    return jax.shard_map(
        body,
        mesh=mesh,
        in_specs=(
            P(("groups", "expert"), None),
            P(("groups", "expert"), None),
            P(("groups", "expert"), None),
            P("expert", None, "hidden"),
            P("expert", None, "hidden"),
            P("expert", "hidden", None),
        ),
        out_specs=P(("groups", "expert"), "hidden"),
        check_vma=False,
    )
```

time: 225 us -> 273 us (1.21)
  blocking collectives: 78.3 us -> 167 us
  waiting for transfers between devices: 57.7 us -> 15.4 us
  Pallas kernels: 6.26 us -> 10.3 us
  starting transfers between devices: 76.9 us -> 73 us
  local copies, waits for them, and re-layouts: 3.1 us -> 6.17 us
    all_to_all x1 -> x2, blocking collectives: 64.3 us -> 141 us  [exchanged(): lax.all_to_all(v, 'expert', split_axis=0, concat_axis=0, tiled=True, axis...]
    all_to_all x1 -> x2, waiting for transfers between devices: 46.8 us -> 0.01 us  [exchanged(): lax.all_to_all(v, 'expert', split_axis=0, concat_axis=0, tiled=True, axis...]
    all_to_all x1 -> x2, starting transfers between devices: 45.8 us -> 26.8 us  [exchanged(): lax.all_to_all(v, 'expert', split_axis=0, concat_axis=0, tiled=True, axis...]
    ppermute x7 -> x11, starting transfers between devices: 24.8 us -> 39.8 us  [turned(): lax.ppermute(v, 'hidden', [(i, (i + s) % columns) for i in range(columns)])]
    all_gather x1 -> x2, blocking collectives: 14 us -> 25.1 us  [body(): act_all = lax.all_gather(act, 'hidden', axis=0, tiled=False)]
    ppermute x7 -> x11, waiting for transfers between devices: 10.9 us -> 15.4 us  [turned(): lax.ppermute(v, 'hidden', [(i, (i + s) % columns) for i in range(columns)])]
    unnamed x12 -> x32, local copies, waits for them, and re-layouts: 1.62 us -> 6.04 us
    pallas_call x3 -> x4, Pallas kernels: 3.44 us -> 5.77 us  [the longest x2 2.5 us: down_of(): pl.pallas_call(down_kernel, out_shape=jax.ShapeDtypeStruct((2 * act.shape...]
  transfers between devices with their start and end apart: 11 -> 16, of which waited for: 5 -> 8; matrix products, arithmetic and copies ran while one was open for 1% -> 0% of each run, Pallas kernels for 1% -> 3%
where the time goes in v1:
time: 273 us; the launch traced here: 272 us
  blocking collectives  167 us (61%)
  starting transfers between devices  73 us (27%)
  waiting for transfers between devices  15.4 us (6%)
  Pallas kernels  10.3 us (4%)
  local copies, waits for them, and re-layouts  6.17 us (2%)
    all_to_all x2, blocking collectives, exchanged(): lax.all_to_all(v, 'expert', split_axis=0, concat_axis=0, tiled=True, axis...  141 us
    ppermute x11, starting transfers between devices, turned(): lax.ppermute(v, 'hidden', [(i, (i + s) % columns) for i in range(columns)])  39.8 us
    all_to_all x2, starting transfers between devices, exchanged(): lax.all_to_all(v, 'expert', split_axis=0, concat_axis=0, tiled=True, axis...  26.8 us
    all_gather x2, blocking collectives, body(): act_all = lax.all_gather(act, 'hidden', axis=0, tiled=False)  25.1 us
    ppermute x11, waiting for transfers between devices, turned(): lax.ppermute(v, 'hidden', [(i, (i + s) % columns) for i in range(columns)])  15.4 us
    ppermute x3, starting transfers between devices, swapped(): return lax.ppermute(v, 'expert', swap)  6.34 us
    unnamed x32, local copies, waits for them, and re-layouts  6.04 us
  transfers between devices with their start and end apart: 16, of which 8 were waited for; matrix products, arithmetic and copies ran while one was open for 0% of the time, Pallas kernels for 3%

profile of v1, /device:TPU:40, one launch (start us, length us, event | category | flops | bytes accessed | tf_op | source)
XLA Modules:
  0.0 272.0 jit_solution(15759833886973841318)
XLA Ops:
  0.0 0.7 copy-done.13
  0.7 0.0 copy-done.12
  0.7 0.9 copy-done.11
  1.6 1.1 pack.1
  2.8 87.6 %all_to_all.20 = bf16[32,8,512]{2,1,0:T(8,128)(2,1)} all-to-all(bf16[32,8,512]{2,1,0:T(8,128)(2,1)S(1)} %get-tuple-element.10), channel_id=1, replica_groups={{0,8,16,24,32,40,48,56,64,72,80,88,96,104,112,120,128,136,144,152,160,1..., dimensions={0} | all-to-all | bytes 524288 | tf_op jit(solution)/shard_map/all_to_all | solution.py:185
  90.3 4.8 %all-to-all-start = ((bf16[32,8,512]{2,1,0:T(8,128)(2,1)}), bf16[32,8,512]{2,1,0:T(8,128)(2,1)S(1)}, u32[]{:S(2)}, u32[]{:S(2)}) async-start(bf16[32,8,512]{2,1,0:T(8,128)(2,1)} %get-tuple-element.9), calls=%async_computation | async-start | bytes 524288 | tf_op jit(solution)/shard_map/all_to_all | solution.py:185
  95.2 0.0 copy-start
  95.2 0.0 copy-start.1
  95.2 0.1 constant_dynamic-slice_fusion
  95.3 5.4 %collective-permute-start.7 = (bf16[128,1024]{1,0:T(8,128)(2,1)S(1)}, bf16[128,1024]{1,0:T(8,128)(2,1)S(1)}, u32[]{:S(2)}, u32[]{:S(2)}) collective-permute-start(bf16[128,1024]{1,0:T(8,128)(2,1)S(1)} %get-tuple-element.16), channel_id=1, source_target_pairs={{0,2},{1,3},{2,0},{3,1},{4,6},{5,7},{6,4},{7,5},{8,10},{9,11},{10,... | collective-permute-start | bytes 786440 | tf_op jit(solution)/shard_map/ppermute | solution.py:179
  100.7 3.0 %collective-permute-start.8 = (bf16[128,1024]{1,0:T(8,128)(2,1)S(1)}, bf16[128,1024]{1,0:T(8,128)(2,1)S(1)}, u32[]{:S(2)}, u32[]{:S(2)}) collective-permute-start(bf16[128,1024]{1,0:T(8,128)(2,1)S(1)} %get-tuple-element.15), channel_id=1, source_target_pairs={{0,3},{1,0},{2,1},{3,2},{4,7},{5,4},{6,5},{7,6},{8,11},{9,8},{10,9... | collective-permute-start | bytes 786440 | tf_op jit(solution)/shard_map/ppermute | solution.py:179
  103.6 3.0 %collective-permute-start.6 = (bf16[128,1024]{1,0:T(8,128)(2,1)S(1)}, bf16[128,1024]{1,0:T(8,128)(2,1)S(1)}, u32[]{:S(2)}, u32[]{:S(2)}) collective-permute-start(bf16[128,1024]{1,0:T(8,128)(2,1)S(1)} %get-tuple-element.14), channel_id=1, source_target_pairs={{0,1},{1,2},{2,3},{3,0},{4,5},{5,6},{6,7},{7,4},{8,9},{9,10},{10,1... | collective-permute-start | bytes 786440 | tf_op jit(solution)/shard_map/ppermute | solution.py:179
  106.6 2.0 collective-permute-start.4
  108.6 2.4 collective-permute-start.5
  111.0 0.0 collective-permute-done.7
  111.0 0.8 collective-permute-done.8
  111.9 1.3 collective-permute-done.6
  113.2 0.1 pad_maximum_fusion.own_ref
  113.3 2.0 collective-permute-start.9
  115.3 2.0 collective-permute-start.10
  117.2 5.2 %collective-permute-start.11 = (bf16[256,512]{1,0:T(8,128)(2,1)S(1)}, bf16[256,512]{1,0:T(8,128)(2,1)S(1)}, u32[]{:S(2)}, u32[]{:S(2)}) collective-permute-start(bf16[256,512]{1,0:T(8,128)(2,1)S(1)} %bitcast.30), channel_id=1, source_target_pairs={{0,3},{1,0},{2,1},{3,2},{4,7},{5,4},{6,5},{7,6},{8,11},{9,8},{10,9... | collective-permute-start | bytes 786440 | tf_op jit(solution)/shard_map/ppermute | solution.py:179
  122.4 4.7 %collective-permute-done.10.left_ref = bf16[256,512]{1,0:T(8,128)(2,1)S(1)} collective-permute-done((bf16[256,512]{1,0:T(8,128)(2,1)S(1)}, bf16[256,512]{1,0:T(8,128)(2,1)S(1)}, u32[]{:S(2)}, u32[]{:S(2)}) %collective-permute-start.10) | collective-permute-done | bytes 262176 | tf_op jit(solution)/shard_map/ppermute | solution.py:179
  127.1 0.0 copy-start.15
  127.1 2.0 collective-permute-start.12
  129.1 5.2 %collective-permute-start.13 = (bf16[128,512]{1,0:T(8,128)(2,1)S(1)}, bf16[128,512]{1,0:T(8,128)(2,1)S(1)}, u32[]{:S(2)}, u32[]{:S(2)}) collective-permute-start(bf16[128,512]{1,0:T(8,128)(2,1)S(1)} %slice.19), channel_id=1, source_target_pairs={{0,3},{1,0},{2,1},{3,2},{4,7},{5,4},{6,5},{7,6},{8,11},{9,8},{10,9... | collective-permute-start | bytes 393224 | tf_op jit(solution)/shard_map/ppermute | solution.py:179
  134.3 0.0 collective-permute-done.4.gate2_ref
  134.4 0.9 collective-permute-done.12.top_ref
  135.3 1.5 collective-permute-done.13.low_ref
  136.8 2.3 act.3
  139.1 12.8 %all-gather.1 = bf16[8,128,128]{2,1,0:T(8,128)(2,1)S(1)} all-gather(bf16[2,128,128]{2,1,0:T(8,128)(2,1)S(1)} %act.3), channel_id=3, replica_groups=mesh['groups'=2,'expert'=64,'hidden'=4] {'hidden'}, dimensions={0}, use_global_device_ids=true | all-gather | bytes 327680 | tf_op jit(solution)/shard_map/all_gather | solution.py:212
  151.9 1.2 down.3
  153.1 0.7 copy-done.8
  153.9 22.0 %all-to-all-start.3 = ((bf16[32,8,512]{2,1,0:T(8,128)(2,1)}), bf16[32,8,512]{2,1,0:T(8,128)(2,1)}, u32[]{:S(2)}, u32[]{:S(2)}) async-start(bf16[32,8,512]{2,1,0:T(8,128)(2,1)} %bitcast.34), calls=%async_computation.3 | async-start | bytes 524288 | tf_op jit(solution)/shard_map/all_to_all | solution.py:185
  175.9 3.9 %collective-permute-start = (bf16[256,512]{1,0:T(8,128)(2,1)S(1)}, bf16[256,512]{1,0:T(8,128)(2,1)S(1)}, u32[]{:S(2)}, u32[]{:S(2)}) collective-permute-start(bf16[256,512]{1,0:T(8,128)(2,1)S(1)} %bitcast.26), channel_id=1, source_target_pairs={{0,1},{1,2},{2,3},{3,0},{4,5},{5,6},{6,7},{7,4},{8,9},{9,10},{10,1... | collective-permute-start | bytes 786440 | tf_op jit(solution)/shard_map/ppermute | solution.py:179
  179.8 3.2 %collective-permute-start.1 = (bf16[256,512]{1,0:T(8,128)(2,1)S(1)}, bf16[256,512]{1,0:T(8,128)(2,1)S(1)}, u32[]{:S(2)}, u32[]{:S(2)}) collective-permute-start(bf16[256,512]{1,0:T(8,128)(2,1)S(1)} %bitcast.27), channel_id=1, source_target_pairs={{0,3},{1,0},{2,1},{3,2},{4,7},{5,4},{6,5},{7,6},{8,11},{9,8},{10,9... | collective-permute-start | bytes 786440 | tf_op jit(solution)/shard_map/ppermute | solution.py:179
  183.0 2.4 collective-permute-done.left_ref
  185.5 4.0 %collective-permute-start.2 = (bf16[128,512]{1,0:T(8,128)(2,1)S(1)}, bf16[128,512]{1,0:T(8,128)(2,1)S(1)}, u32[]{:S(2)}, u32[]{:S(2)}) collective-permute-start(bf16[128,512]{1,0:T(8,128)(2,1)S(1)} %slice.16), channel_id=1, source_target_pairs={{0,1},{1,2},{2,3},{3,0},{4,5},{5,6},{6,7},{7,4},{8,9},{9,10},{10,1... | collective-permute-start | bytes 393224 | tf_op jit(solution)/shard_map/ppermute | solution.py:179
  189.5 3.2 %collective-permute-start.3 = (bf16[128,512]{1,0:T(8,128)(2,1)S(1)}, bf16[128,512]{1,0:T(8,128)(2,1)S(1)}, u32[]{:S(2)}, u32[]{:S(2)}) collective-permute-start(bf16[128,512]{1,0:T(8,128)(2,1)S(1)} %slice.17), channel_id=1, source_target_pairs={{0,3},{1,0},{2,1},{3,2},{4,7},{5,4},{6,5},{7,6},{8,11},{9,8},{10,9... | collective-permute-start | bytes 393224 | tf_op jit(solution)/shard_map/ppermute | solution.py:179
  192.7 0.9 collective-permute-done.2.top_ref
  193.6 2.8 %collective-permute-done.3.low_ref = bf16[128,512]{1,0:T(8,128)(2,1)S(1)} collective-permute-done((bf16[128,512]{1,0:T(8,128)(2,1)S(1)}, bf16[128,512]{1,0:T(8,128)(2,1)S(1)}, u32[]{:S(2)}, u32[]{:S(2)}) %collective-permute-start.3) | collective-permute-done | bytes 131104 | tf_op jit(solution)/shard_map/ppermute | solution.py:179
  196.4 1.2 copy-done.2
  197.7 1.2 copy-done.4
  198.9 1.2 copy-done.6
  200.1 2.3 act.2
  202.4 12.3 %all-gather = bf16[8,128,128]{2,1,0:T(8,128)(2,1)S(1)} all-gather(bf16[2,128,128]{2,1,0:T(8,128)(2,1)S(1)} %act.2), channel_id=2, replica_groups=mesh['groups'=2,'expert'=64,'hidden'=4] {'hidden'}, dimensions={0}, use_global_device_ids=true | all-gather | bytes 327680 | tf_op jit(solution)/shard_map/all_gather | solution.py:212
  214.7 1.3 down.2
  216.0 53.9 %all_to_all.21.refs_0_ = bf16[32,8,512]{2,1,0:T(8,128)(2,1)S(1)} all-to-all(bf16[32,8,512]{2,1,0:T(8,128)(2,1)S(1)} %bitcast.35), channel_id=1, replica_groups={{0,8,16,24,32,40,48,56,64,72,80,88,96,104,112,120,128,136,144,152,160,1..., dimensions={0} | all-to-all | bytes 524288 | tf_op jit(solution)/shard_map/all_to_all | solution.py:185
  269.9 2.1 combine.1
  (34 shorter events, 0.1 us)
Async XLA Ops:
  0.0 0.7 copy-start.13
  0.0 0.7 copy-start.12
  0.7 0.9 copy-start.11
  1.6 93.6 %copy-start.14 = (bf16[1,128,4096]{2,1,0:T(8,128)(2,1)S(1)}, bf16[1,128,4096]{2,1,0:T(8,128)(2,1)}, u32[]{:S(2)}) copy-start(bf16[1,128,4096]{2,1,0:T(8,128)(2,1)} %param.12) | copy-start | bytes 3145732
  2.8 87.6 %copy-start.9 = (f32[256,16]{1,0:T(8,128)}, f32[256,16]{1,0:T(8,128)S(1)}, u32[]{:S(2)}) copy-start(f32[256,16]{1,0:T(8,128)S(1)} %get-tuple-element.12.refs_3_) | copy-start | bytes 49156
  90.3 63.5 %all-to-all-start = ((bf16[32,8,512]{2,1,0:T(8,128)(2,1)}), bf16[32,8,512]{2,1,0:T(8,128)(2,1)S(1)}, u32[]{:S(2)}, u32[]{:S(2)}) async-start(bf16[32,8,512]{2,1,0:T(8,128)(2,1)} %get-tuple-element.9), calls=%async_computation | async-start | bytes 524288 | tf_op jit(solution)/shard_map/all_to_all | solution.py:185
  95.2 11.4 %copy-start = (bf16[1,4096,128]{2,1,0:T(8,128)(2,1)S(1)}, bf16[1,4096,128]{2,1,0:T(8,128)(2,1)}, u32[]{:S(2)}) copy-start(bf16[1,4096,128]{2,1,0:T(8,128)(2,1)} %param.10) | copy-start | bytes 3145732
  95.2 13.4 %copy-start.1 = (bf16[1,4096,128]{2,1,0:T(8,128)(2,1)S(1)}, bf16[1,4096,128]{2,1,0:T(8,128)(2,1)}, u32[]{:S(2)}) copy-start(bf16[1,4096,128]{2,1,0:T(8,128)(2,1)} %param.11) | copy-start | bytes 3145732
  95.3 15.7 %collective-permute-start.7 = (bf16[128,1024]{1,0:T(8,128)(2,1)S(1)}, bf16[128,1024]{1,0:T(8,128)(2,1)S(1)}, u32[]{:S(2)}, u32[]{:S(2)}) collective-permute-start(bf16[128,1024]{1,0:T(8,128)(2,1)S(1)} %get-tuple-element.16), channel_id=1, source_target_pairs={{0,2},{1,3},{2,0},{3,1},{4,6},{5,7},{6,4},{7,5},{8,10},{9,11},{10,... | collective-permute-start | bytes 786440 | tf_op jit(solution)/shard_map/ppermute | solution.py:179
  100.7 11.2 %collective-permute-start.8 = (bf16[128,1024]{1,0:T(8,128)(2,1)S(1)}, bf16[128,1024]{1,0:T(8,128)(2,1)S(1)}, u32[]{:S(2)}, u32[]{:S(2)}) collective-permute-start(bf16[128,1024]{1,0:T(8,128)(2,1)S(1)} %get-tuple-element.15), channel_id=1, source_target_pairs={{0,3},{1,0},{2,1},{3,2},{4,7},{5,4},{6,5},{7,6},{8,11},{9,8},{10,9... | collective-permute-start | bytes 786440 | tf_op jit(solution)/shard_map/ppermute | solution.py:179
  103.6 9.5 %collective-permute-start.6 = (bf16[128,1024]{1,0:T(8,128)(2,1)S(1)}, bf16[128,1024]{1,0:T(8,128)(2,1)S(1)}, u32[]{:S(2)}, u32[]{:S(2)}) collective-permute-start(bf16[128,1024]{1,0:T(8,128)(2,1)S(1)} %get-tuple-element.14), channel_id=1, source_target_pairs={{0,1},{1,2},{2,3},{3,0},{4,5},{5,6},{6,7},{7,4},{8,9},{9,10},{10,1... | collective-permute-start | bytes 786440 | tf_op jit(solution)/shard_map/ppermute | solution.py:179
  106.6 27.7 %collective-permute-start.4 = (bf16[4096,128]{1,0:T(8,128)(2,1)S(1)}, bf16[4096,128]{1,0:T(8,128)(2,1)S(1)}, u32[]{:S(2)}, u32[]{:S(2)}) collective-permute-start(bf16[4096,128]{1,0:T(8,128)(2,1)S(1)} %bitcast.20), channel_id=1, source_target_pairs={{0,4},{4,0},{8,12},{12,8},{16,20},{20,16},{24,28},{28,24},{32,36},... | collective-permute-start | bytes 3145736 | tf_op jit(solution)/shard_map/ppermute | solution.py:182
  108.6 25.8 %collective-permute-start.5 = (bf16[4096,128]{1,0:T(8,128)(2,1)S(1)}, bf16[4096,128]{1,0:T(8,128)(2,1)S(1)}, u32[]{:S(2)}, u32[]{:S(2)}) collective-permute-start(bf16[4096,128]{1,0:T(8,128)(2,1)S(1)} %bitcast.23), channel_id=1, source_target_pairs={{0,4},{4,0},{8,12},{12,8},{16,20},{20,16},{24,28},{28,24},{32,36},... | collective-permute-start | bytes 3145736 | tf_op jit(solution)/shard_map/ppermute | solution.py:182
  113.2 2.1 copy-start.7
  113.3 38.6 %collective-permute-start.9 = (bf16[4,128,1024]{2,1,0:T(8,128)(2,1)S(1)}, bf16[4,128,1024]{2,1,0:T(8,128)(2,1)S(1)}, u32[]{:S(2)}, u32[]{:S(2)}) collective-permute-start(bf16[4,128,1024]{2,1,0:T(8,128)(2,1)S(1)} %pad_maximum_fusion.own_ref), channel_id=1, source_target_pairs={{0,4},{4,0},{8,12},{12,8},{16,20},{20,16},{24,28},{28,24},{32,36},... | collective-permute-start | bytes 3145736 | tf_op jit(solution)/shard_map/ppermute | solution.py:182
  115.3 11.8 %collective-permute-start.10 = (bf16[256,512]{1,0:T(8,128)(2,1)S(1)}, bf16[256,512]{1,0:T(8,128)(2,1)S(1)}, u32[]{:S(2)}, u32[]{:S(2)}) collective-permute-start(bf16[256,512]{1,0:T(8,128)(2,1)S(1)} %bitcast.29), channel_id=1, source_target_pairs={{0,1},{1,2},{2,3},{3,0},{4,5},{5,6},{6,7},{7,4},{8,9},{9,10},{10,1... | collective-permute-start | bytes 786440 | tf_op jit(solution)/shard_map/ppermute | solution.py:179
  117.2 11.9 %collective-permute-start.11 = (bf16[256,512]{1,0:T(8,128)(2,1)S(1)}, bf16[256,512]{1,0:T(8,128)(2,1)S(1)}, u32[]{:S(2)}, u32[]{:S(2)}) collective-permute-start(bf16[256,512]{1,0:T(8,128)(2,1)S(1)} %bitcast.30), channel_id=1, source_target_pairs={{0,3},{1,0},{2,1},{3,2},{4,7},{5,4},{6,5},{7,6},{8,11},{9,8},{10,9... | collective-permute-start | bytes 786440 | tf_op jit(solution)/shard_map/ppermute | solution.py:179
  127.1 7.2 %copy-start.15 = (s32[4]{0:T(128)S(1)}, s32[4]{0:T(128)}, u32[]{:S(2)}) copy-start(s32[4]{0:T(128)} %constant.58.clone) | copy-start | bytes 52
  127.1 8.2 %collective-permute-start.12 = (bf16[128,512]{1,0:T(8,128)(2,1)S(1)}, bf16[128,512]{1,0:T(8,128)(2,1)S(1)}, u32[]{:S(2)}, u32[]{:S(2)}) collective-permute-start(bf16[128,512]{1,0:T(8,128)(2,1)S(1)} %slice.18), channel_id=1, source_target_pairs={{0,1},{1,2},{2,3},{3,0},{4,5},{5,6},{6,7},{7,4},{8,9},{9,10},{10,1... | collective-permute-start | bytes 393224 | tf_op jit(solution)/shard_map/ppermute | solution.py:179
  129.1 7.7 %collective-permute-start.13 = (bf16[128,512]{1,0:T(8,128)(2,1)S(1)}, bf16[128,512]{1,0:T(8,128)(2,1)S(1)}, u32[]{:S(2)}, u32[]{:S(2)}) collective-permute-start(bf16[128,512]{1,0:T(8,128)(2,1)S(1)} %slice.19), channel_id=1, source_target_pairs={{0,3},{1,0},{2,1},{3,2},{4,7},{5,4},{6,5},{7,6},{8,11},{9,8},{10,9... | collective-permute-start | bytes 393224 | tf_op jit(solution)/shard_map/ppermute | solution.py:179
  134.3 4.7 %copy-start.3 = (bf16[4096,128]{1,0:T(8,128)(2,1)}, bf16[4096,128]{1,0:T(8,128)(2,1)S(1)}, u32[]{:S(2)}) copy-start(bf16[4096,128]{1,0:T(8,128)(2,1)S(1)} %collective-permute-done.4.gate2_ref) | copy-start | bytes 3145732
  134.4 4.7 %copy-start.5 = (bf16[4096,128]{1,0:T(8,128)(2,1)}, bf16[4096,128]{1,0:T(8,128)(2,1)S(1)}, u32[]{:S(2)}) copy-start(bf16[4096,128]{1,0:T(8,128)(2,1)S(1)} %collective-permute-done.5.up2_ref) | copy-start | bytes 3145732
  153.1 0.7 copy-start.8
  153.9 62.1 %all-to-all-start.3 = ((bf16[32,8,512]{2,1,0:T(8,128)(2,1)}), bf16[32,8,512]{2,1,0:T(8,128)(2,1)}, u32[]{:S(2)}, u32[]{:S(2)}) async-start(bf16[32,8,512]{2,1,0:T(8,128)(2,1)} %bitcast.34), calls=%async_computation.3 | async-start | bytes 524288 | tf_op jit(solution)/shard_map/all_to_all | solution.py:185
  175.9 9.6 %collective-permute-start = (bf16[256,512]{1,0:T(8,128)(2,1)S(1)}, bf16[256,512]{1,0:T(8,128)(2,1)S(1)}, u32[]{:S(2)}, u32[]{:S(2)}) collective-permute-start(bf16[256,512]{1,0:T(8,128)(2,1)S(1)} %bitcast.26), channel_id=1, source_target_pairs={{0,1},{1,2},{2,3},{3,0},{4,5},{5,6},{6,7},{7,4},{8,9},{9,10},{10,1... | collective-permute-start | bytes 786440 | tf_op jit(solution)/shard_map/ppermute | solution.py:179
  179.8 9.7 %collective-permute-start.1 = (bf16[256,512]{1,0:T(8,128)(2,1)S(1)}, bf16[256,512]{1,0:T(8,128)(2,1)S(1)}, u32[]{:S(2)}, u32[]{:S(2)}) collective-permute-start(bf16[256,512]{1,0:T(8,128)(2,1)S(1)} %bitcast.27), channel_id=1, source_target_pairs={{0,3},{1,0},{2,1},{3,2},{4,7},{5,4},{6,5},{7,6},{8,11},{9,8},{10,9... | collective-permute-start | bytes 786440 | tf_op jit(solution)/shard_map/ppermute | solution.py:179
  185.5 8.2 %collective-permute-start.2 = (bf16[128,512]{1,0:T(8,128)(2,1)S(1)}, bf16[128,512]{1,0:T(8,128)(2,1)S(1)}, u32[]{:S(2)}, u32[]{:S(2)}) collective-permute-start(bf16[128,512]{1,0:T(8,128)(2,1)S(1)} %slice.16), channel_id=1, source_target_pairs={{0,1},{1,2},{2,3},{3,0},{4,5},{5,6},{6,7},{7,4},{8,9},{9,10},{10,1... | collective-permute-start | bytes 393224 | tf_op jit(solution)/shard_map/ppermute | solution.py:179
  189.5 6.9 %collective-permute-start.3 = (bf16[128,512]{1,0:T(8,128)(2,1)S(1)}, bf16[128,512]{1,0:T(8,128)(2,1)S(1)}, u32[]{:S(2)}, u32[]{:S(2)}) collective-permute-start(bf16[128,512]{1,0:T(8,128)(2,1)S(1)} %slice.17), channel_id=1, source_target_pairs={{0,3},{1,0},{2,1},{3,2},{4,7},{5,4},{6,5},{7,6},{8,11},{9,8},{10,9... | collective-permute-start | bytes 393224 | tf_op jit(solution)/shard_map/ppermute | solution.py:179
  196.4 1.2 copy-start.2
  197.6 1.2 copy-start.4
  198.9 1.2 copy-start.6
  216.0 53.9 %copy-start.10 = (f32[256,16]{1,0:T(8,128)S(1)}, f32[256,16]{1,0:T(8,128)}, u32[]{:S(2)}) copy-start(f32[256,16]{1,0:T(8,128)} %copy-done.9) | copy-start | bytes 49156

commit v2 on v0

--- a/solution.py
+++ b/solution.py
@@ -57,31 +57,49 @@
     )(x, ids, scores, tokens)
 
 
-def act_kernel(at_ref, own_ref, left_ref, right_ref, top_ref, low_ref, gate_ref, up_ref, gate2_ref, up2_ref, out_ref):
-    part = own_ref.shape[1]
-    width = gate_ref.shape[1]
-    far = jnp.concatenate([top_ref[...], low_ref[...]], axis=0)
-    val = None
-    for d, rows in enumerate((own_ref[...], left_ref[...], right_ref[...], far)):
-        at = pl.ds(pl.multiple_of(at_ref[d] * part, part), part)
-        weights = jnp.concatenate([r[at, :] for r in (gate_ref, up_ref, gate2_ref, up2_ref)], axis=1)
-        more = jnp.dot(rows, weights, preferred_element_type=F32)
-        val = more if val is None else val + more
+def partial_kernel(at_ref, rows_ref, own_ref, other_ref, out_ref):
+    rows = rows_ref[...]
+    for s in range(own_ref.shape[0]):
+        weights = jnp.concatenate([r[s, i] for r in (own_ref, other_ref) for i in range(2)], axis=1)
+        out_ref[at_ref[s]] = jnp.dot(rows, weights, preferred_element_type=F32).astype(BF)
+
+
+def partial_of(at, rows, own, other):
+    blocks, _, _, width = own.shape
+    return pl.pallas_call(
+        partial_kernel,
+        out_shape=jax.ShapeDtypeStruct((blocks, rows.shape[0], 2 * SPAN * width), BF),
+        in_specs=[pl.BlockSpec(memory_space=pltpu.MemorySpace.SMEM)] + [pl.BlockSpec(memory_space=VM)] * 3,
+        out_specs=pl.BlockSpec(memory_space=VM),
+        compiler_params=pltpu.CompilerParams(vmem_limit_bytes=24 << 20),
+        name="partial",
+    )(at, rows, own, other)
+
+
+def act_kernel(parts_ref, out_ref):
+    blocks = parts_ref.shape[0]
+    width = out_ref.shape[3]
+    val = parts_ref[0].astype(F32)
+    for i in range(1, blocks):
+        val = val + parts_ref[i].astype(F32)
     for i in range(SPAN):
         gate = val[:, 2 * i * width : (2 * i + 1) * width]
         up = val[:, (2 * i + 1) * width : (2 * i + 2) * width]
-        out_ref[i] = (gate / (1.0 + jnp.exp(-gate)) * up).astype(BF)
-
-
-def act_of(at, pieces, weights):
+        act = (gate / (1.0 + jnp.exp(-gate)) * up).astype(BF)
+        for copy in range(blocks):
+            out_ref[copy, i] = act
+
+
+def act_of(parts):
+    blocks, count, width = parts.shape
     return pl.pallas_call(
         act_kernel,
-        out_shape=jax.ShapeDtypeStruct((SPAN, pieces[0].shape[0], weights[0].shape[1]), BF),
-        in_specs=[pl.BlockSpec(memory_space=pltpu.MemorySpace.SMEM)] + [pl.BlockSpec(memory_space=VM)] * 9,
+        out_shape=jax.ShapeDtypeStruct((blocks, SPAN, count, width // (2 * SPAN)), BF),
+        in_specs=[pl.BlockSpec(memory_space=VM)],
         out_specs=pl.BlockSpec(memory_space=VM),
         compiler_params=pltpu.CompilerParams(vmem_limit_bytes=24 << 20),
         name="act",
-    )(at, *pieces, *weights)
+    )(parts)
 
 
 def down_kernel(at_ref, act_ref, own_ref, other_ref, out_ref):
@@ -151,24 +169,25 @@
             v, "expert", split_axis=0, concat_axis=0, tiled=True, axis_index_groups=same_core
         )
 
-    arrived = []
+    def over_columns(v):
+        return lax.all_to_all(v, "hidden", split_axis=0, concat_axis=0, tiled=True)
+
+    downs, others = [], []
     for s in range(columns):
-        share = lax.dynamic_slice_in_dim(down_weight[0], (x + s) % columns * part, part, 1)
-        arrived.append(turned(share, s) if s else share)
+        at = (x + s) % columns * part
+        share = lax.dynamic_slice_in_dim(down_weight[0], at, part, 1)
+        both = jnp.stack([lax.dynamic_slice_in_dim(w[0], at, part, 0) for w in (gate_weight, up_weight)])
+        downs.append(turned(share, s) if s else share)
+        others.append(turned(both, s) if s else both)
+    down = jnp.stack(downs)
+    wide = jnp.stack(others)
+    wide_other = swapped(wide)
+    down_other = swapped(down)
     outgoing, weight = pack(x.reshape(1), expert_ids.T, router_scores.T, tokens, experts, part)
     own = exchanged(outgoing).reshape(experts * CAP, part)
-    half = experts * CAP // 2
-    left, right = turned(own, 1), turned(own, columns - 1)
-    gate_other, up_other = swapped(gate_weight[0]), swapped(up_weight[0])
-    far_top, far_low = turned(left[:half], 1), turned(right[half:], columns - 1)
-    down = jnp.stack(arrived)
-    down_other = swapped(down)
-    at = (x + jnp.array([0, columns - 1, 1, 2], jnp.int32)) % columns
-    act = act_of(
-        at, (own, left, right, far_top, far_low), (gate_weight[0], up_weight[0], gate_other, up_other)
-    )
-    act_all = lax.all_gather(act, "hidden", axis=0, tiled=False)
     source = (x - jnp.arange(columns, dtype=jnp.int32)) % columns
+    parts = over_columns(partial_of(source, own, wide, wide_other))
+    act_all = over_columns(act_of(parts))
     val = down_of(source, act_all, down, down_other)
     back = exchanged(val.reshape(experts, CAP, part))
     return combine(back, weight)

time: 225 us -> 220 us (0.978)
  blocking collectives: 78.3 us -> 67.8 us
  local copies, waits for them, and re-layouts: 3.1 us -> 7.66 us
  starting transfers between devices: 76.9 us -> 80.6 us
  waiting for transfers between devices: 57.7 us -> 54.3 us
    all_to_all x1, waiting for transfers between devices: 46.8 us -> 16.5 us  [exchanged(): lax.all_to_all(v, 'expert', split_axis=0, concat_axis=0, tiled=True, axis...]
    all_to_all x0 -> x2, waiting for transfers between devices: none -> 19.1 us  [over_columns(): return lax.all_to_all(v, 'hidden', split_axis=0, concat_axis=0, tiled=True)]
    all_gather x1 -> x0, blocking collectives: 14 us -> none  [body(): act_all = lax.all_gather(act, 'hidden', axis=0, tiled=False)]
    all_to_all x0 -> x2, starting transfers between devices: none -> 8.14 us  [over_columns(): return lax.all_to_all(v, 'hidden', split_axis=0, concat_axis=0, tiled=True)]
    ppermute x7 -> x6, waiting for transfers between devices: 10.9 us -> 18.7 us  [turned(): lax.ppermute(v, 'hidden', [(i, (i + s) % columns) for i in range(columns)])]
    unnamed x12, local copies, waits for them, and re-layouts: 1.62 us -> 5.19 us
    all_to_all x1, blocking collectives: 64.3 us -> 67.8 us  [exchanged(): lax.all_to_all(v, 'expert', split_axis=0, concat_axis=0, tiled=True, axis...]
    ppermute x3 -> x2, starting transfers between devices: 6.34 us -> 4.03 us  [swapped(): return lax.ppermute(v, 'expert', swap)]
  transfers between devices with their start and end apart: 11 -> 11, of which waited for: 5 -> 6; matrix products, arithmetic and copies ran while one was open for 1% -> 2% of each run, Pallas kernels for 1% -> 2%
where the time goes in v2:
time: 220 us
  starting transfers between devices  80.6 us (37%)
  blocking collectives  67.8 us (31%)
  waiting for transfers between devices  54.3 us (25%)
  local copies, waits for them, and re-layouts  7.66 us (3%)
  Pallas kernels  7.25 us (3%)
    all_to_all x1, blocking collectives, exchanged(): lax.all_to_all(v, 'expert', split_axis=0, concat_axis=0, tiled=True, axis...  67.8 us
    all_to_all x1, starting transfers between devices, exchanged(): lax.all_to_all(v, 'expert', split_axis=0, concat_axis=0, tiled=True, axis...  45.8 us
    ppermute x6, starting transfers between devices, turned(): lax.ppermute(v, 'hidden', [(i, (i + s) % columns) for i in range(columns)])  22.7 us
    all_to_all x2, waiting for transfers between devices, over_columns(): return lax.all_to_all(v, 'hidden', split_axis=0, concat_axis=0, tiled=True)  19.1 us
    ppermute x6, waiting for transfers between devices, turned(): lax.ppermute(v, 'hidden', [(i, (i + s) % columns) for i in range(columns)])  18.7 us
    all_to_all x1, waiting for transfers between devices, exchanged(): lax.all_to_all(v, 'expert', split_axis=0, concat_axis=0, tiled=True, axis...  16.5 us
    all_to_all x2, starting transfers between devices, over_columns(): return lax.all_to_all(v, 'hidden', split_axis=0, concat_axis=0, tiled=True)  8.14 us
    unnamed x12, local copies, waits for them, and re-layouts  5.19 us
  transfers between devices with their start and end apart: 11, of which 6 were waited for; matrix products, arithmetic and copies ran while one was open for 2% of the time, Pallas kernels for 2%

profile of v2, /device:TPU:40, one launch (start us, length us, event | category | flops | bytes accessed | tf_op | source)
XLA Modules:
  0.0 219.6 jit_solution(11511519182701530210)
XLA Ops:
  0.0 0.0 copy-start.2
  0.0 0.9 copy-done.2
  0.9 0.0 copy-start.3
  0.9 0.7 copy-done.3
  1.6 0.0 copy-start.4
  1.6 0.7 copy-done.4
  2.3 1.2 pack.1
  3.5 45.8 %all-to-all-start = ((bf16[32,8,1024]{2,1,0:T(8,128)(2,1)}), bf16[32,8,1024]{2,1,0:T(8,128)(2,1)S(1)}, u32[]{:S(2)}, u32[]{:S(2)}) async-start(bf16[32,8,1024]{2,1,0:T(8,128)(2,1)} %get-tuple-element.7), calls=%async_computation | async-start | bytes 1048576 | tf_op jit(solution)/shard_map/all_to_all | solution.py:168
  49.3 1.7 constant_dynamic-slice_fusion.7
  51.0 0.1 pad_maximum_fusion.2
  51.0 3.6 %collective-permute-start = (bf16[2,1024,128]{2,1,0:T(8,128)(2,1)S(1)}, bf16[2,1024,128]{2,1,0:T(8,128)(2,1)S(1)}, u32[]{:S(2)}, u32[]{:S(2)}) collective-permute-start(bf16[2,1024,128]{2,1,0:T(8,128)(2,1)S(1)} %pad_maximum_fusion.2), channel_id=1, source_target_pairs={{0,1},{1,2},{2,3},{3,0},{4,5},{5,6},{6,7},{7,4},{8,9},{9,10},{10,1... | collective-permute-start | bytes 1572872 | tf_op jit(solution)/shard_map/ppermute | solution.py:162
  54.6 0.1 pad_maximum_fusion.3
  54.7 4.9 %collective-permute-start.1 = (bf16[2,1024,128]{2,1,0:T(8,128)(2,1)S(1)}, bf16[2,1024,128]{2,1,0:T(8,128)(2,1)S(1)}, u32[]{:S(2)}, u32[]{:S(2)}) collective-permute-start(bf16[2,1024,128]{2,1,0:T(8,128)(2,1)S(1)} %pad_maximum_fusion.3), channel_id=1, source_target_pairs={{0,2},{1,3},{2,0},{3,1},{4,6},{5,7},{6,4},{7,5},{8,10},{9,11},{10,... | collective-permute-start | bytes 1572872 | tf_op jit(solution)/shard_map/ppermute | solution.py:162
  59.6 0.1 pad_maximum_fusion.4
  59.7 3.2 %collective-permute-start.2 = (bf16[2,1024,128]{2,1,0:T(8,128)(2,1)S(1)}, bf16[2,1024,128]{2,1,0:T(8,128)(2,1)S(1)}, u32[]{:S(2)}, u32[]{:S(2)}) collective-permute-start(bf16[2,1024,128]{2,1,0:T(8,128)(2,1)S(1)} %pad_maximum_fusion.4), channel_id=1, source_target_pairs={{0,3},{1,0},{2,1},{3,2},{4,7},{5,4},{6,5},{7,6},{8,11},{9,8},{10,9... | collective-permute-start | bytes 1572872 | tf_op jit(solution)/shard_map/ppermute | solution.py:162
  62.9 0.1 maximum_bitcast_fusion
  63.0 5.0 %collective-permute-done = bf16[2,1024,128]{2,1,0:T(8,128)(2,1)S(1)} collective-permute-done((bf16[2,1024,128]{2,1,0:T(8,128)(2,1)S(1)}, bf16[2,1024,128]{2,1,0:T(8,128)(2,1)S(1)}, u32[]{:S(2)}, u32[]{:S(2)}) %collective-permute-start) | collective-permute-done | bytes 524320 | tf_op jit(solution)/shard_map/ppermute | solution.py:162
  68.0 12.2 %collective-permute-done.1 = bf16[2,1024,128]{2,1,0:T(8,128)(2,1)S(1)} collective-permute-done((bf16[2,1024,128]{2,1,0:T(8,128)(2,1)S(1)}, bf16[2,1024,128]{2,1,0:T(8,128)(2,1)S(1)}, u32[]{:S(2)}, u32[]{:S(2)}) %collective-permute-start.1) | collective-permute-done | bytes 524320 | tf_op jit(solution)/shard_map/ppermute | solution.py:162
  80.3 1.5 collective-permute-done.2
  81.7 0.0 copy-start.5
  81.7 0.3 pad_maximum_fusion.own_ref
  82.0 2.1 collective-permute-start.3
  84.1 0.0 copy-done.5
  84.1 0.8 constant_dynamic-slice_fusion
  84.9 5.0 %collective-permute-start.5 = (bf16[128,1024]{1,0:T(8,128)(2,1)}, bf16[128,1024]{1,0:T(8,128)(2,1)}, u32[]{:S(2)}, u32[]{:S(2)}) collective-permute-start(bf16[128,1024]{1,0:T(8,128)(2,1)} %get-tuple-element.12), channel_id=1, source_target_pairs={{0,2},{1,3},{2,0},{3,1},{4,6},{5,7},{6,4},{7,5},{8,10},{9,11},{10,... | collective-permute-start | bytes 786440 | tf_op jit(solution)/shard_map/ppermute | solution.py:162
  89.9 4.0 %collective-permute-start.6 = (bf16[128,1024]{1,0:T(8,128)(2,1)S(1)}, bf16[128,1024]{1,0:T(8,128)(2,1)}, u32[]{:S(2)}, u32[]{:S(2)}) collective-permute-start(bf16[128,1024]{1,0:T(8,128)(2,1)S(1)} %get-tuple-element.11), channel_id=1, source_target_pairs={{0,3},{1,0},{2,1},{3,2},{4,7},{5,4},{6,5},{7,6},{8,11},{9,8},{10,9... | collective-permute-start | bytes 786440 | tf_op jit(solution)/shard_map/ppermute | solution.py:162
  93.9 2.0 collective-permute-start.4
  95.9 0.0 collective-permute-done.3.other_ref
  95.9 0.0 copy-start
  95.9 1.3 copy-done
  97.2 16.5 %all-to-all-done = bf16[32,8,1024]{2,1,0:T(8,128)(2,1)S(1)} async-done(((bf16[32,8,1024]{2,1,0:T(8,128)(2,1)}), bf16[32,8,1024]{2,1,0:T(8,128)(2,1)S(1)}, u32[]{:S(2)}, u32[]{:S(2)}) %all-to-all-start) | async-done | bytes 524320 | tf_op jit(solution)/shard_map/all_to_all | solution.py:168
  113.7 0.0 copy-start.1
  113.7 1.6 copy-done.1
  115.3 2.8 %partial.1 = bf16[4,256,512]{2,1,0:T(8,128)(2,1)} custom-call(s32[4]{0:T(128)S(1)} %and_select_fusion.at_ref, bf16[256,1024]{1,0:T(8,128)(2,1)S(1)} %bitcast.19, bf16[4,2,1024,128]{3,2,1,0:T(8,128)(2,1)S(1)} %pad_maximum_fusion.own_ref, bf16[4,2,1024,128]{3,2,1,0:T(8,128)(2,1)S(1)} %copy-done.1), custom_call_target="tpu_custom_call" | custom-call | tf_op jit(solution)/shard_map/partial/pallas_call | solution.py:69
  118.1 4.6 %all-to-all-start.1 = ((bf16[4,256,512]{2,1,0:T(8,128)(2,1)}), bf16[4,256,512]{2,1,0:T(8,128)(2,1)S(1)}, u32[]{:S(2)}, u32[]{:S(2)}) async-start(bf16[4,256,512]{2,1,0:T(8,128)(2,1)} %partial.1), calls=%async_computation.1 | async-start | bytes 2097152 | tf_op jit(solution)/shard_map/all_to_all | solution.py:173
  122.7 0.0 collective-permute-done.5
  122.7 0.0 collective-permute-done.6
  122.7 0.0 collective-permute-done.4
  122.7 1.2 pad_maximum_fusion.1.own_ref
  123.9 2.0 collective-permute-start.7
  125.9 11.2 %all-to-all-done.1.parts_ref = bf16[4,256,512]{2,1,0:T(8,128)(2,1)S(1)} async-done(((bf16[4,256,512]{2,1,0:T(8,128)(2,1)}), bf16[4,256,512]{2,1,0:T(8,128)(2,1)S(1)}, u32[]{:S(2)}, u32[]{:S(2)}) %all-to-all-start.1) | async-done | bytes 1048608 | tf_op jit(solution)/shard_map/all_to_all | solution.py:173
  137.1 1.0 act.1
  138.1 3.6 %all-to-all-start.2 = ((bf16[4,2,256,128]{3,2,1,0:T(8,128)(2,1)}), bf16[4,2,256,128]{3,2,1,0:T(8,128)(2,1)S(1)}, u32[]{:S(2)}, u32[]{:S(2)}) async-start(bf16[4,2,256,128]{3,2,1,0:T(8,128)(2,1)} %act.1), calls=%async_computation.2 | async-start | bytes 1048576 | tf_op jit(solution)/shard_map/all_to_all | solution.py:173
  141.6 0.0 collective-permute-done.7.other_ref
  141.6 8.0 %all-to-all-done.2.act_ref = bf16[4,2,256,128]{3,2,1,0:T(8,128)(2,1)S(1)} async-done(((bf16[4,2,256,128]{3,2,1,0:T(8,128)(2,1)}), bf16[4,2,256,128]{3,2,1,0:T(8,128)(2,1)S(1)}, u32[]{:S(2)}, u32[]{:S(2)}) %all-to-all-start.2) | async-done | bytes 524320 | tf_op jit(solution)/shard_map/all_to_all | solution.py:173
  149.6 1.2 down.1
  150.9 67.8 %all_to_all.20.back_ref = bf16[32,8,1024]{2,1,0:T(8,128)(2,1)S(1)} all-to-all(bf16[32,8,1024]{2,1,0:T(8,128)(2,1)S(1)} %bitcast.20), channel_id=1, replica_groups={{0,8,16,24,32,40,48,56,64,72,80,88,96,104,112,120,128,136,144,152,160,1..., dimensions={0} | all-to-all | bytes 1048576 | tf_op jit(solution)/shard_map/all_to_all | solution.py:168
  218.7 1.0 combine.1
  (1 shorter events, 0.0 us)
Async XLA Ops:
  0.0 0.9 copy-start.2
  0.9 0.7 copy-start.3
  1.6 0.7 copy-start.4
  3.5 110.2 %all-to-all-start = ((bf16[32,8,1024]{2,1,0:T(8,128)(2,1)}), bf16[32,8,1024]{2,1,0:T(8,128)(2,1)S(1)}, u32[]{:S(2)}, u32[]{:S(2)}) async-start(bf16[32,8,1024]{2,1,0:T(8,128)(2,1)} %get-tuple-element.7), calls=%async_computation | async-start | bytes 1048576 | tf_op jit(solution)/shard_map/all_to_all | solution.py:168
  51.0 17.0 %collective-permute-start = (bf16[2,1024,128]{2,1,0:T(8,128)(2,1)S(1)}, bf16[2,1024,128]{2,1,0:T(8,128)(2,1)S(1)}, u32[]{:S(2)}, u32[]{:S(2)}) collective-permute-start(bf16[2,1024,128]{2,1,0:T(8,128)(2,1)S(1)} %pad_maximum_fusion.2), channel_id=1, source_target_pairs={{0,1},{1,2},{2,3},{3,0},{4,5},{5,6},{6,7},{7,4},{8,9},{9,10},{10,1... | collective-permute-start | bytes 1572872 | tf_op jit(solution)/shard_map/ppermute | solution.py:162
  54.7 25.6 %collective-permute-start.1 = (bf16[2,1024,128]{2,1,0:T(8,128)(2,1)S(1)}, bf16[2,1024,128]{2,1,0:T(8,128)(2,1)S(1)}, u32[]{:S(2)}, u32[]{:S(2)}) collective-permute-start(bf16[2,1024,128]{2,1,0:T(8,128)(2,1)S(1)} %pad_maximum_fusion.3), channel_id=1, source_target_pairs={{0,2},{1,3},{2,0},{3,1},{4,6},{5,7},{6,4},{7,5},{8,10},{9,11},{10,... | collective-permute-start | bytes 1572872 | tf_op jit(solution)/shard_map/ppermute | solution.py:162
  59.7 22.0 %collective-permute-start.2 = (bf16[2,1024,128]{2,1,0:T(8,128)(2,1)S(1)}, bf16[2,1024,128]{2,1,0:T(8,128)(2,1)S(1)}, u32[]{:S(2)}, u32[]{:S(2)}) collective-permute-start(bf16[2,1024,128]{2,1,0:T(8,128)(2,1)S(1)} %pad_maximum_fusion.4), channel_id=1, source_target_pairs={{0,3},{1,0},{2,1},{3,2},{4,7},{5,4},{6,5},{7,6},{8,11},{9,8},{10,9... | collective-permute-start | bytes 1572872 | tf_op jit(solution)/shard_map/ppermute | solution.py:162
  81.7 2.4 %copy-start.5 = (bf16[1,128,4096]{2,1,0:T(8,128)(2,1)S(1)}, bf16[1,128,4096]{2,1,0:T(8,128)(2,1)}, u32[]{:S(2)}) copy-start(bf16[1,128,4096]{2,1,0:T(8,128)(2,1)} %param.11) | copy-start | bytes 3145732
  82.0 13.9 %collective-permute-start.3 = (bf16[4,2,1024,128]{3,2,1,0:T(8,128)(2,1)S(1)}, bf16[4,2,1024,128]{3,2,1,0:T(8,128)(2,1)S(1)}, u32[]{:S(2)}, u32[]{:S(2)}) collective-permute-start(bf16[4,2,1024,128]{3,2,1,0:T(8,128)(2,1)S(1)} %pad_maximum_fusion.own_ref), channel_id=1, source_target_pairs={{0,4},{4,0},{8,12},{12,8},{16,20},{20,16},{24,28},{28,24},{32,36},... | collective-permute-start | bytes 6291464 | tf_op jit(solution)/shard_map/ppermute | solution.py:165
  84.9 37.8 %collective-permute-start.5 = (bf16[128,1024]{1,0:T(8,128)(2,1)}, bf16[128,1024]{1,0:T(8,128)(2,1)}, u32[]{:S(2)}, u32[]{:S(2)}) collective-permute-start(bf16[128,1024]{1,0:T(8,128)(2,1)} %get-tuple-element.12), channel_id=1, source_target_pairs={{0,2},{1,3},{2,0},{3,1},{4,6},{5,7},{6,4},{7,5},{8,10},{9,11},{10,... | collective-permute-start | bytes 786440 | tf_op jit(solution)/shard_map/ppermute | solution.py:162
  89.9 32.8 %collective-permute-start.6 = (bf16[128,1024]{1,0:T(8,128)(2,1)S(1)}, bf16[128,1024]{1,0:T(8,128)(2,1)}, u32[]{:S(2)}, u32[]{:S(2)}) collective-permute-start(bf16[128,1024]{1,0:T(8,128)(2,1)S(1)} %get-tuple-element.11), channel_id=1, source_target_pairs={{0,3},{1,0},{2,1},{3,2},{4,7},{5,4},{6,5},{7,6},{8,11},{9,8},{10,9... | collective-permute-start | bytes 786440 | tf_op jit(solution)/shard_map/ppermute | solution.py:162
  93.9 28.8 %collective-permute-start.4 = (bf16[128,1024]{1,0:T(8,128)(2,1)S(1)}, bf16[128,1024]{1,0:T(8,128)(2,1)}, u32[]{:S(2)}, u32[]{:S(2)}) collective-permute-start(bf16[128,1024]{1,0:T(8,128)(2,1)S(1)} %get-tuple-element.10), channel_id=1, source_target_pairs={{0,1},{1,2},{2,3},{3,0},{4,5},{5,6},{6,7},{7,4},{8,9},{9,10},{10,1... | collective-permute-start | bytes 786440 | tf_op jit(solution)/shard_map/ppermute | solution.py:162
  95.9 1.3 copy-start
  113.7 1.6 copy-start.1
  118.1 19.0 %all-to-all-start.1 = ((bf16[4,256,512]{2,1,0:T(8,128)(2,1)}), bf16[4,256,512]{2,1,0:T(8,128)(2,1)S(1)}, u32[]{:S(2)}, u32[]{:S(2)}) async-start(bf16[4,256,512]{2,1,0:T(8,128)(2,1)} %partial.1), calls=%async_computation.1 | async-start | bytes 2097152 | tf_op jit(solution)/shard_map/all_to_all | solution.py:173
  123.9 17.7 %collective-permute-start.7 = (bf16[4,128,1024]{2,1,0:T(8,128)(2,1)S(1)}, bf16[4,128,1024]{2,1,0:T(8,128)(2,1)S(1)}, u32[]{:S(2)}, u32[]{:S(2)}) collective-permute-start(bf16[4,128,1024]{2,1,0:T(8,128)(2,1)S(1)} %pad_maximum_fusion.1.own_ref), channel_id=1, source_target_pairs={{0,4},{4,0},{8,12},{12,8},{16,20},{20,16},{24,28},{28,24},{32,36},... | collective-permute-start | bytes 3145736 | tf_op jit(solution)/shard_map/ppermute | solution.py:165
  138.1 11.6 %all-to-all-start.2 = ((bf16[4,2,256,128]{3,2,1,0:T(8,128)(2,1)}), bf16[4,2,256,128]{3,2,1,0:T(8,128)(2,1)S(1)}, u32[]{:S(2)}, u32[]{:S(2)}) async-start(bf16[4,2,256,128]{3,2,1,0:T(8,128)(2,1)} %act.1), calls=%async_computation.2 | async-start | bytes 1048576 | tf_op jit(solution)/shard_map/all_to_all | solution.py:173

commit v3 on v2

--- a/solution.py
+++ b/solution.py
@@ -11,6 +11,10 @@
 F32 = jnp.float32
 BF = jnp.bfloat16
 VM = pltpu.MemorySpace.VMEM
+
+
+def stride(experts):
+    return max(1, experts // 2 - 1)
 
 
 def pack_kernel(x_ref, ids_ref, scores_ref, tok_ref, out_ref, weight_ref):
@@ -20,7 +24,7 @@
     scores = scores_ref[...]
     routed = 2.5 * scores / jnp.sum(scores, axis=0, keepdims=True)
     row = lax.broadcasted_iota(jnp.int32, (pairs, count), 0)
-    expert = row // cap
+    expert = row // cap * stride(experts) % experts
     member = jnp.zeros((pairs, count), F32)
     weight = jnp.zeros((pairs, count), F32)
     for k in range(top):
@@ -33,7 +37,7 @@
     place = jnp.dot(
         member.astype(BF), jnp.where(earlier, 1.0, 0.0).astype(BF), preferred_element_type=F32
     )
-    mine = (member > 0.5) & (place == (row - expert * cap).astype(F32))
+    mine = (member > 0.5) & (place == (row % cap).astype(F32))
     weight_ref[...] = jnp.where(mine, weight, 0.0)
     chosen = jnp.where(mine, 1.0, 0.0).astype(BF)
     col = pl.multiple_of(x_ref[0] * part, part)
@@ -155,7 +159,8 @@
     experts = slots // SPAN
     part = tokens.shape[1] // columns
     x = lax.axis_index("hidden").astype(jnp.int32)
-    same_core = [[SPAN * z + core for z in range(experts)] for core in range(SPAN)]
+    order = [j * stride(experts) % experts for j in range(experts)]
+    same_core = [[SPAN * z + core for z in order] for core in range(SPAN)]
     swap = [(i, i ^ 1) for i in range(slots)]
 
     def turned(v, s):

time: 220 us -> 219 us (level)
  no operation moved by 1% of the time
where the time goes in v3:
time: 219 us; the launch traced here: 218 us
  starting transfers between devices  80.6 us (37%)
  blocking collectives  66.8 us (31%)
  waiting for transfers between devices  53.8 us (25%)
  local copies, waits for them, and re-layouts  7.66 us (3%)
  Pallas kernels  7.28 us (3%)
    all_to_all x1, blocking collectives, exchanged(): lax.all_to_all(v, 'expert', split_axis=0, concat_axis=0, tiled=True, axis...  66.8 us
    all_to_all x1, starting transfers between devices, exchanged(): lax.all_to_all(v, 'expert', split_axis=0, concat_axis=0, tiled=True, axis...  45.8 us
    ppermute x6, starting transfers between devices, turned(): lax.ppermute(v, 'hidden', [(i, (i + s) % columns) for i in range(columns)])  22.7 us
    all_to_all x2, waiting for transfers between devices, over_columns(): return lax.all_to_all(v, 'hidden', split_axis=0, concat_axis=0, tiled=True)  19.9 us
    ppermute x6, waiting for transfers between devices, turned(): lax.ppermute(v, 'hidden', [(i, (i + s) % columns) for i in range(columns)])  18.7 us
    all_to_all x1, waiting for transfers between devices, exchanged(): lax.all_to_all(v, 'expert', split_axis=0, concat_axis=0, tiled=True, axis...  15.2 us
    all_to_all x2, starting transfers between devices, over_columns(): return lax.all_to_all(v, 'hidden', split_axis=0, concat_axis=0, tiled=True)  8.14 us
    unnamed x12, local copies, waits for them, and re-layouts  5.19 us
  transfers between devices with their start and end apart: 11, of which 6 were waited for; matrix products, arithmetic and copies ran while one was open for 2% of the time, Pallas kernels for 2%

profile of v3, /device:TPU:40, one launch (start us, length us, event | category | flops | bytes accessed | tf_op | source)
XLA Modules:
  0.0 218.1 jit_solution(12054913129838723581)
XLA Ops:
  0.0 0.0 copy-start.2
  0.0 0.9 copy-done.2
  0.9 0.0 copy-start.3
  0.9 0.7 copy-done.3
  1.6 0.0 copy-start.4
  1.6 0.7 copy-done.4
  2.3 1.3 pack.1
  3.5 45.8 %all-to-all-start = ((bf16[32,8,1024]{2,1,0:T(8,128)(2,1)}), bf16[32,8,1024]{2,1,0:T(8,128)(2,1)S(1)}, u32[]{:S(2)}, u32[]{:S(2)}) async-start(bf16[32,8,1024]{2,1,0:T(8,128)(2,1)} %get-tuple-element.7), calls=%async_computation | async-start | bytes 1048576 | tf_op jit(solution)/shard_map/all_to_all | solution.py:173
  49.4 1.7 constant_dynamic-slice_fusion.7
  51.0 0.1 pad_maximum_fusion.2
  51.1 3.6 %collective-permute-start = (bf16[2,1024,128]{2,1,0:T(8,128)(2,1)S(1)}, bf16[2,1024,128]{2,1,0:T(8,128)(2,1)S(1)}, u32[]{:S(2)}, u32[]{:S(2)}) collective-permute-start(bf16[2,1024,128]{2,1,0:T(8,128)(2,1)S(1)} %pad_maximum_fusion.2), channel_id=1, source_target_pairs={{0,1},{1,2},{2,3},{3,0},{4,5},{5,6},{6,7},{7,4},{8,9},{9,10},{10,1... | collective-permute-start | bytes 1572872 | tf_op jit(solution)/shard_map/ppermute | solution.py:167
  54.7 0.1 pad_maximum_fusion.3
  54.7 4.9 %collective-permute-start.1 = (bf16[2,1024,128]{2,1,0:T(8,128)(2,1)S(1)}, bf16[2,1024,128]{2,1,0:T(8,128)(2,1)S(1)}, u32[]{:S(2)}, u32[]{:S(2)}) collective-permute-start(bf16[2,1024,128]{2,1,0:T(8,128)(2,1)S(1)} %pad_maximum_fusion.3), channel_id=1, source_target_pairs={{0,2},{1,3},{2,0},{3,1},{4,6},{5,7},{6,4},{7,5},{8,10},{9,11},{10,... | collective-permute-start | bytes 1572872 | tf_op jit(solution)/shard_map/ppermute | solution.py:167
  59.7 0.1 pad_maximum_fusion.4
  59.7 3.2 %collective-permute-start.2 = (bf16[2,1024,128]{2,1,0:T(8,128)(2,1)S(1)}, bf16[2,1024,128]{2,1,0:T(8,128)(2,1)S(1)}, u32[]{:S(2)}, u32[]{:S(2)}) collective-permute-start(bf16[2,1024,128]{2,1,0:T(8,128)(2,1)S(1)} %pad_maximum_fusion.4), channel_id=1, source_target_pairs={{0,3},{1,0},{2,1},{3,2},{4,7},{5,4},{6,5},{7,6},{8,11},{9,8},{10,9... | collective-permute-start | bytes 1572872 | tf_op jit(solution)/shard_map/ppermute | solution.py:167
  63.0 0.1 maximum_bitcast_fusion
  63.0 5.0 %collective-permute-done = bf16[2,1024,128]{2,1,0:T(8,128)(2,1)S(1)} collective-permute-done((bf16[2,1024,128]{2,1,0:T(8,128)(2,1)S(1)}, bf16[2,1024,128]{2,1,0:T(8,128)(2,1)S(1)}, u32[]{:S(2)}, u32[]{:S(2)}) %collective-permute-start) | collective-permute-done | bytes 524320 | tf_op jit(solution)/shard_map/ppermute | solution.py:167
  68.1 12.2 %collective-permute-done.1 = bf16[2,1024,128]{2,1,0:T(8,128)(2,1)S(1)} collective-permute-done((bf16[2,1024,128]{2,1,0:T(8,128)(2,1)S(1)}, bf16[2,1024,128]{2,1,0:T(8,128)(2,1)S(1)}, u32[]{:S(2)}, u32[]{:S(2)}) %collective-permute-start.1) | collective-permute-done | bytes 524320 | tf_op jit(solution)/shard_map/ppermute | solution.py:167
  80.3 1.5 collective-permute-done.2
  81.7 0.0 copy-start.5
  81.7 0.3 pad_maximum_fusion.own_ref
  82.0 2.1 collective-permute-start.3
  84.1 0.0 copy-done.5
  84.1 0.8 constant_dynamic-slice_fusion
  84.9 5.0 %collective-permute-start.5 = (bf16[128,1024]{1,0:T(8,128)(2,1)}, bf16[128,1024]{1,0:T(8,128)(2,1)}, u32[]{:S(2)}, u32[]{:S(2)}) collective-permute-start(bf16[128,1024]{1,0:T(8,128)(2,1)} %get-tuple-element.12), channel_id=1, source_target_pairs={{0,2},{1,3},{2,0},{3,1},{4,6},{5,7},{6,4},{7,5},{8,10},{9,11},{10,... | collective-permute-start | bytes 786440 | tf_op jit(solution)/shard_map/ppermute | solution.py:167
  89.9 4.0 %collective-permute-start.6 = (bf16[128,1024]{1,0:T(8,128)(2,1)S(1)}, bf16[128,1024]{1,0:T(8,128)(2,1)}, u32[]{:S(2)}, u32[]{:S(2)}) collective-permute-start(bf16[128,1024]{1,0:T(8,128)(2,1)S(1)} %get-tuple-element.11), channel_id=1, source_target_pairs={{0,3},{1,0},{2,1},{3,2},{4,7},{5,4},{6,5},{7,6},{8,11},{9,8},{10,9... | collective-permute-start | bytes 786440 | tf_op jit(solution)/shard_map/ppermute | solution.py:167
  93.9 2.0 collective-permute-start.4
  95.9 0.0 collective-permute-done.3.other_ref
  95.9 0.0 copy-start
  95.9 1.3 copy-done
  97.2 15.2 %all-to-all-done = bf16[32,8,1024]{2,1,0:T(8,128)(2,1)S(1)} async-done(((bf16[32,8,1024]{2,1,0:T(8,128)(2,1)}), bf16[32,8,1024]{2,1,0:T(8,128)(2,1)S(1)}, u32[]{:S(2)}, u32[]{:S(2)}) %all-to-all-start) | async-done | bytes 524320 | tf_op jit(solution)/shard_map/all_to_all | solution.py:173
  112.4 0.0 copy-start.1
  112.4 1.6 copy-done.1
  114.0 2.8 %partial.1 = bf16[4,256,512]{2,1,0:T(8,128)(2,1)} custom-call(s32[4]{0:T(128)S(1)} %and_select_fusion.at_ref, bf16[256,1024]{1,0:T(8,128)(2,1)S(1)} %bitcast.19, bf16[4,2,1024,128]{3,2,1,0:T(8,128)(2,1)S(1)} %pad_maximum_fusion.own_ref, bf16[4,2,1024,128]{3,2,1,0:T(8,128)(2,1)S(1)} %copy-done.1), custom_call_target="tpu_custom_call" | custom-call | tf_op jit(solution)/shard_map/partial/pallas_call | solution.py:73
  116.8 4.6 %all-to-all-start.1 = ((bf16[4,256,512]{2,1,0:T(8,128)(2,1)}), bf16[4,256,512]{2,1,0:T(8,128)(2,1)S(1)}, u32[]{:S(2)}, u32[]{:S(2)}) async-start(bf16[4,256,512]{2,1,0:T(8,128)(2,1)} %partial.1), calls=%async_computation.1 | async-start | bytes 2097152 | tf_op jit(solution)/shard_map/all_to_all | solution.py:178
  121.4 0.0 collective-permute-done.5
  121.4 0.0 collective-permute-done.6
  121.4 0.0 collective-permute-done.4
  121.4 1.2 pad_maximum_fusion.1.own_ref
  122.7 2.0 collective-permute-start.7
  124.6 11.6 %all-to-all-done.1.parts_ref = bf16[4,256,512]{2,1,0:T(8,128)(2,1)S(1)} async-done(((bf16[4,256,512]{2,1,0:T(8,128)(2,1)}), bf16[4,256,512]{2,1,0:T(8,128)(2,1)S(1)}, u32[]{:S(2)}, u32[]{:S(2)}) %all-to-all-start.1) | async-done | bytes 1048608 | tf_op jit(solution)/shard_map/all_to_all | solution.py:178
  136.3 1.0 act.1
  137.3 3.6 %all-to-all-start.2 = ((bf16[4,2,256,128]{3,2,1,0:T(8,128)(2,1)}), bf16[4,2,256,128]{3,2,1,0:T(8,128)(2,1)S(1)}, u32[]{:S(2)}, u32[]{:S(2)}) async-start(bf16[4,2,256,128]{3,2,1,0:T(8,128)(2,1)} %act.1), calls=%async_computation.2 | async-start | bytes 1048576 | tf_op jit(solution)/shard_map/all_to_all | solution.py:178
  140.8 0.0 collective-permute-done.7.other_ref
  140.8 8.3 %all-to-all-done.2.act_ref = bf16[4,2,256,128]{3,2,1,0:T(8,128)(2,1)S(1)} async-done(((bf16[4,2,256,128]{3,2,1,0:T(8,128)(2,1)}), bf16[4,2,256,128]{3,2,1,0:T(8,128)(2,1)S(1)}, u32[]{:S(2)}, u32[]{:S(2)}) %all-to-all-start.2) | async-done | bytes 524320 | tf_op jit(solution)/shard_map/all_to_all | solution.py:178
  149.1 1.2 down.1
  150.4 66.8 %all_to_all.20.back_ref = bf16[32,8,1024]{2,1,0:T(8,128)(2,1)S(1)} all-to-all(bf16[32,8,1024]{2,1,0:T(8,128)(2,1)S(1)} %bitcast.20), channel_id=1, replica_groups={{0,120,240,104,224,88,208,72,192,56,176,40,160,24,144,8,128,248,112,232..., dimensions={0} | all-to-all | bytes 1048576 | tf_op jit(solution)/shard_map/all_to_all | solution.py:173
  217.2 1.0 combine.1
  (1 shorter events, 0.0 us)
Async XLA Ops:
  0.0 0.9 copy-start.2
  0.9 0.7 copy-start.3
  1.6 0.7 copy-start.4
  3.5 108.9 %all-to-all-start = ((bf16[32,8,1024]{2,1,0:T(8,128)(2,1)}), bf16[32,8,1024]{2,1,0:T(8,128)(2,1)S(1)}, u32[]{:S(2)}, u32[]{:S(2)}) async-start(bf16[32,8,1024]{2,1,0:T(8,128)(2,1)} %get-tuple-element.7), calls=%async_computation | async-start | bytes 1048576 | tf_op jit(solution)/shard_map/all_to_all | solution.py:173
  51.1 17.0 %collective-permute-start = (bf16[2,1024,128]{2,1,0:T(8,128)(2,1)S(1)}, bf16[2,1024,128]{2,1,0:T(8,128)(2,1)S(1)}, u32[]{:S(2)}, u32[]{:S(2)}) collective-permute-start(bf16[2,1024,128]{2,1,0:T(8,128)(2,1)S(1)} %pad_maximum_fusion.2), channel_id=1, source_target_pairs={{0,1},{1,2},{2,3},{3,0},{4,5},{5,6},{6,7},{7,4},{8,9},{9,10},{10,1... | collective-permute-start | bytes 1572872 | tf_op jit(solution)/shard_map/ppermute | solution.py:167
  54.7 25.6 %collective-permute-start.1 = (bf16[2,1024,128]{2,1,0:T(8,128)(2,1)S(1)}, bf16[2,1024,128]{2,1,0:T(8,128)(2,1)S(1)}, u32[]{:S(2)}, u32[]{:S(2)}) collective-permute-start(bf16[2,1024,128]{2,1,0:T(8,128)(2,1)S(1)} %pad_maximum_fusion.3), channel_id=1, source_target_pairs={{0,2},{1,3},{2,0},{3,1},{4,6},{5,7},{6,4},{7,5},{8,10},{9,11},{10,... | collective-permute-start | bytes 1572872 | tf_op jit(solution)/shard_map/ppermute | solution.py:167
  59.7 22.0 %collective-permute-start.2 = (bf16[2,1024,128]{2,1,0:T(8,128)(2,1)S(1)}, bf16[2,1024,128]{2,1,0:T(8,128)(2,1)S(1)}, u32[]{:S(2)}, u32[]{:S(2)}) collective-permute-start(bf16[2,1024,128]{2,1,0:T(8,128)(2,1)S(1)} %pad_maximum_fusion.4), channel_id=1, source_target_pairs={{0,3},{1,0},{2,1},{3,2},{4,7},{5,4},{6,5},{7,6},{8,11},{9,8},{10,9... | collective-permute-start | bytes 1572872 | tf_op jit(solution)/shard_map/ppermute | solution.py:167
  81.7 2.4 %copy-start.5 = (bf16[1,128,4096]{2,1,0:T(8,128)(2,1)S(1)}, bf16[1,128,4096]{2,1,0:T(8,128)(2,1)}, u32[]{:S(2)}) copy-start(bf16[1,128,4096]{2,1,0:T(8,128)(2,1)} %param.11) | copy-start | bytes 3145732
  82.0 13.9 %collective-permute-start.3 = (bf16[4,2,1024,128]{3,2,1,0:T(8,128)(2,1)S(1)}, bf16[4,2,1024,128]{3,2,1,0:T(8,128)(2,1)S(1)}, u32[]{:S(2)}, u32[]{:S(2)}) collective-permute-start(bf16[4,2,1024,128]{3,2,1,0:T(8,128)(2,1)S(1)} %pad_maximum_fusion.own_ref), channel_id=1, source_target_pairs={{0,4},{4,0},{8,12},{12,8},{16,20},{20,16},{24,28},{28,24},{32,36},... | collective-permute-start | bytes 6291464 | tf_op jit(solution)/shard_map/ppermute | solution.py:170
  84.9 36.5 %collective-permute-start.5 = (bf16[128,1024]{1,0:T(8,128)(2,1)}, bf16[128,1024]{1,0:T(8,128)(2,1)}, u32[]{:S(2)}, u32[]{:S(2)}) collective-permute-start(bf16[128,1024]{1,0:T(8,128)(2,1)} %get-tuple-element.12), channel_id=1, source_target_pairs={{0,2},{1,3},{2,0},{3,1},{4,6},{5,7},{6,4},{7,5},{8,10},{9,11},{10,... | collective-permute-start | bytes 786440 | tf_op jit(solution)/shard_map/ppermute | solution.py:167
  89.9 31.5 %collective-permute-start.6 = (bf16[128,1024]{1,0:T(8,128)(2,1)S(1)}, bf16[128,1024]{1,0:T(8,128)(2,1)}, u32[]{:S(2)}, u32[]{:S(2)}) collective-permute-start(bf16[128,1024]{1,0:T(8,128)(2,1)S(1)} %get-tuple-element.11), channel_id=1, source_target_pairs={{0,3},{1,0},{2,1},{3,2},{4,7},{5,4},{6,5},{7,6},{8,11},{9,8},{10,9... | collective-permute-start | bytes 786440 | tf_op jit(solution)/shard_map/ppermute | solution.py:167
  93.9 27.5 %collective-permute-start.4 = (bf16[128,1024]{1,0:T(8,128)(2,1)S(1)}, bf16[128,1024]{1,0:T(8,128)(2,1)}, u32[]{:S(2)}, u32[]{:S(2)}) collective-permute-start(bf16[128,1024]{1,0:T(8,128)(2,1)S(1)} %get-tuple-element.10), channel_id=1, source_target_pairs={{0,1},{1,2},{2,3},{3,0},{4,5},{5,6},{6,7},{7,4},{8,9},{9,10},{10,1... | collective-permute-start | bytes 786440 | tf_op jit(solution)/shard_map/ppermute | solution.py:167
  95.9 1.3 copy-start
  112.4 1.6 copy-start.1
  116.8 19.4 %all-to-all-start.1 = ((bf16[4,256,512]{2,1,0:T(8,128)(2,1)}), bf16[4,256,512]{2,1,0:T(8,128)(2,1)S(1)}, u32[]{:S(2)}, u32[]{:S(2)}) async-start(bf16[4,256,512]{2,1,0:T(8,128)(2,1)} %partial.1), calls=%async_computation.1 | async-start | bytes 2097152 | tf_op jit(solution)/shard_map/all_to_all | solution.py:178
  122.7 18.2 %collective-permute-start.7 = (bf16[4,128,1024]{2,1,0:T(8,128)(2,1)S(1)}, bf16[4,128,1024]{2,1,0:T(8,128)(2,1)S(1)}, u32[]{:S(2)}, u32[]{:S(2)}) collective-permute-start(bf16[4,128,1024]{2,1,0:T(8,128)(2,1)S(1)} %pad_maximum_fusion.1.own_ref), channel_id=1, source_target_pairs={{0,4},{4,0},{8,12},{12,8},{16,20},{20,16},{24,28},{28,24},{32,36},... | collective-permute-start | bytes 3145736 | tf_op jit(solution)/shard_map/ppermute | solution.py:170
  137.3 11.9 %all-to-all-start.2 = ((bf16[4,2,256,128]{3,2,1,0:T(8,128)(2,1)}), bf16[4,2,256,128]{3,2,1,0:T(8,128)(2,1)S(1)}, u32[]{:S(2)}, u32[]{:S(2)}) async-start(bf16[4,2,256,128]{3,2,1,0:T(8,128)(2,1)} %act.1), calls=%async_computation.2 | async-start | bytes 1048576 | tf_op jit(solution)/shard_map/all_to_all | solution.py:178

commit v4 on v3

--- a/solution.py
+++ b/solution.py
@@ -11,15 +11,27 @@
 F32 = jnp.float32
 BF = jnp.bfloat16
 VM = pltpu.MemorySpace.VMEM
+HB = pltpu.MemorySpace.HBM
 
 
 def stride(experts):
     return max(1, experts // 2 - 1)
 
 
-def pack_kernel(x_ref, ids_ref, scores_ref, tok_ref, out_ref, weight_ref):
+def pack_kernel(x_ref, ids_hbm, scores_hbm, tok_hbm, out_ref, weight_ref, ids_ref, scores_ref, tok_ref, sems):
+    width = tok_ref.shape[1]
+    col = pl.multiple_of(x_ref[0] * width, width)
+    copies = [
+        pltpu.make_async_copy(ids_hbm, ids_ref, sems.at[0]),
+        pltpu.make_async_copy(scores_hbm, scores_ref, sems.at[1]),
+        pltpu.make_async_copy(tok_hbm.at[:, pl.ds(col, width)], tok_ref, sems.at[2]),
+    ]
+    for copy in copies:
+        copy.start()
+    for copy in copies:
+        copy.wait()
     top, count = ids_ref.shape
-    experts, cap, part = out_ref.shape
+    experts, cap, _ = out_ref.shape
     pairs = experts * cap
     scores = scores_ref[...]
     routed = 2.5 * scores / jnp.sum(scores, axis=0, keepdims=True)
@@ -40,8 +52,7 @@
     mine = (member > 0.5) & (place == (row % cap).astype(F32))
     weight_ref[...] = jnp.where(mine, weight, 0.0)
     chosen = jnp.where(mine, 1.0, 0.0).astype(BF)
-    col = pl.multiple_of(x_ref[0] * part, part)
-    rows = jnp.dot(chosen, tok_ref[:, pl.ds(col, part)], preferred_element_type=F32)
+    rows = jnp.dot(chosen, tok_ref[...], preferred_element_type=F32)
     for e in range(experts):
         out_ref[e] = rows[e * cap : (e + 1) * cap].astype(BF)
 
@@ -54,30 +65,62 @@
             jax.ShapeDtypeStruct((experts, CAP, part), BF),
             jax.ShapeDtypeStruct((experts * CAP, count), F32),
         ),
-        in_specs=[pl.BlockSpec(memory_space=pltpu.MemorySpace.SMEM)] + [pl.BlockSpec(memory_space=VM)] * 3,
+        in_specs=[pl.BlockSpec(memory_space=pltpu.MemorySpace.SMEM)] + [pl.BlockSpec(memory_space=HB)] * 3,
         out_specs=[pl.BlockSpec(memory_space=VM)] * 2,
-        compiler_params=pltpu.CompilerParams(vmem_limit_bytes=24 << 20),
+        scratch_shapes=[
+            pltpu.VMEM(ids.shape, ids.dtype),
+            pltpu.VMEM(scores.shape, scores.dtype),
+            pltpu.VMEM((count, part), tokens.dtype),
+            pltpu.SemaphoreType.DMA((3,)),
+        ],
         name="pack",
     )(x, ids, scores, tokens)
 
 
-def partial_kernel(at_ref, rows_ref, own_ref, other_ref, out_ref):
+def partial_kernel(at_ref, rows_ref, own_ref, other_hbm, out_hbm, other_ref, out_ref, sem, sems):
+    fetch = pltpu.make_async_copy(other_hbm, other_ref, sem)
+    fetch.start()
     rows = rows_ref[...]
-    for s in range(own_ref.shape[0]):
-        weights = jnp.concatenate([r[s, i] for r in (own_ref, other_ref) for i in range(2)], axis=1)
-        out_ref[at_ref[s]] = jnp.dot(rows, weights, preferred_element_type=F32).astype(BF)
+    blocks, _, _, width = own_ref.shape
+
+    def product(weights_ref, s):
+        weights = jnp.concatenate([weights_ref[s, i] for i in range(2)], axis=1)
+        return jnp.dot(rows, weights, preferred_element_type=F32).astype(BF)
+
+    for s in range(blocks):
+        out_ref[s, :, : 2 * width] = product(own_ref, s)
+    fetch.wait()
+    stores = []
+    for s in range(blocks):
+        out_ref[s, :, 2 * width :] = product(other_ref, s)
+        stores.append(pltpu.make_async_copy(out_ref.at[s], out_hbm.at[at_ref[s]], sems.at[s]))
+        stores[-1].start()
+    for store in stores:
+        store.wait()
 
 
 def partial_of(at, rows, own, other):
     blocks, _, _, width = own.shape
+    shape = (blocks, rows.shape[0], 2 * SPAN * width)
     return pl.pallas_call(
         partial_kernel,
-        out_shape=jax.ShapeDtypeStruct((blocks, rows.shape[0], 2 * SPAN * width), BF),
-        in_specs=[pl.BlockSpec(memory_space=pltpu.MemorySpace.SMEM)] + [pl.BlockSpec(memory_space=VM)] * 3,
-        out_specs=pl.BlockSpec(memory_space=VM),
+        out_shape=pltpu.MemorySpace.HBM(shape, BF),
+        in_specs=[
+            pl.BlockSpec(memory_space=pltpu.MemorySpace.SMEM),
+            pl.BlockSpec(memory_space=VM),
+            pl.BlockSpec(memory_space=VM),
+            pl.BlockSpec(memory_space=HB),
+        ],
+        out_specs=pl.BlockSpec(memory_space=HB),
+        scratch_shapes=[
+            pltpu.VMEM(other.shape, BF),
+            pltpu.VMEM(shape, BF),
+            pltpu.SemaphoreType.DMA,
+            pltpu.SemaphoreType.DMA((blocks,)),
+        ],
         compiler_params=pltpu.CompilerParams(vmem_limit_bytes=24 << 20),
         name="partial",
-    )(at, rows, own, other)
+    )(at, rows, own, pltpu.with_memory_space_constraint(other, pltpu.MemorySpace.HBM))
 
 
 def act_kernel(parts_ref, out_ref):

time: 219 us -> 216 us (0.986)
  local copies, waits for them, and re-layouts: 7.66 us -> 2.48 us
  Pallas kernels: 7.28 us -> 9.57 us
    unnamed x12 -> x4, local copies, waits for them, and re-layouts: 5.19 us -> 0.01 us
where the time goes in v4:
time: 216 us
  starting transfers between devices  80.6 us (37%)
  blocking collectives  66 us (31%)
  waiting for transfers between devices  55.1 us (26%)
  Pallas kernels  9.57 us (4%)
  local copies, waits for them, and re-layouts  2.48 us (1%)
    all_to_all x1, blocking collectives, exchanged(): lax.all_to_all(v, 'expert', split_axis=0, concat_axis=0, tiled=True, axis...  66 us
    all_to_all x1, starting transfers between devices, exchanged(): lax.all_to_all(v, 'expert', split_axis=0, concat_axis=0, tiled=True, axis...  45.8 us
    ppermute x6, starting transfers between devices, turned(): lax.ppermute(v, 'hidden', [(i, (i + s) % columns) for i in range(columns)])  22.7 us
    all_to_all x2, waiting for transfers between devices, over_columns(): return lax.all_to_all(v, 'hidden', split_axis=0, concat_axis=0, tiled=True)  19.9 us
    ppermute x6, waiting for transfers between devices, turned(): lax.ppermute(v, 'hidden', [(i, (i + s) % columns) for i in range(columns)])  18.7 us
    all_to_all x1, waiting for transfers between devices, exchanged(): lax.all_to_all(v, 'expert', split_axis=0, concat_axis=0, tiled=True, axis...  16.5 us
    all_to_all x2, starting transfers between devices, over_columns(): return lax.all_to_all(v, 'hidden', split_axis=0, concat_axis=0, tiled=True)  8.16 us
  transfers between devices with their start and end apart: 11, of which 6 were waited for; matrix products, arithmetic and copies ran while one was open for 2% of the time, Pallas kernels for 2%

profile of v4, /device:TPU:40, one launch (start us, length us, event | category | flops | bytes accessed | tf_op | source)
XLA Modules:
  0.0 215.8 jit_solution(12353922021047312880)
XLA Ops:
  0.0 2.2 %pack.1 = (bf16[32,8,1024]{2,1,0:T(8,128)(2,1)}, f32[256,16]{1,0:T(8,128)}) custom-call(s32[1]{0:T(128)} %bitcast.x_ref, s32[8,16]{1,0:T(8,128)} %bitcast.24, f32[8,16]{1,0:T(8,128)} %bitcast.25, bf16[16,4096]{1,0:T(8,128)(2,1)} %tok_hbm.1), custom_call_target="tpu_custom_call" | custom-call | tf_op jit(solution)/shard_map/pack/pallas_call | solution.py:62
  2.2 45.8 %all-to-all-start = ((bf16[32,8,1024]{2,1,0:T(8,128)(2,1)}), bf16[32,8,1024]{2,1,0:T(8,128)(2,1)S(1)}, u32[]{:S(2)}, u32[]{:S(2)}) async-start(bf16[32,8,1024]{2,1,0:T(8,128)(2,1)} %get-tuple-element.7), calls=%async_computation | async-start | bytes 1048576 | tf_op jit(solution)/shard_map/all_to_all | solution.py:216
  48.0 1.7 constant_dynamic-slice_fusion.7
  49.7 0.1 pad_maximum_fusion.2
  49.7 3.6 %collective-permute-start = (bf16[2,1024,128]{2,1,0:T(8,128)(2,1)S(1)}, bf16[2,1024,128]{2,1,0:T(8,128)(2,1)S(1)}, u32[]{:S(2)}, u32[]{:S(2)}) collective-permute-start(bf16[2,1024,128]{2,1,0:T(8,128)(2,1)S(1)} %pad_maximum_fusion.2), channel_id=1, source_target_pairs={{0,1},{1,2},{2,3},{3,0},{4,5},{5,6},{6,7},{7,4},{8,9},{9,10},{10,1... | collective-permute-start | bytes 1572872 | tf_op jit(solution)/shard_map/ppermute | solution.py:210
  53.3 0.1 pad_maximum_fusion.3
  53.4 4.9 %collective-permute-start.1 = (bf16[2,1024,128]{2,1,0:T(8,128)(2,1)S(1)}, bf16[2,1024,128]{2,1,0:T(8,128)(2,1)S(1)}, u32[]{:S(2)}, u32[]{:S(2)}) collective-permute-start(bf16[2,1024,128]{2,1,0:T(8,128)(2,1)S(1)} %pad_maximum_fusion.3), channel_id=1, source_target_pairs={{0,2},{1,3},{2,0},{3,1},{4,6},{5,7},{6,4},{7,5},{8,10},{9,11},{10,... | collective-permute-start | bytes 1572872 | tf_op jit(solution)/shard_map/ppermute | solution.py:210
  58.3 0.1 pad_maximum_fusion.4
  58.4 3.2 %collective-permute-start.2 = (bf16[2,1024,128]{2,1,0:T(8,128)(2,1)S(1)}, bf16[2,1024,128]{2,1,0:T(8,128)(2,1)S(1)}, u32[]{:S(2)}, u32[]{:S(2)}) collective-permute-start(bf16[2,1024,128]{2,1,0:T(8,128)(2,1)S(1)} %pad_maximum_fusion.4), channel_id=1, source_target_pairs={{0,3},{1,0},{2,1},{3,2},{4,7},{5,4},{6,5},{7,6},{8,11},{9,8},{10,9... | collective-permute-start | bytes 1572872 | tf_op jit(solution)/shard_map/ppermute | solution.py:210
  61.6 0.1 maximum_bitcast_fusion
  61.7 5.0 %collective-permute-done = bf16[2,1024,128]{2,1,0:T(8,128)(2,1)S(1)} collective-permute-done((bf16[2,1024,128]{2,1,0:T(8,128)(2,1)S(1)}, bf16[2,1024,128]{2,1,0:T(8,128)(2,1)S(1)}, u32[]{:S(2)}, u32[]{:S(2)}) %collective-permute-start) | collective-permute-done | bytes 524320 | tf_op jit(solution)/shard_map/ppermute | solution.py:210
  66.7 12.2 %collective-permute-done.1 = bf16[2,1024,128]{2,1,0:T(8,128)(2,1)S(1)} collective-permute-done((bf16[2,1024,128]{2,1,0:T(8,128)(2,1)S(1)}, bf16[2,1024,128]{2,1,0:T(8,128)(2,1)S(1)}, u32[]{:S(2)}, u32[]{:S(2)}) %collective-permute-start.1) | collective-permute-done | bytes 524320 | tf_op jit(solution)/shard_map/ppermute | solution.py:210
  79.0 1.5 collective-permute-done.2
  80.4 0.0 copy-start.1
  80.4 0.3 pad_maximum_fusion.own_ref
  80.7 2.1 collective-permute-start.3
  82.8 0.0 copy-done.1
  82.8 0.8 constant_dynamic-slice_fusion
  83.6 5.0 %collective-permute-start.5 = (bf16[128,1024]{1,0:T(8,128)(2,1)}, bf16[128,1024]{1,0:T(8,128)(2,1)}, u32[]{:S(2)}, u32[]{:S(2)}) collective-permute-start(bf16[128,1024]{1,0:T(8,128)(2,1)} %get-tuple-element.12), channel_id=1, source_target_pairs={{0,2},{1,3},{2,0},{3,1},{4,6},{5,7},{6,4},{7,5},{8,10},{9,11},{10,... | collective-permute-start | bytes 786440 | tf_op jit(solution)/shard_map/ppermute | solution.py:210
  88.6 4.0 %collective-permute-start.6 = (bf16[128,1024]{1,0:T(8,128)(2,1)S(1)}, bf16[128,1024]{1,0:T(8,128)(2,1)}, u32[]{:S(2)}, u32[]{:S(2)}) collective-permute-start(bf16[128,1024]{1,0:T(8,128)(2,1)S(1)} %get-tuple-element.11), channel_id=1, source_target_pairs={{0,3},{1,0},{2,1},{3,2},{4,7},{5,4},{6,5},{7,6},{8,11},{9,8},{10,9... | collective-permute-start | bytes 786440 | tf_op jit(solution)/shard_map/ppermute | solution.py:210
  92.6 2.0 collective-permute-start.4
  94.5 0.0 collective-permute-done.3.other_hbm
  94.6 16.5 %all-to-all-done = bf16[32,8,1024]{2,1,0:T(8,128)(2,1)S(1)} async-done(((bf16[32,8,1024]{2,1,0:T(8,128)(2,1)}), bf16[32,8,1024]{2,1,0:T(8,128)(2,1)S(1)}, u32[]{:S(2)}, u32[]{:S(2)}) %all-to-all-start) | async-done | bytes 524320 | tf_op jit(solution)/shard_map/all_to_all | solution.py:216
  111.0 4.2 %partial.1 = bf16[4,256,512]{2,1,0:T(8,128)(2,1)} custom-call(s32[4]{0:T(128)S(1)} %and_select_fusion.at_ref, bf16[256,1024]{1,0:T(8,128)(2,1)S(1)} %bitcast.19, bf16[4,2,1024,128]{3,2,1,0:T(8,128)(2,1)S(1)} %pad_maximum_fusion.own_ref, bf16[4,2,1024,128]{3,2,1,0:T(8,128)(2,1)} %collective-permute-done.3.other_hbm), custom_call_target="tpu_custom_call" | custom-call | tf_op jit(solution)/shard_map/partial/pallas_call | solution.py:105
  115.3 4.6 %all-to-all-start.1 = ((bf16[4,256,512]{2,1,0:T(8,128)(2,1)}), bf16[4,256,512]{2,1,0:T(8,128)(2,1)S(1)}, u32[]{:S(2)}, u32[]{:S(2)}) async-start(bf16[4,256,512]{2,1,0:T(8,128)(2,1)} %partial.1), calls=%async_computation.1 | async-start | bytes 2097152 | tf_op jit(solution)/shard_map/all_to_all | solution.py:221
  119.9 0.0 collective-permute-done.5
  119.9 0.0 collective-permute-done.6
  119.9 0.0 collective-permute-done.4
  119.9 1.2 pad_maximum_fusion.1.own_ref
  121.1 2.0 collective-permute-start.7
  123.1 11.6 %all-to-all-done.1.parts_ref = bf16[4,256,512]{2,1,0:T(8,128)(2,1)S(1)} async-done(((bf16[4,256,512]{2,1,0:T(8,128)(2,1)}), bf16[4,256,512]{2,1,0:T(8,128)(2,1)S(1)}, u32[]{:S(2)}, u32[]{:S(2)}) %all-to-all-start.1) | async-done | bytes 1048608 | tf_op jit(solution)/shard_map/all_to_all | solution.py:221
  134.7 1.0 act.1
  135.7 3.6 %all-to-all-start.2 = ((bf16[4,2,256,128]{3,2,1,0:T(8,128)(2,1)}), bf16[4,2,256,128]{3,2,1,0:T(8,128)(2,1)S(1)}, u32[]{:S(2)}, u32[]{:S(2)}) async-start(bf16[4,2,256,128]{3,2,1,0:T(8,128)(2,1)} %act.1), calls=%async_computation.2 | async-start | bytes 1048576 | tf_op jit(solution)/shard_map/all_to_all | solution.py:221
  139.3 0.0 copy-start
  139.3 0.0 collective-permute-done.7.other_ref
  139.3 8.3 %all-to-all-done.2.act_ref = bf16[4,2,256,128]{3,2,1,0:T(8,128)(2,1)S(1)} async-done(((bf16[4,2,256,128]{3,2,1,0:T(8,128)(2,1)}), bf16[4,2,256,128]{3,2,1,0:T(8,128)(2,1)S(1)}, u32[]{:S(2)}, u32[]{:S(2)}) %all-to-all-start.2) | async-done | bytes 524320 | tf_op jit(solution)/shard_map/all_to_all | solution.py:221
  147.6 1.2 down.1
  148.8 66.0 %all_to_all.20.back_ref = bf16[32,8,1024]{2,1,0:T(8,128)(2,1)S(1)} all-to-all(bf16[32,8,1024]{2,1,0:T(8,128)(2,1)S(1)} %bitcast.20), channel_id=1, replica_groups={{0,120,240,104,224,88,208,72,192,56,176,40,160,24,144,8,128,248,112,232..., dimensions={0} | all-to-all | bytes 1048576 | tf_op jit(solution)/shard_map/all_to_all | solution.py:216
  214.8 0.0 copy-done
  214.8 1.0 combine.1
  (1 shorter events, 0.0 us)
Async XLA Ops:
  2.2 108.9 %all-to-all-start = ((bf16[32,8,1024]{2,1,0:T(8,128)(2,1)}), bf16[32,8,1024]{2,1,0:T(8,128)(2,1)S(1)}, u32[]{:S(2)}, u32[]{:S(2)}) async-start(bf16[32,8,1024]{2,1,0:T(8,128)(2,1)} %get-tuple-element.7), calls=%async_computation | async-start | bytes 1048576 | tf_op jit(solution)/shard_map/all_to_all | solution.py:216
  49.7 17.0 %collective-permute-start = (bf16[2,1024,128]{2,1,0:T(8,128)(2,1)S(1)}, bf16[2,1024,128]{2,1,0:T(8,128)(2,1)S(1)}, u32[]{:S(2)}, u32[]{:S(2)}) collective-permute-start(bf16[2,1024,128]{2,1,0:T(8,128)(2,1)S(1)} %pad_maximum_fusion.2), channel_id=1, source_target_pairs={{0,1},{1,2},{2,3},{3,0},{4,5},{5,6},{6,7},{7,4},{8,9},{9,10},{10,1... | collective-permute-start | bytes 1572872 | tf_op jit(solution)/shard_map/ppermute | solution.py:210
  53.4 25.6 %collective-permute-start.1 = (bf16[2,1024,128]{2,1,0:T(8,128)(2,1)S(1)}, bf16[2,1024,128]{2,1,0:T(8,128)(2,1)S(1)}, u32[]{:S(2)}, u32[]{:S(2)}) collective-permute-start(bf16[2,1024,128]{2,1,0:T(8,128)(2,1)S(1)} %pad_maximum_fusion.3), channel_id=1, source_target_pairs={{0,2},{1,3},{2,0},{3,1},{4,6},{5,7},{6,4},{7,5},{8,10},{9,11},{10,... | collective-permute-start | bytes 1572872 | tf_op jit(solution)/shard_map/ppermute | solution.py:210
  58.4 22.0 %collective-permute-start.2 = (bf16[2,1024,128]{2,1,0:T(8,128)(2,1)S(1)}, bf16[2,1024,128]{2,1,0:T(8,128)(2,1)S(1)}, u32[]{:S(2)}, u32[]{:S(2)}) collective-permute-start(bf16[2,1024,128]{2,1,0:T(8,128)(2,1)S(1)} %pad_maximum_fusion.4), channel_id=1, source_target_pairs={{0,3},{1,0},{2,1},{3,2},{4,7},{5,4},{6,5},{7,6},{8,11},{9,8},{10,9... | collective-permute-start | bytes 1572872 | tf_op jit(solution)/shard_map/ppermute | solution.py:210
  80.4 2.4 %copy-start.1 = (bf16[1,128,4096]{2,1,0:T(8,128)(2,1)S(1)}, bf16[1,128,4096]{2,1,0:T(8,128)(2,1)}, u32[]{:S(2)}) copy-start(bf16[1,128,4096]{2,1,0:T(8,128)(2,1)} %param.11) | copy-start | bytes 3145732
  80.7 13.9 %collective-permute-start.3 = (bf16[4,2,1024,128]{3,2,1,0:T(8,128)(2,1)S(1)}, bf16[4,2,1024,128]{3,2,1,0:T(8,128)(2,1)}, u32[]{:S(2)}, u32[]{:S(2)}) collective-permute-start(bf16[4,2,1024,128]{3,2,1,0:T(8,128)(2,1)S(1)} %pad_maximum_fusion.own_ref), channel_id=1, source_target_pairs={{0,4},{4,0},{8,12},{12,8},{16,20},{20,16},{24,28},{28,24},{32,36},... | collective-permute-start | bytes 6291464 | tf_op jit(solution)/shard_map/ppermute | solution.py:213
  83.6 36.3 %collective-permute-start.5 = (bf16[128,1024]{1,0:T(8,128)(2,1)}, bf16[128,1024]{1,0:T(8,128)(2,1)}, u32[]{:S(2)}, u32[]{:S(2)}) collective-permute-start(bf16[128,1024]{1,0:T(8,128)(2,1)} %get-tuple-element.12), channel_id=1, source_target_pairs={{0,2},{1,3},{2,0},{3,1},{4,6},{5,7},{6,4},{7,5},{8,10},{9,11},{10,... | collective-permute-start | bytes 786440 | tf_op jit(solution)/shard_map/ppermute | solution.py:210
  88.6 31.3 %collective-permute-start.6 = (bf16[128,1024]{1,0:T(8,128)(2,1)S(1)}, bf16[128,1024]{1,0:T(8,128)(2,1)}, u32[]{:S(2)}, u32[]{:S(2)}) collective-permute-start(bf16[128,1024]{1,0:T(8,128)(2,1)S(1)} %get-tuple-element.11), channel_id=1, source_target_pairs={{0,3},{1,0},{2,1},{3,2},{4,7},{5,4},{6,5},{7,6},{8,11},{9,8},{10,9... | collective-permute-start | bytes 786440 | tf_op jit(solution)/shard_map/ppermute | solution.py:210
  92.6 27.3 %collective-permute-start.4 = (bf16[128,1024]{1,0:T(8,128)(2,1)S(1)}, bf16[128,1024]{1,0:T(8,128)(2,1)}, u32[]{:S(2)}, u32[]{:S(2)}) collective-permute-start(bf16[128,1024]{1,0:T(8,128)(2,1)S(1)} %get-tuple-element.10), channel_id=1, source_target_pairs={{0,1},{1,2},{2,3},{3,0},{4,5},{5,6},{6,7},{7,4},{8,9},{9,10},{10,1... | collective-permute-start | bytes 786440 | tf_op jit(solution)/shard_map/ppermute | solution.py:210
  115.3 19.5 %all-to-all-start.1 = ((bf16[4,256,512]{2,1,0:T(8,128)(2,1)}), bf16[4,256,512]{2,1,0:T(8,128)(2,1)S(1)}, u32[]{:S(2)}, u32[]{:S(2)}) async-start(bf16[4,256,512]{2,1,0:T(8,128)(2,1)} %partial.1), calls=%async_computation.1 | async-start | bytes 2097152 | tf_op jit(solution)/shard_map/all_to_all | solution.py:221
  121.1 18.2 %collective-permute-start.7 = (bf16[4,128,1024]{2,1,0:T(8,128)(2,1)S(1)}, bf16[4,128,1024]{2,1,0:T(8,128)(2,1)S(1)}, u32[]{:S(2)}, u32[]{:S(2)}) collective-permute-start(bf16[4,128,1024]{2,1,0:T(8,128)(2,1)S(1)} %pad_maximum_fusion.1.own_ref), channel_id=1, source_target_pairs={{0,4},{4,0},{8,12},{12,8},{16,20},{20,16},{24,28},{28,24},{32,36},... | collective-permute-start | bytes 3145736 | tf_op jit(solution)/shard_map/ppermute | solution.py:213
  135.7 11.9 %all-to-all-start.2 = ((bf16[4,2,256,128]{3,2,1,0:T(8,128)(2,1)}), bf16[4,2,256,128]{3,2,1,0:T(8,128)(2,1)S(1)}, u32[]{:S(2)}, u32[]{:S(2)}) async-start(bf16[4,2,256,128]{3,2,1,0:T(8,128)(2,1)} %act.1), calls=%async_computation.2 | async-start | bytes 1048576 | tf_op jit(solution)/shard_map/all_to_all | solution.py:221
  139.3 75.5 %copy-start = (f32[256,16]{1,0:T(8,128)S(1)}, f32[256,16]{1,0:T(8,128)}, u32[]{:S(2)}) copy-start(f32[256,16]{1,0:T(8,128)} %get-tuple-element.8.weight_ref) | copy-start | bytes 49156

commit v5 on v4

--- a/solution.py
+++ b/solution.py
@@ -36,7 +36,7 @@
     scores = scores_ref[...]
     routed = 2.5 * scores / jnp.sum(scores, axis=0, keepdims=True)
     row = lax.broadcasted_iota(jnp.int32, (pairs, count), 0)
-    expert = row // cap * stride(experts) % experts
+    expert = row // cap * x_ref[1] % experts
     member = jnp.zeros((pairs, count), F32)
     weight = jnp.zeros((pairs, count), F32)
     for k in range(top):
@@ -202,8 +202,10 @@
     experts = slots // SPAN
     part = tokens.shape[1] // columns
     x = lax.axis_index("hidden").astype(jnp.int32)
-    order = [j * stride(experts) % experts for j in range(experts)]
-    same_core = [[SPAN * z + core for z in order] for core in range(SPAN)]
+    steps = [stride(experts), experts - stride(experts)]
+    same_core = [[SPAN * (j * steps[c] % experts) + c for j in range(experts)] for c in range(SPAN)]
+    core = (lax.axis_index("expert") % SPAN).astype(jnp.int32)
+    step = jnp.where(core == 0, steps[0], steps[1]).astype(jnp.int32)
     swap = [(i, i ^ 1) for i in range(slots)]
 
     def turned(v, s):
@@ -231,7 +233,7 @@
     wide = jnp.stack(others)
     wide_other = swapped(wide)
     down_other = swapped(down)
-    outgoing, weight = pack(x.reshape(1), expert_ids.T, router_scores.T, tokens, experts, part)
+    outgoing, weight = pack(jnp.stack([x, step]), expert_ids.T, router_scores.T, tokens, experts, part)
     own = exchanged(outgoing).reshape(experts * CAP, part)
     source = (x - jnp.arange(columns, dtype=jnp.int32)) % columns
     parts = over_columns(partial_of(source, own, wide, wide_other))

time: 216 us -> 219 us (1.014)
  blocking collectives: 66 us -> 68.3 us
  waiting for transfers between devices: 55.1 us -> 52.9 us
    all_to_all x1, blocking collectives: 66 us -> 68.3 us  [exchanged(): lax.all_to_all(v, 'expert', split_axis=0, concat_axis=0, tiled=True, axis...]
where the time goes in v5:
time: 219 us; the launch traced here: 218 us
  starting transfers between devices  81.2 us (37%)
  blocking collectives  68.3 us (31%)
  waiting for transfers between devices  52.9 us (24%)
  Pallas kernels  10.2 us (5%)
  local copies, waits for them, and re-layouts  2.48 us (1%)
  other arithmetic  2.33 us (1%)
    all_to_all x1, blocking collectives, exchanged(): lax.all_to_all(v, 'expert', split_axis=0, concat_axis=0, tiled=True, axis...  68.3 us
    all_to_all x1, starting transfers between devices, exchanged(): lax.all_to_all(v, 'expert', split_axis=0, concat_axis=0, tiled=True, axis...  45.8 us
    ppermute x6, starting transfers between devices, turned(): lax.ppermute(v, 'hidden', [(i, (i + s) % columns) for i in range(columns)])  23.3 us
    all_to_all x2, waiting for transfers between devices, over_columns(): return lax.all_to_all(v, 'hidden', split_axis=0, concat_axis=0, tiled=True)  19.3 us
    ppermute x6, waiting for transfers between devices, turned(): lax.ppermute(v, 'hidden', [(i, (i + s) % columns) for i in range(columns)])  18.7 us
    all_to_all x1, waiting for transfers between devices, exchanged(): lax.all_to_all(v, 'expert', split_axis=0, concat_axis=0, tiled=True, axis...  14.8 us
    all_to_all x2, starting transfers between devices, over_columns(): return lax.all_to_all(v, 'hidden', split_axis=0, concat_axis=0, tiled=True)  8.16 us
  transfers between devices with their start and end apart: 11, of which 6 were waited for; matrix products, arithmetic and copies ran while one was open for 2% of the time, Pallas kernels for 2%

profile of v5, /device:TPU:40, one launch (start us, length us, event | category | flops | bytes accessed | tf_op | source)
XLA Modules:
  0.0 217.7 jit_solution(13665969273345708906)
XLA Ops:
  0.0 0.6 pad_add_fusion.x_ref
  0.6 2.8 %pack.1 = (bf16[32,8,1024]{2,1,0:T(8,128)(2,1)}, f32[256,16]{1,0:T(8,128)}) custom-call(s32[2]{0:T(128)} %pad_add_fusion.x_ref, s32[8,16]{1,0:T(8,128)} %bitcast.25, f32[8,16]{1,0:T(8,128)} %bitcast.26, bf16[16,4096]{1,0:T(8,128)(2,1)} %tok_hbm.1), custom_call_target="tpu_custom_call" | custom-call | tf_op jit(solution)/shard_map/pack/pallas_call | solution.py:62
  3.4 45.8 %all-to-all-start = ((bf16[32,8,1024]{2,1,0:T(8,128)(2,1)}), bf16[32,8,1024]{2,1,0:T(8,128)(2,1)S(1)}, u32[]{:S(2)}, u32[]{:S(2)}) async-start(bf16[32,8,1024]{2,1,0:T(8,128)(2,1)} %get-tuple-element.7), calls=%async_computation | async-start | bytes 1048576 | tf_op jit(solution)/shard_map/all_to_all | solution.py:218
  49.3 1.7 constant_dynamic-slice_fusion.7
  50.9 0.1 pad_maximum_fusion.2
  51.0 3.6 %collective-permute-start = (bf16[2,1024,128]{2,1,0:T(8,128)(2,1)S(1)}, bf16[2,1024,128]{2,1,0:T(8,128)(2,1)S(1)}, u32[]{:S(2)}, u32[]{:S(2)}) collective-permute-start(bf16[2,1024,128]{2,1,0:T(8,128)(2,1)S(1)} %pad_maximum_fusion.2), channel_id=1, source_target_pairs={{0,1},{1,2},{2,3},{3,0},{4,5},{5,6},{6,7},{7,4},{8,9},{9,10},{10,1... | collective-permute-start | bytes 1572872 | tf_op jit(solution)/shard_map/ppermute | solution.py:212
  54.6 0.1 pad_maximum_fusion.3
  54.6 4.9 %collective-permute-start.1 = (bf16[2,1024,128]{2,1,0:T(8,128)(2,1)S(1)}, bf16[2,1024,128]{2,1,0:T(8,128)(2,1)S(1)}, u32[]{:S(2)}, u32[]{:S(2)}) collective-permute-start(bf16[2,1024,128]{2,1,0:T(8,128)(2,1)S(1)} %pad_maximum_fusion.3), channel_id=1, source_target_pairs={{0,2},{1,3},{2,0},{3,1},{4,6},{5,7},{6,4},{7,5},{8,10},{9,11},{10,... | collective-permute-start | bytes 1572872 | tf_op jit(solution)/shard_map/ppermute | solution.py:212
  59.6 0.1 pad_maximum_fusion.4
  59.6 3.2 %collective-permute-start.2 = (bf16[2,1024,128]{2,1,0:T(8,128)(2,1)S(1)}, bf16[2,1024,128]{2,1,0:T(8,128)(2,1)S(1)}, u32[]{:S(2)}, u32[]{:S(2)}) collective-permute-start(bf16[2,1024,128]{2,1,0:T(8,128)(2,1)S(1)} %pad_maximum_fusion.4), channel_id=1, source_target_pairs={{0,3},{1,0},{2,1},{3,2},{4,7},{5,4},{6,5},{7,6},{8,11},{9,8},{10,9... | collective-permute-start | bytes 1572872 | tf_op jit(solution)/shard_map/ppermute | solution.py:212
  62.9 0.1 maximum_bitcast_fusion
  63.0 5.0 %collective-permute-done = bf16[2,1024,128]{2,1,0:T(8,128)(2,1)S(1)} collective-permute-done((bf16[2,1024,128]{2,1,0:T(8,128)(2,1)S(1)}, bf16[2,1024,128]{2,1,0:T(8,128)(2,1)S(1)}, u32[]{:S(2)}, u32[]{:S(2)}) %collective-permute-start) | collective-permute-done | bytes 524320 | tf_op jit(solution)/shard_map/ppermute | solution.py:212
  68.0 12.2 %collective-permute-done.1 = bf16[2,1024,128]{2,1,0:T(8,128)(2,1)S(1)} collective-permute-done((bf16[2,1024,128]{2,1,0:T(8,128)(2,1)S(1)}, bf16[2,1024,128]{2,1,0:T(8,128)(2,1)S(1)}, u32[]{:S(2)}, u32[]{:S(2)}) %collective-permute-start.1) | collective-permute-done | bytes 524320 | tf_op jit(solution)/shard_map/ppermute | solution.py:212
  80.2 1.5 collective-permute-done.2
  81.7 0.0 copy-start.1
  81.7 0.3 pad_maximum_fusion.own_ref
  81.9 2.1 collective-permute-start.3
  84.0 0.0 copy-done.1
  84.0 0.8 constant_dynamic-slice_fusion
  84.9 4.4 %collective-permute-start.4 = (bf16[128,1024]{1,0:T(8,128)(2,1)}, bf16[128,1024]{1,0:T(8,128)(2,1)}, u32[]{:S(2)}, u32[]{:S(2)}) collective-permute-start(bf16[128,1024]{1,0:T(8,128)(2,1)} %get-tuple-element.10), channel_id=1, source_target_pairs={{0,1},{1,2},{2,3},{3,0},{4,5},{5,6},{6,7},{7,4},{8,9},{9,10},{10,1... | collective-permute-start | bytes 786440 | tf_op jit(solution)/shard_map/ppermute | solution.py:212
  89.2 3.6 %collective-permute-start.5 = (bf16[128,1024]{1,0:T(8,128)(2,1)S(1)}, bf16[128,1024]{1,0:T(8,128)(2,1)}, u32[]{:S(2)}, u32[]{:S(2)}) collective-permute-start(bf16[128,1024]{1,0:T(8,128)(2,1)S(1)} %get-tuple-element.12), channel_id=1, source_target_pairs={{0,2},{1,3},{2,0},{3,1},{4,6},{5,7},{6,4},{7,5},{8,10},{9,11},{10,... | collective-permute-start | bytes 786440 | tf_op jit(solution)/shard_map/ppermute | solution.py:212
  92.8 3.6 %collective-permute-start.6 = (bf16[128,1024]{1,0:T(8,128)(2,1)S(1)}, bf16[128,1024]{1,0:T(8,128)(2,1)}, u32[]{:S(2)}, u32[]{:S(2)}) collective-permute-start(bf16[128,1024]{1,0:T(8,128)(2,1)S(1)} %get-tuple-element.11), channel_id=1, source_target_pairs={{0,3},{1,0},{2,1},{3,2},{4,7},{5,4},{6,5},{7,6},{8,11},{9,8},{10,9... | collective-permute-start | bytes 786440 | tf_op jit(solution)/shard_map/ppermute | solution.py:212
  96.4 0.0 collective-permute-done.3.other_hbm
  96.4 14.8 %all-to-all-done = bf16[32,8,1024]{2,1,0:T(8,128)(2,1)S(1)} async-done(((bf16[32,8,1024]{2,1,0:T(8,128)(2,1)}), bf16[32,8,1024]{2,1,0:T(8,128)(2,1)S(1)}, u32[]{:S(2)}, u32[]{:S(2)}) %all-to-all-start) | async-done | bytes 524320 | tf_op jit(solution)/shard_map/all_to_all | solution.py:218
  111.3 4.2 %partial.1 = bf16[4,256,512]{2,1,0:T(8,128)(2,1)} custom-call(s32[4]{0:T(128)S(1)} %and_select_fusion.at_ref, bf16[256,1024]{1,0:T(8,128)(2,1)S(1)} %bitcast.20, bf16[4,2,1024,128]{3,2,1,0:T(8,128)(2,1)S(1)} %pad_maximum_fusion.own_ref, bf16[4,2,1024,128]{3,2,1,0:T(8,128)(2,1)} %collective-permute-done.3.other_hbm), custom_call_target="tpu_custom_call" | custom-call | tf_op jit(solution)/shard_map/partial/pallas_call | solution.py:105
  115.5 4.6 %all-to-all-start.1 = ((bf16[4,256,512]{2,1,0:T(8,128)(2,1)}), bf16[4,256,512]{2,1,0:T(8,128)(2,1)S(1)}, u32[]{:S(2)}, u32[]{:S(2)}) async-start(bf16[4,256,512]{2,1,0:T(8,128)(2,1)} %partial.1), calls=%async_computation.1 | async-start | bytes 2097152 | tf_op jit(solution)/shard_map/all_to_all | solution.py:223
  120.1 0.0 collective-permute-done.4
  120.1 0.0 collective-permute-done.5
  120.1 0.0 collective-permute-done.6
  120.1 1.2 pad_maximum_fusion.1.own_ref
  121.3 2.0 collective-permute-start.7
  123.3 11.3 %all-to-all-done.1.parts_ref = bf16[4,256,512]{2,1,0:T(8,128)(2,1)S(1)} async-done(((bf16[4,256,512]{2,1,0:T(8,128)(2,1)}), bf16[4,256,512]{2,1,0:T(8,128)(2,1)S(1)}, u32[]{:S(2)}, u32[]{:S(2)}) %all-to-all-start.1) | async-done | bytes 1048608 | tf_op jit(solution)/shard_map/all_to_all | solution.py:223
  134.6 1.0 act.1
  135.6 3.6 %all-to-all-start.2 = ((bf16[4,2,256,128]{3,2,1,0:T(8,128)(2,1)}), bf16[4,2,256,128]{3,2,1,0:T(8,128)(2,1)S(1)}, u32[]{:S(2)}, u32[]{:S(2)}) async-start(bf16[4,2,256,128]{3,2,1,0:T(8,128)(2,1)} %act.1), calls=%async_computation.2 | async-start | bytes 1048576 | tf_op jit(solution)/shard_map/all_to_all | solution.py:223
  139.2 0.0 copy-start
  139.2 0.0 collective-permute-done.7.other_ref
  139.2 8.0 %all-to-all-done.2.act_ref = bf16[4,2,256,128]{3,2,1,0:T(8,128)(2,1)S(1)} async-done(((bf16[4,2,256,128]{3,2,1,0:T(8,128)(2,1)}), bf16[4,2,256,128]{3,2,1,0:T(8,128)(2,1)S(1)}, u32[]{:S(2)}, u32[]{:S(2)}) %all-to-all-start.2) | async-done | bytes 524320 | tf_op jit(solution)/shard_map/all_to_all | solution.py:223
  147.2 1.2 down.1
  148.5 68.3 %all_to_all.20.back_ref = bf16[32,8,1024]{2,1,0:T(8,128)(2,1)S(1)} all-to-all(bf16[32,8,1024]{2,1,0:T(8,128)(2,1)S(1)} %bitcast.21), channel_id=1, replica_groups={{0,120,240,104,224,88,208,72,192,56,176,40,160,24,144,8,128,248,112,232..., dimensions={0} | all-to-all | bytes 1048576 | tf_op jit(solution)/shard_map/all_to_all | solution.py:218
  216.7 0.0 copy-done
  216.7 1.0 combine.1
  (1 shorter events, 0.0 us)
Async XLA Ops:
  3.4 107.8 %all-to-all-start = ((bf16[32,8,1024]{2,1,0:T(8,128)(2,1)}), bf16[32,8,1024]{2,1,0:T(8,128)(2,1)S(1)}, u32[]{:S(2)}, u32[]{:S(2)}) async-start(bf16[32,8,1024]{2,1,0:T(8,128)(2,1)} %get-tuple-element.7), calls=%async_computation | async-start | bytes 1048576 | tf_op jit(solution)/shard_map/all_to_all | solution.py:218
  51.0 17.0 %collective-permute-start = (bf16[2,1024,128]{2,1,0:T(8,128)(2,1)S(1)}, bf16[2,1024,128]{2,1,0:T(8,128)(2,1)S(1)}, u32[]{:S(2)}, u32[]{:S(2)}) collective-permute-start(bf16[2,1024,128]{2,1,0:T(8,128)(2,1)S(1)} %pad_maximum_fusion.2), channel_id=1, source_target_pairs={{0,1},{1,2},{2,3},{3,0},{4,5},{5,6},{6,7},{7,4},{8,9},{9,10},{10,1... | collective-permute-start | bytes 1572872 | tf_op jit(solution)/shard_map/ppermute | solution.py:212
  54.6 25.6 %collective-permute-start.1 = (bf16[2,1024,128]{2,1,0:T(8,128)(2,1)S(1)}, bf16[2,1024,128]{2,1,0:T(8,128)(2,1)S(1)}, u32[]{:S(2)}, u32[]{:S(2)}) collective-permute-start(bf16[2,1024,128]{2,1,0:T(8,128)(2,1)S(1)} %pad_maximum_fusion.3), channel_id=1, source_target_pairs={{0,2},{1,3},{2,0},{3,1},{4,6},{5,7},{6,4},{7,5},{8,10},{9,11},{10,... | collective-permute-start | bytes 1572872 | tf_op jit(solution)/shard_map/ppermute | solution.py:212
  59.6 22.0 %collective-permute-start.2 = (bf16[2,1024,128]{2,1,0:T(8,128)(2,1)S(1)}, bf16[2,1024,128]{2,1,0:T(8,128)(2,1)S(1)}, u32[]{:S(2)}, u32[]{:S(2)}) collective-permute-start(bf16[2,1024,128]{2,1,0:T(8,128)(2,1)S(1)} %pad_maximum_fusion.4), channel_id=1, source_target_pairs={{0,3},{1,0},{2,1},{3,2},{4,7},{5,4},{6,5},{7,6},{8,11},{9,8},{10,9... | collective-permute-start | bytes 1572872 | tf_op jit(solution)/shard_map/ppermute | solution.py:212
  81.7 2.4 %copy-start.1 = (bf16[1,128,4096]{2,1,0:T(8,128)(2,1)S(1)}, bf16[1,128,4096]{2,1,0:T(8,128)(2,1)}, u32[]{:S(2)}) copy-start(bf16[1,128,4096]{2,1,0:T(8,128)(2,1)} %param.11) | copy-start | bytes 3145732
  81.9 14.5 %collective-permute-start.3 = (bf16[4,2,1024,128]{3,2,1,0:T(8,128)(2,1)S(1)}, bf16[4,2,1024,128]{3,2,1,0:T(8,128)(2,1)}, u32[]{:S(2)}, u32[]{:S(2)}) collective-permute-start(bf16[4,2,1024,128]{3,2,1,0:T(8,128)(2,1)S(1)} %pad_maximum_fusion.own_ref), channel_id=1, source_target_pairs={{0,4},{4,0},{8,12},{12,8},{16,20},{20,16},{24,28},{28,24},{32,36},... | collective-permute-start | bytes 6291464 | tf_op jit(solution)/shard_map/ppermute | solution.py:215
  84.9 35.2 %collective-permute-start.4 = (bf16[128,1024]{1,0:T(8,128)(2,1)}, bf16[128,1024]{1,0:T(8,128)(2,1)}, u32[]{:S(2)}, u32[]{:S(2)}) collective-permute-start(bf16[128,1024]{1,0:T(8,128)(2,1)} %get-tuple-element.10), channel_id=1, source_target_pairs={{0,1},{1,2},{2,3},{3,0},{4,5},{5,6},{6,7},{7,4},{8,9},{9,10},{10,1... | collective-permute-start | bytes 786440 | tf_op jit(solution)/shard_map/ppermute | solution.py:212
  89.2 30.9 %collective-permute-start.5 = (bf16[128,1024]{1,0:T(8,128)(2,1)S(1)}, bf16[128,1024]{1,0:T(8,128)(2,1)}, u32[]{:S(2)}, u32[]{:S(2)}) collective-permute-start(bf16[128,1024]{1,0:T(8,128)(2,1)S(1)} %get-tuple-element.12), channel_id=1, source_target_pairs={{0,2},{1,3},{2,0},{3,1},{4,6},{5,7},{6,4},{7,5},{8,10},{9,11},{10,... | collective-permute-start | bytes 786440 | tf_op jit(solution)/shard_map/ppermute | solution.py:212
  92.8 27.3 %collective-permute-start.6 = (bf16[128,1024]{1,0:T(8,128)(2,1)S(1)}, bf16[128,1024]{1,0:T(8,128)(2,1)}, u32[]{:S(2)}, u32[]{:S(2)}) collective-permute-start(bf16[128,1024]{1,0:T(8,128)(2,1)S(1)} %get-tuple-element.11), channel_id=1, source_target_pairs={{0,3},{1,0},{2,1},{3,2},{4,7},{5,4},{6,5},{7,6},{8,11},{9,8},{10,9... | collective-permute-start | bytes 786440 | tf_op jit(solution)/shard_map/ppermute | solution.py:212
  115.5 19.2 %all-to-all-start.1 = ((bf16[4,256,512]{2,1,0:T(8,128)(2,1)}), bf16[4,256,512]{2,1,0:T(8,128)(2,1)S(1)}, u32[]{:S(2)}, u32[]{:S(2)}) async-start(bf16[4,256,512]{2,1,0:T(8,128)(2,1)} %partial.1), calls=%async_computation.1 | async-start | bytes 2097152 | tf_op jit(solution)/shard_map/all_to_all | solution.py:223
  121.3 17.9 %collective-permute-start.7 = (bf16[4,128,1024]{2,1,0:T(8,128)(2,1)S(1)}, bf16[4,128,1024]{2,1,0:T(8,128)(2,1)S(1)}, u32[]{:S(2)}, u32[]{:S(2)}) collective-permute-start(bf16[4,128,1024]{2,1,0:T(8,128)(2,1)S(1)} %pad_maximum_fusion.1.own_ref), channel_id=1, source_target_pairs={{0,4},{4,0},{8,12},{12,8},{16,20},{20,16},{24,28},{28,24},{32,36},... | collective-permute-start | bytes 3145736 | tf_op jit(solution)/shard_map/ppermute | solution.py:215
  135.6 11.6 %all-to-all-start.2 = ((bf16[4,2,256,128]{3,2,1,0:T(8,128)(2,1)}), bf16[4,2,256,128]{3,2,1,0:T(8,128)(2,1)S(1)}, u32[]{:S(2)}, u32[]{:S(2)}) async-start(bf16[4,2,256,128]{3,2,1,0:T(8,128)(2,1)} %act.1), calls=%async_computation.2 | async-start | bytes 1048576 | tf_op jit(solution)/shard_map/all_to_all | solution.py:223
  139.2 77.5 %copy-start = (f32[256,16]{1,0:T(8,128)S(1)}, f32[256,16]{1,0:T(8,128)}, u32[]{:S(2)}) copy-start(f32[256,16]{1,0:T(8,128)} %get-tuple-element.8.weight_ref) | copy-start | bytes 49156

commit v6 on v4

--- a/solution.py
+++ b/solution.py
@@ -77,22 +77,17 @@
     )(x, ids, scores, tokens)
 
 
-def partial_kernel(at_ref, rows_ref, own_ref, other_hbm, out_hbm, other_ref, out_ref, sem, sems):
-    fetch = pltpu.make_async_copy(other_hbm, other_ref, sem)
-    fetch.start()
+def partial_kernel(at_ref, rows_ref, own_ref, other_hbm, out_hbm, other_ref, out_ref, fetch_sems, sems):
+    blocks = own_ref.shape[0]
+    fetches = [pltpu.make_async_copy(other_hbm.at[s], other_ref.at[s], fetch_sems.at[s]) for s in range(blocks)]
+    for fetch in fetches:
+        fetch.start()
     rows = rows_ref[...]
-    blocks, _, _, width = own_ref.shape
-
-    def product(weights_ref, s):
-        weights = jnp.concatenate([weights_ref[s, i] for i in range(2)], axis=1)
-        return jnp.dot(rows, weights, preferred_element_type=F32).astype(BF)
-
-    for s in range(blocks):
-        out_ref[s, :, : 2 * width] = product(own_ref, s)
-    fetch.wait()
     stores = []
     for s in range(blocks):
-        out_ref[s, :, 2 * width :] = product(other_ref, s)
+        fetches[s].wait()
+        weights = jnp.concatenate([r[s, i] for r in (own_ref, other_ref) for i in range(2)], axis=1)
+        out_ref[s] = jnp.dot(rows, weights, preferred_element_type=F32).astype(BF)
         stores.append(pltpu.make_async_copy(out_ref.at[s], out_hbm.at[at_ref[s]], sems.at[s]))
         stores[-1].start()
     for store in stores:
@@ -115,7 +110,7 @@
         scratch_shapes=[
             pltpu.VMEM(other.shape, BF),
             pltpu.VMEM(shape, BF),
-            pltpu.SemaphoreType.DMA,
+            pltpu.SemaphoreType.DMA((blocks,)),
             pltpu.SemaphoreType.DMA((blocks,)),
         ],
         compiler_params=pltpu.CompilerParams(vmem_limit_bytes=24 << 20),

time: 216 us -> 216 us (level)
  no operation moved by 1% of the time
where the time goes in v6:
time: 216 us
  starting transfers between devices  80.6 us (37%)
  blocking collectives  66 us (31%)
  waiting for transfers between devices  55.1 us (26%)
  Pallas kernels  9.49 us (4%)
  local copies, waits for them, and re-layouts  2.48 us (1%)
    all_to_all x1, blocking collectives, exchanged(): lax.all_to_all(v, 'expert', split_axis=0, concat_axis=0, tiled=True, axis...  66 us
    all_to_all x1, starting transfers between devices, exchanged(): lax.all_to_all(v, 'expert', split_axis=0, concat_axis=0, tiled=True, axis...  45.8 us
    ppermute x6, starting transfers between devices, turned(): lax.ppermute(v, 'hidden', [(i, (i + s) % columns) for i in range(columns)])  22.7 us
    all_to_all x2, waiting for transfers between devices, over_columns(): return lax.all_to_all(v, 'hidden', split_axis=0, concat_axis=0, tiled=True)  19.9 us
    ppermute x6, waiting for transfers between devices, turned(): lax.ppermute(v, 'hidden', [(i, (i + s) % columns) for i in range(columns)])  18.7 us
    all_to_all x1, waiting for transfers between devices, exchanged(): lax.all_to_all(v, 'expert', split_axis=0, concat_axis=0, tiled=True, axis...  16.5 us
    all_to_all x2, starting transfers between devices, over_columns(): return lax.all_to_all(v, 'hidden', split_axis=0, concat_axis=0, tiled=True)  8.13 us
  transfers between devices with their start and end apart: 11, of which 6 were waited for; matrix products, arithmetic and copies ran while one was open for 2% of the time, Pallas kernels for 2%

profile of v6, /device:TPU:40, one launch (start us, length us, event | category | flops | bytes accessed | tf_op | source)
XLA Modules:
  0.0 215.7 jit_solution(12205298117529022090)
XLA Ops:
  0.0 2.2 %pack.1 = (bf16[32,8,1024]{2,1,0:T(8,128)(2,1)}, f32[256,16]{1,0:T(8,128)}) custom-call(s32[1]{0:T(128)} %bitcast.x_ref, s32[8,16]{1,0:T(8,128)} %bitcast.24, f32[8,16]{1,0:T(8,128)} %bitcast.25, bf16[16,4096]{1,0:T(8,128)(2,1)} %tok_hbm.1), custom_call_target="tpu_custom_call" | custom-call | tf_op jit(solution)/shard_map/pack/pallas_call | solution.py:62
  2.2 45.8 %all-to-all-start = ((bf16[32,8,1024]{2,1,0:T(8,128)(2,1)}), bf16[32,8,1024]{2,1,0:T(8,128)(2,1)S(1)}, u32[]{:S(2)}, u32[]{:S(2)}) async-start(bf16[32,8,1024]{2,1,0:T(8,128)(2,1)} %get-tuple-element.7), calls=%async_computation | async-start | bytes 1048576 | tf_op jit(solution)/shard_map/all_to_all | solution.py:211
  48.0 1.7 constant_dynamic-slice_fusion.7
  49.7 0.1 pad_maximum_fusion.2
  49.7 3.6 %collective-permute-start = (bf16[2,1024,128]{2,1,0:T(8,128)(2,1)S(1)}, bf16[2,1024,128]{2,1,0:T(8,128)(2,1)S(1)}, u32[]{:S(2)}, u32[]{:S(2)}) collective-permute-start(bf16[2,1024,128]{2,1,0:T(8,128)(2,1)S(1)} %pad_maximum_fusion.2), channel_id=1, source_target_pairs={{0,1},{1,2},{2,3},{3,0},{4,5},{5,6},{6,7},{7,4},{8,9},{9,10},{10,1... | collective-permute-start | bytes 1572872 | tf_op jit(solution)/shard_map/ppermute | solution.py:205
  53.3 0.1 pad_maximum_fusion.3
  53.4 4.9 %collective-permute-start.1 = (bf16[2,1024,128]{2,1,0:T(8,128)(2,1)S(1)}, bf16[2,1024,128]{2,1,0:T(8,128)(2,1)S(1)}, u32[]{:S(2)}, u32[]{:S(2)}) collective-permute-start(bf16[2,1024,128]{2,1,0:T(8,128)(2,1)S(1)} %pad_maximum_fusion.3), channel_id=1, source_target_pairs={{0,2},{1,3},{2,0},{3,1},{4,6},{5,7},{6,4},{7,5},{8,10},{9,11},{10,... | collective-permute-start | bytes 1572872 | tf_op jit(solution)/shard_map/ppermute | solution.py:205
  58.3 0.1 pad_maximum_fusion.4
  58.4 3.2 %collective-permute-start.2 = (bf16[2,1024,128]{2,1,0:T(8,128)(2,1)S(1)}, bf16[2,1024,128]{2,1,0:T(8,128)(2,1)S(1)}, u32[]{:S(2)}, u32[]{:S(2)}) collective-permute-start(bf16[2,1024,128]{2,1,0:T(8,128)(2,1)S(1)} %pad_maximum_fusion.4), channel_id=1, source_target_pairs={{0,3},{1,0},{2,1},{3,2},{4,7},{5,4},{6,5},{7,6},{8,11},{9,8},{10,9... | collective-permute-start | bytes 1572872 | tf_op jit(solution)/shard_map/ppermute | solution.py:205
  61.6 0.1 maximum_bitcast_fusion
  61.7 5.0 %collective-permute-done = bf16[2,1024,128]{2,1,0:T(8,128)(2,1)S(1)} collective-permute-done((bf16[2,1024,128]{2,1,0:T(8,128)(2,1)S(1)}, bf16[2,1024,128]{2,1,0:T(8,128)(2,1)S(1)}, u32[]{:S(2)}, u32[]{:S(2)}) %collective-permute-start) | collective-permute-done | bytes 524320 | tf_op jit(solution)/shard_map/ppermute | solution.py:205
  66.7 12.2 %collective-permute-done.1 = bf16[2,1024,128]{2,1,0:T(8,128)(2,1)S(1)} collective-permute-done((bf16[2,1024,128]{2,1,0:T(8,128)(2,1)S(1)}, bf16[2,1024,128]{2,1,0:T(8,128)(2,1)S(1)}, u32[]{:S(2)}, u32[]{:S(2)}) %collective-permute-start.1) | collective-permute-done | bytes 524320 | tf_op jit(solution)/shard_map/ppermute | solution.py:205
  79.0 1.5 collective-permute-done.2
  80.4 0.0 copy-start.1
  80.4 0.3 pad_maximum_fusion.own_ref
  80.7 2.1 collective-permute-start.3
  82.8 0.0 copy-done.1
  82.8 0.8 constant_dynamic-slice_fusion
  83.6 5.0 %collective-permute-start.5 = (bf16[128,1024]{1,0:T(8,128)(2,1)}, bf16[128,1024]{1,0:T(8,128)(2,1)}, u32[]{:S(2)}, u32[]{:S(2)}) collective-permute-start(bf16[128,1024]{1,0:T(8,128)(2,1)} %get-tuple-element.12), channel_id=1, source_target_pairs={{0,2},{1,3},{2,0},{3,1},{4,6},{5,7},{6,4},{7,5},{8,10},{9,11},{10,... | collective-permute-start | bytes 786440 | tf_op jit(solution)/shard_map/ppermute | solution.py:205
  88.6 4.0 %collective-permute-start.6 = (bf16[128,1024]{1,0:T(8,128)(2,1)S(1)}, bf16[128,1024]{1,0:T(8,128)(2,1)}, u32[]{:S(2)}, u32[]{:S(2)}) collective-permute-start(bf16[128,1024]{1,0:T(8,128)(2,1)S(1)} %get-tuple-element.11), channel_id=1, source_target_pairs={{0,3},{1,0},{2,1},{3,2},{4,7},{5,4},{6,5},{7,6},{8,11},{9,8},{10,9... | collective-permute-start | bytes 786440 | tf_op jit(solution)/shard_map/ppermute | solution.py:205
  92.6 2.0 collective-permute-start.4
  94.5 0.0 collective-permute-done.3.other_hbm
  94.6 16.5 %all-to-all-done = bf16[32,8,1024]{2,1,0:T(8,128)(2,1)S(1)} async-done(((bf16[32,8,1024]{2,1,0:T(8,128)(2,1)}), bf16[32,8,1024]{2,1,0:T(8,128)(2,1)S(1)}, u32[]{:S(2)}, u32[]{:S(2)}) %all-to-all-start) | async-done | bytes 524320 | tf_op jit(solution)/shard_map/all_to_all | solution.py:211
  111.0 4.1 %partial.1 = bf16[4,256,512]{2,1,0:T(8,128)(2,1)} custom-call(s32[4]{0:T(128)S(1)} %and_select_fusion.at_ref, bf16[256,1024]{1,0:T(8,128)(2,1)S(1)} %bitcast.19, bf16[4,2,1024,128]{3,2,1,0:T(8,128)(2,1)S(1)} %pad_maximum_fusion.own_ref, bf16[4,2,1024,128]{3,2,1,0:T(8,128)(2,1)} %collective-permute-done.3.other_hbm), custom_call_target="tpu_custom_call" | custom-call | tf_op jit(solution)/shard_map/partial/pallas_call | solution.py:100
  115.2 4.6 %all-to-all-start.1 = ((bf16[4,256,512]{2,1,0:T(8,128)(2,1)}), bf16[4,256,512]{2,1,0:T(8,128)(2,1)S(1)}, u32[]{:S(2)}, u32[]{:S(2)}) async-start(bf16[4,256,512]{2,1,0:T(8,128)(2,1)} %partial.1), calls=%async_computation.1 | async-start | bytes 2097152 | tf_op jit(solution)/shard_map/all_to_all | solution.py:216
  119.7 0.0 collective-permute-done.5
  119.8 0.0 collective-permute-done.6
  119.8 0.0 collective-permute-done.4
  119.8 1.2 pad_maximum_fusion.1.own_ref
  121.0 2.0 collective-permute-start.7
  123.0 11.6 %all-to-all-done.1.parts_ref = bf16[4,256,512]{2,1,0:T(8,128)(2,1)S(1)} async-done(((bf16[4,256,512]{2,1,0:T(8,128)(2,1)}), bf16[4,256,512]{2,1,0:T(8,128)(2,1)S(1)}, u32[]{:S(2)}, u32[]{:S(2)}) %all-to-all-start.1) | async-done | bytes 1048608 | tf_op jit(solution)/shard_map/all_to_all | solution.py:216
  134.6 1.0 act.1
  135.6 3.6 %all-to-all-start.2 = ((bf16[4,2,256,128]{3,2,1,0:T(8,128)(2,1)}), bf16[4,2,256,128]{3,2,1,0:T(8,128)(2,1)S(1)}, u32[]{:S(2)}, u32[]{:S(2)}) async-start(bf16[4,2,256,128]{3,2,1,0:T(8,128)(2,1)} %act.1), calls=%async_computation.2 | async-start | bytes 1048576 | tf_op jit(solution)/shard_map/all_to_all | solution.py:216
  139.2 0.0 copy-start
  139.2 0.0 collective-permute-done.7.other_ref
  139.2 8.3 %all-to-all-done.2.act_ref = bf16[4,2,256,128]{3,2,1,0:T(8,128)(2,1)S(1)} async-done(((bf16[4,2,256,128]{3,2,1,0:T(8,128)(2,1)}), bf16[4,2,256,128]{3,2,1,0:T(8,128)(2,1)S(1)}, u32[]{:S(2)}, u32[]{:S(2)}) %all-to-all-start.2) | async-done | bytes 524320 | tf_op jit(solution)/shard_map/all_to_all | solution.py:216
  147.5 1.2 down.1
  148.7 66.0 %all_to_all.20.back_ref = bf16[32,8,1024]{2,1,0:T(8,128)(2,1)S(1)} all-to-all(bf16[32,8,1024]{2,1,0:T(8,128)(2,1)S(1)} %bitcast.20), channel_id=1, replica_groups={{0,120,240,104,224,88,208,72,192,56,176,40,160,24,144,8,128,248,112,232..., dimensions={0} | all-to-all | bytes 1048576 | tf_op jit(solution)/shard_map/all_to_all | solution.py:211
  214.7 0.0 copy-done
  214.7 1.0 combine.1
  (1 shorter events, 0.0 us)
Async XLA Ops:
  2.2 108.9 %all-to-all-start = ((bf16[32,8,1024]{2,1,0:T(8,128)(2,1)}), bf16[32,8,1024]{2,1,0:T(8,128)(2,1)S(1)}, u32[]{:S(2)}, u32[]{:S(2)}) async-start(bf16[32,8,1024]{2,1,0:T(8,128)(2,1)} %get-tuple-element.7), calls=%async_computation | async-start | bytes 1048576 | tf_op jit(solution)/shard_map/all_to_all | solution.py:211
  49.7 17.0 %collective-permute-start = (bf16[2,1024,128]{2,1,0:T(8,128)(2,1)S(1)}, bf16[2,1024,128]{2,1,0:T(8,128)(2,1)S(1)}, u32[]{:S(2)}, u32[]{:S(2)}) collective-permute-start(bf16[2,1024,128]{2,1,0:T(8,128)(2,1)S(1)} %pad_maximum_fusion.2), channel_id=1, source_target_pairs={{0,1},{1,2},{2,3},{3,0},{4,5},{5,6},{6,7},{7,4},{8,9},{9,10},{10,1... | collective-permute-start | bytes 1572872 | tf_op jit(solution)/shard_map/ppermute | solution.py:205
  53.4 25.6 %collective-permute-start.1 = (bf16[2,1024,128]{2,1,0:T(8,128)(2,1)S(1)}, bf16[2,1024,128]{2,1,0:T(8,128)(2,1)S(1)}, u32[]{:S(2)}, u32[]{:S(2)}) collective-permute-start(bf16[2,1024,128]{2,1,0:T(8,128)(2,1)S(1)} %pad_maximum_fusion.3), channel_id=1, source_target_pairs={{0,2},{1,3},{2,0},{3,1},{4,6},{5,7},{6,4},{7,5},{8,10},{9,11},{10,... | collective-permute-start | bytes 1572872 | tf_op jit(solution)/shard_map/ppermute | solution.py:205
  58.4 22.0 %collective-permute-start.2 = (bf16[2,1024,128]{2,1,0:T(8,128)(2,1)S(1)}, bf16[2,1024,128]{2,1,0:T(8,128)(2,1)S(1)}, u32[]{:S(2)}, u32[]{:S(2)}) collective-permute-start(bf16[2,1024,128]{2,1,0:T(8,128)(2,1)S(1)} %pad_maximum_fusion.4), channel_id=1, source_target_pairs={{0,3},{1,0},{2,1},{3,2},{4,7},{5,4},{6,5},{7,6},{8,11},{9,8},{10,9... | collective-permute-start | bytes 1572872 | tf_op jit(solution)/shard_map/ppermute | solution.py:205
  80.4 2.4 %copy-start.1 = (bf16[1,128,4096]{2,1,0:T(8,128)(2,1)S(1)}, bf16[1,128,4096]{2,1,0:T(8,128)(2,1)}, u32[]{:S(2)}) copy-start(bf16[1,128,4096]{2,1,0:T(8,128)(2,1)} %param.11) | copy-start | bytes 3145732
  80.7 13.9 %collective-permute-start.3 = (bf16[4,2,1024,128]{3,2,1,0:T(8,128)(2,1)S(1)}, bf16[4,2,1024,128]{3,2,1,0:T(8,128)(2,1)}, u32[]{:S(2)}, u32[]{:S(2)}) collective-permute-start(bf16[4,2,1024,128]{3,2,1,0:T(8,128)(2,1)S(1)} %pad_maximum_fusion.own_ref), channel_id=1, source_target_pairs={{0,4},{4,0},{8,12},{12,8},{16,20},{20,16},{24,28},{28,24},{32,36},... | collective-permute-start | bytes 6291464 | tf_op jit(solution)/shard_map/ppermute | solution.py:208
  83.6 36.2 %collective-permute-start.5 = (bf16[128,1024]{1,0:T(8,128)(2,1)}, bf16[128,1024]{1,0:T(8,128)(2,1)}, u32[]{:S(2)}, u32[]{:S(2)}) collective-permute-start(bf16[128,1024]{1,0:T(8,128)(2,1)} %get-tuple-element.12), channel_id=1, source_target_pairs={{0,2},{1,3},{2,0},{3,1},{4,6},{5,7},{6,4},{7,5},{8,10},{9,11},{10,... | collective-permute-start | bytes 786440 | tf_op jit(solution)/shard_map/ppermute | solution.py:205
  88.6 31.2 %collective-permute-start.6 = (bf16[128,1024]{1,0:T(8,128)(2,1)S(1)}, bf16[128,1024]{1,0:T(8,128)(2,1)}, u32[]{:S(2)}, u32[]{:S(2)}) collective-permute-start(bf16[128,1024]{1,0:T(8,128)(2,1)S(1)} %get-tuple-element.11), channel_id=1, source_target_pairs={{0,3},{1,0},{2,1},{3,2},{4,7},{5,4},{6,5},{7,6},{8,11},{9,8},{10,9... | collective-permute-start | bytes 786440 | tf_op jit(solution)/shard_map/ppermute | solution.py:205
  92.6 27.2 %collective-permute-start.4 = (bf16[128,1024]{1,0:T(8,128)(2,1)S(1)}, bf16[128,1024]{1,0:T(8,128)(2,1)}, u32[]{:S(2)}, u32[]{:S(2)}) collective-permute-start(bf16[128,1024]{1,0:T(8,128)(2,1)S(1)} %get-tuple-element.10), channel_id=1, source_target_pairs={{0,1},{1,2},{2,3},{3,0},{4,5},{5,6},{6,7},{7,4},{8,9},{9,10},{10,1... | collective-permute-start | bytes 786440 | tf_op jit(solution)/shard_map/ppermute | solution.py:205
  115.2 19.4 %all-to-all-start.1 = ((bf16[4,256,512]{2,1,0:T(8,128)(2,1)}), bf16[4,256,512]{2,1,0:T(8,128)(2,1)S(1)}, u32[]{:S(2)}, u32[]{:S(2)}) async-start(bf16[4,256,512]{2,1,0:T(8,128)(2,1)} %partial.1), calls=%async_computation.1 | async-start | bytes 2097152 | tf_op jit(solution)/shard_map/all_to_all | solution.py:216
  121.0 18.2 %collective-permute-start.7 = (bf16[4,128,1024]{2,1,0:T(8,128)(2,1)S(1)}, bf16[4,128,1024]{2,1,0:T(8,128)(2,1)S(1)}, u32[]{:S(2)}, u32[]{:S(2)}) collective-permute-start(bf16[4,128,1024]{2,1,0:T(8,128)(2,1)S(1)} %pad_maximum_fusion.1.own_ref), channel_id=1, source_target_pairs={{0,4},{4,0},{8,12},{12,8},{16,20},{20,16},{24,28},{28,24},{32,36},... | collective-permute-start | bytes 3145736 | tf_op jit(solution)/shard_map/ppermute | solution.py:208
  135.6 11.9 %all-to-all-start.2 = ((bf16[4,2,256,128]{3,2,1,0:T(8,128)(2,1)}), bf16[4,2,256,128]{3,2,1,0:T(8,128)(2,1)S(1)}, u32[]{:S(2)}, u32[]{:S(2)}) async-start(bf16[4,2,256,128]{3,2,1,0:T(8,128)(2,1)} %act.1), calls=%async_computation.2 | async-start | bytes 1048576 | tf_op jit(solution)/shard_map/all_to_all | solution.py:216
  139.2 75.5 %copy-start = (f32[256,16]{1,0:T(8,128)S(1)}, f32[256,16]{1,0:T(8,128)}, u32[]{:S(2)}) copy-start(f32[256,16]{1,0:T(8,128)} %get-tuple-element.8.weight_ref) | copy-start | bytes 49156

commit v7 on v6

--- a/solution.py
+++ b/solution.py
@@ -77,11 +77,14 @@
     )(x, ids, scores, tokens)
 
 
-def partial_kernel(at_ref, rows_ref, own_ref, other_hbm, out_hbm, other_ref, out_ref, fetch_sems, sems):
+def partial_kernel(at_ref, rows_hbm, own_ref, other_hbm, out_hbm, rows_ref, other_ref, out_ref, fetch_sems, sems, sem):
     blocks = own_ref.shape[0]
     fetches = [pltpu.make_async_copy(other_hbm.at[s], other_ref.at[s], fetch_sems.at[s]) for s in range(blocks)]
+    first = pltpu.make_async_copy(rows_hbm, rows_ref, sem)
+    first.start()
     for fetch in fetches:
         fetch.start()
+    first.wait()
     rows = rows_ref[...]
     stores = []
     for s in range(blocks):
@@ -102,20 +105,22 @@
         out_shape=pltpu.MemorySpace.HBM(shape, BF),
         in_specs=[
             pl.BlockSpec(memory_space=pltpu.MemorySpace.SMEM),
-            pl.BlockSpec(memory_space=VM),
+            pl.BlockSpec(memory_space=HB),
             pl.BlockSpec(memory_space=VM),
             pl.BlockSpec(memory_space=HB),
         ],
         out_specs=pl.BlockSpec(memory_space=HB),
         scratch_shapes=[
+            pltpu.VMEM(rows.shape, BF),
             pltpu.VMEM(other.shape, BF),
             pltpu.VMEM(shape, BF),
             pltpu.SemaphoreType.DMA((blocks,)),
             pltpu.SemaphoreType.DMA((blocks,)),
+            pltpu.SemaphoreType.DMA,
         ],
         compiler_params=pltpu.CompilerParams(vmem_limit_bytes=24 << 20),
         name="partial",
-    )(at, rows, own, pltpu.with_memory_space_constraint(other, pltpu.MemorySpace.HBM))
+    )(at, pltpu.with_memory_space_constraint(rows, pltpu.MemorySpace.HBM), own, pltpu.with_memory_space_constraint(other, pltpu.MemorySpace.HBM))
 
 
 def act_kernel(parts_ref, out_ref):

time: 216 us -> 218 us (level)
  transfers between devices with their start and end apart: 11 -> 11, of which waited for: 6 -> 6; matrix products, arithmetic and copies ran while one was open for 2% -> 2% of each run, Pallas kernels for 2% -> 3%
where the time goes in v7:
time: 218 us; the launch traced here: 217 us
  starting transfers between devices  80.6 us (37%)
  blocking collectives  66 us (30%)
  waiting for transfers between devices  55.1 us (25%)
  Pallas kernels  9.99 us (5%)
  local copies, waits for them, and re-layouts  3.26 us (1%)
    all_to_all x1, blocking collectives, exchanged(): lax.all_to_all(v, 'expert', split_axis=0, concat_axis=0, tiled=True, axis...  66 us
    all_to_all x1, starting transfers between devices, exchanged(): lax.all_to_all(v, 'expert', split_axis=0, concat_axis=0, tiled=True, axis...  45.8 us
    ppermute x6, starting transfers between devices, turned(): lax.ppermute(v, 'hidden', [(i, (i + s) % columns) for i in range(columns)])  22.7 us
    all_to_all x2, waiting for transfers between devices, over_columns(): return lax.all_to_all(v, 'hidden', split_axis=0, concat_axis=0, tiled=True)  19.9 us
    ppermute x6, waiting for transfers between devices, turned(): lax.ppermute(v, 'hidden', [(i, (i + s) % columns) for i in range(columns)])  18.7 us
    all_to_all x1, waiting for transfers between devices, exchanged(): lax.all_to_all(v, 'expert', split_axis=0, concat_axis=0, tiled=True, axis...  16.5 us
    all_to_all x2, starting transfers between devices, over_columns(): return lax.all_to_all(v, 'hidden', split_axis=0, concat_axis=0, tiled=True)  8.13 us
    pallas_call x1, Pallas kernels, partial_of(): pl.pallas_call(partial_kernel, out_shape=pltpu.MemorySpace.HBM(shape, BF)...  4.64 us
  transfers between devices with their start and end apart: 11, of which 6 were waited for; matrix products, arithmetic and copies ran while one was open for 2% of the time, Pallas kernels for 3%

profile of v7, /device:TPU:40, one launch (start us, length us, event | category | flops | bytes accessed | tf_op | source)
XLA Modules:
  0.0 217.0 jit_solution(13450191909842219484)
XLA Ops:
  0.0 2.2 pack.1
  2.2 45.8 %all-to-all-start = ((bf16[32,8,1024]{2,1,0:T(8,128)(2,1)}), bf16[32,8,1024]{2,1,0:T(8,128)(2,1)S(1)}, u32[]{:S(2)}, u32[]{:S(2)}) async-start(bf16[32,8,1024]{2,1,0:T(8,128)(2,1)} %get-tuple-element.7), calls=%async_computation | async-start | bytes 1048576 | tf_op jit(solution)/shard_map/all_to_all | solution.py:216
  48.0 1.7 constant_dynamic-slice_fusion.7
  49.7 0.1 pad_maximum_fusion.2
  49.7 3.6 %collective-permute-start = (bf16[2,1024,128]{2,1,0:T(8,128)(2,1)S(1)}, bf16[2,1024,128]{2,1,0:T(8,128)(2,1)S(1)}, u32[]{:S(2)}, u32[]{:S(2)}) collective-permute-start(bf16[2,1024,128]{2,1,0:T(8,128)(2,1)S(1)} %pad_maximum_fusion.2), channel_id=1, source_target_pairs={{0,1},{1,2},{2,3},{3,0},{4,5},{5,6},{6,7},{7,4},{8,9},{9,10},{10,1... | collective-permute-start | bytes 1572872 | tf_op jit(solution)/shard_map/ppermute | solution.py:210
  53.3 0.1 pad_maximum_fusion.3
  53.4 4.9 %collective-permute-start.1 = (bf16[2,1024,128]{2,1,0:T(8,128)(2,1)S(1)}, bf16[2,1024,128]{2,1,0:T(8,128)(2,1)S(1)}, u32[]{:S(2)}, u32[]{:S(2)}) collective-permute-start(bf16[2,1024,128]{2,1,0:T(8,128)(2,1)S(1)} %pad_maximum_fusion.3), channel_id=1, source_target_pairs={{0,2},{1,3},{2,0},{3,1},{4,6},{5,7},{6,4},{7,5},{8,10},{9,11},{10,... | collective-permute-start | bytes 1572872 | tf_op jit(solution)/shard_map/ppermute | solution.py:210
  58.3 0.1 pad_maximum_fusion.4
  58.4 3.2 %collective-permute-start.2 = (bf16[2,1024,128]{2,1,0:T(8,128)(2,1)S(1)}, bf16[2,1024,128]{2,1,0:T(8,128)(2,1)S(1)}, u32[]{:S(2)}, u32[]{:S(2)}) collective-permute-start(bf16[2,1024,128]{2,1,0:T(8,128)(2,1)S(1)} %pad_maximum_fusion.4), channel_id=1, source_target_pairs={{0,3},{1,0},{2,1},{3,2},{4,7},{5,4},{6,5},{7,6},{8,11},{9,8},{10,9... | collective-permute-start | bytes 1572872 | tf_op jit(solution)/shard_map/ppermute | solution.py:210
  61.6 0.1 maximum_bitcast_fusion
  61.7 5.0 %collective-permute-done = bf16[2,1024,128]{2,1,0:T(8,128)(2,1)S(1)} collective-permute-done((bf16[2,1024,128]{2,1,0:T(8,128)(2,1)S(1)}, bf16[2,1024,128]{2,1,0:T(8,128)(2,1)S(1)}, u32[]{:S(2)}, u32[]{:S(2)}) %collective-permute-start) | collective-permute-done | bytes 524320 | tf_op jit(solution)/shard_map/ppermute | solution.py:210
  66.7 12.2 %collective-permute-done.1 = bf16[2,1024,128]{2,1,0:T(8,128)(2,1)S(1)} collective-permute-done((bf16[2,1024,128]{2,1,0:T(8,128)(2,1)S(1)}, bf16[2,1024,128]{2,1,0:T(8,128)(2,1)S(1)}, u32[]{:S(2)}, u32[]{:S(2)}) %collective-permute-start.1) | collective-permute-done | bytes 524320 | tf_op jit(solution)/shard_map/ppermute | solution.py:210
  79.0 1.5 collective-permute-done.2
  80.4 0.0 copy-start.2
  80.4 0.3 pad_maximum_fusion.own_ref
  80.7 2.1 collective-permute-start.3
  82.8 0.0 copy-done.2
  82.8 0.8 constant_dynamic-slice_fusion
  83.6 5.0 %collective-permute-start.5 = (bf16[128,1024]{1,0:T(8,128)(2,1)}, bf16[128,1024]{1,0:T(8,128)(2,1)}, u32[]{:S(2)}, u32[]{:S(2)}) collective-permute-start(bf16[128,1024]{1,0:T(8,128)(2,1)} %get-tuple-element.12), channel_id=1, source_target_pairs={{0,2},{1,3},{2,0},{3,1},{4,6},{5,7},{6,4},{7,5},{8,10},{9,11},{10,... | collective-permute-start | bytes 786440 | tf_op jit(solution)/shard_map/ppermute | solution.py:210
  88.6 4.0 %collective-permute-start.6 = (bf16[128,1024]{1,0:T(8,128)(2,1)S(1)}, bf16[128,1024]{1,0:T(8,128)(2,1)}, u32[]{:S(2)}, u32[]{:S(2)}) collective-permute-start(bf16[128,1024]{1,0:T(8,128)(2,1)S(1)} %get-tuple-element.11), channel_id=1, source_target_pairs={{0,3},{1,0},{2,1},{3,2},{4,7},{5,4},{6,5},{7,6},{8,11},{9,8},{10,9... | collective-permute-start | bytes 786440 | tf_op jit(solution)/shard_map/ppermute | solution.py:210
  92.6 2.0 collective-permute-start.4
  94.5 0.0 collective-permute-done.3.other_hbm
  94.5 16.5 %all-to-all-done = bf16[32,8,1024]{2,1,0:T(8,128)(2,1)S(1)} async-done(((bf16[32,8,1024]{2,1,0:T(8,128)(2,1)}), bf16[32,8,1024]{2,1,0:T(8,128)(2,1)S(1)}, u32[]{:S(2)}, u32[]{:S(2)}) %all-to-all-start) | async-done | bytes 524320 | tf_op jit(solution)/shard_map/all_to_all | solution.py:216
  111.0 0.0 copy-start.1
  111.0 0.8 copy-done.1
  111.8 4.6 %partial.1 = bf16[4,256,512]{2,1,0:T(8,128)(2,1)} custom-call(s32[4]{0:T(128)S(1)} %and_select_fusion.at_ref, bf16[256,1024]{1,0:T(8,128)(2,1)} %bitcast.20, bf16[4,2,1024,128]{3,2,1,0:T(8,128)(2,1)S(1)} %pad_maximum_fusion.own_ref, bf16[4,2,1024,128]{3,2,1,0:T(8,128)(2,1)} %collective-permute-done.3.other_hbm), custom_call_target="tpu_custom_call" | custom-call | tf_op jit(solution)/shard_map/partial/pallas_call | solution.py:103
  116.5 4.6 %all-to-all-start.1 = ((bf16[4,256,512]{2,1,0:T(8,128)(2,1)}), bf16[4,256,512]{2,1,0:T(8,128)(2,1)S(1)}, u32[]{:S(2)}, u32[]{:S(2)}) async-start(bf16[4,256,512]{2,1,0:T(8,128)(2,1)} %partial.1), calls=%async_computation.1 | async-start | bytes 2097152 | tf_op jit(solution)/shard_map/all_to_all | solution.py:221
  121.1 0.0 collective-permute-done.5
  121.1 0.0 collective-permute-done.6
  121.1 0.0 collective-permute-done.4
  121.1 1.2 pad_maximum_fusion.1.own_ref
  122.3 2.0 collective-permute-start.7
  124.3 11.6 %all-to-all-done.1.parts_ref = bf16[4,256,512]{2,1,0:T(8,128)(2,1)S(1)} async-done(((bf16[4,256,512]{2,1,0:T(8,128)(2,1)}), bf16[4,256,512]{2,1,0:T(8,128)(2,1)S(1)}, u32[]{:S(2)}, u32[]{:S(2)}) %all-to-all-start.1) | async-done | bytes 1048608 | tf_op jit(solution)/shard_map/all_to_all | solution.py:221
  135.9 1.0 act.1
  136.9 3.6 %all-to-all-start.2 = ((bf16[4,2,256,128]{3,2,1,0:T(8,128)(2,1)}), bf16[4,2,256,128]{3,2,1,0:T(8,128)(2,1)S(1)}, u32[]{:S(2)}, u32[]{:S(2)}) async-start(bf16[4,2,256,128]{3,2,1,0:T(8,128)(2,1)} %act.1), calls=%async_computation.2 | async-start | bytes 1048576 | tf_op jit(solution)/shard_map/all_to_all | solution.py:221
  140.5 0.0 copy-start
  140.5 0.0 collective-permute-done.7.other_ref
  140.5 8.3 %all-to-all-done.2.act_ref = bf16[4,2,256,128]{3,2,1,0:T(8,128)(2,1)S(1)} async-done(((bf16[4,2,256,128]{3,2,1,0:T(8,128)(2,1)}), bf16[4,2,256,128]{3,2,1,0:T(8,128)(2,1)S(1)}, u32[]{:S(2)}, u32[]{:S(2)}) %all-to-all-start.2) | async-done | bytes 524320 | tf_op jit(solution)/shard_map/all_to_all | solution.py:221
  148.8 1.2 down.1
  150.0 66.0 %all_to_all.20.back_ref = bf16[32,8,1024]{2,1,0:T(8,128)(2,1)S(1)} all-to-all(bf16[32,8,1024]{2,1,0:T(8,128)(2,1)S(1)} %bitcast.19), channel_id=1, replica_groups={{0,120,240,104,224,88,208,72,192,56,176,40,160,24,144,8,128,248,112,232..., dimensions={0} | all-to-all | bytes 1048576 | tf_op jit(solution)/shard_map/all_to_all | solution.py:216
  216.0 0.0 copy-done
  216.0 1.0 combine.1
  (1 shorter events, 0.0 us)
Async XLA Ops:
  2.2 108.9 %all-to-all-start = ((bf16[32,8,1024]{2,1,0:T(8,128)(2,1)}), bf16[32,8,1024]{2,1,0:T(8,128)(2,1)S(1)}, u32[]{:S(2)}, u32[]{:S(2)}) async-start(bf16[32,8,1024]{2,1,0:T(8,128)(2,1)} %get-tuple-element.7), calls=%async_computation | async-start | bytes 1048576 | tf_op jit(solution)/shard_map/all_to_all | solution.py:216
  49.7 17.0 %collective-permute-start = (bf16[2,1024,128]{2,1,0:T(8,128)(2,1)S(1)}, bf16[2,1024,128]{2,1,0:T(8,128)(2,1)S(1)}, u32[]{:S(2)}, u32[]{:S(2)}) collective-permute-start(bf16[2,1024,128]{2,1,0:T(8,128)(2,1)S(1)} %pad_maximum_fusion.2), channel_id=1, source_target_pairs={{0,1},{1,2},{2,3},{3,0},{4,5},{5,6},{6,7},{7,4},{8,9},{9,10},{10,1... | collective-permute-start | bytes 1572872 | tf_op jit(solution)/shard_map/ppermute | solution.py:210
  53.4 25.6 %collective-permute-start.1 = (bf16[2,1024,128]{2,1,0:T(8,128)(2,1)S(1)}, bf16[2,1024,128]{2,1,0:T(8,128)(2,1)S(1)}, u32[]{:S(2)}, u32[]{:S(2)}) collective-permute-start(bf16[2,1024,128]{2,1,0:T(8,128)(2,1)S(1)} %pad_maximum_fusion.3), channel_id=1, source_target_pairs={{0,2},{1,3},{2,0},{3,1},{4,6},{5,7},{6,4},{7,5},{8,10},{9,11},{10,... | collective-permute-start | bytes 1572872 | tf_op jit(solution)/shard_map/ppermute | solution.py:210
  58.4 22.0 %collective-permute-start.2 = (bf16[2,1024,128]{2,1,0:T(8,128)(2,1)S(1)}, bf16[2,1024,128]{2,1,0:T(8,128)(2,1)S(1)}, u32[]{:S(2)}, u32[]{:S(2)}) collective-permute-start(bf16[2,1024,128]{2,1,0:T(8,128)(2,1)S(1)} %pad_maximum_fusion.4), channel_id=1, source_target_pairs={{0,3},{1,0},{2,1},{3,2},{4,7},{5,4},{6,5},{7,6},{8,11},{9,8},{10,9... | collective-permute-start | bytes 1572872 | tf_op jit(solution)/shard_map/ppermute | solution.py:210
  80.4 2.4 %copy-start.2 = (bf16[1,128,4096]{2,1,0:T(8,128)(2,1)S(1)}, bf16[1,128,4096]{2,1,0:T(8,128)(2,1)}, u32[]{:S(2)}) copy-start(bf16[1,128,4096]{2,1,0:T(8,128)(2,1)} %param.11) | copy-start | bytes 3145732
  80.7 13.9 %collective-permute-start.3 = (bf16[4,2,1024,128]{3,2,1,0:T(8,128)(2,1)S(1)}, bf16[4,2,1024,128]{3,2,1,0:T(8,128)(2,1)}, u32[]{:S(2)}, u32[]{:S(2)}) collective-permute-start(bf16[4,2,1024,128]{3,2,1,0:T(8,128)(2,1)S(1)} %pad_maximum_fusion.own_ref), channel_id=1, source_target_pairs={{0,4},{4,0},{8,12},{12,8},{16,20},{20,16},{24,28},{28,24},{32,36},... | collective-permute-start | bytes 6291464 | tf_op jit(solution)/shard_map/ppermute | solution.py:213
  83.6 37.5 %collective-permute-start.5 = (bf16[128,1024]{1,0:T(8,128)(2,1)}, bf16[128,1024]{1,0:T(8,128)(2,1)}, u32[]{:S(2)}, u32[]{:S(2)}) collective-permute-start(bf16[128,1024]{1,0:T(8,128)(2,1)} %get-tuple-element.12), channel_id=1, source_target_pairs={{0,2},{1,3},{2,0},{3,1},{4,6},{5,7},{6,4},{7,5},{8,10},{9,11},{10,... | collective-permute-start | bytes 786440 | tf_op jit(solution)/shard_map/ppermute | solution.py:210
  88.6 32.5 %collective-permute-start.6 = (bf16[128,1024]{1,0:T(8,128)(2,1)S(1)}, bf16[128,1024]{1,0:T(8,128)(2,1)}, u32[]{:S(2)}, u32[]{:S(2)}) collective-permute-start(bf16[128,1024]{1,0:T(8,128)(2,1)S(1)} %get-tuple-element.11), channel_id=1, source_target_pairs={{0,3},{1,0},{2,1},{3,2},{4,7},{5,4},{6,5},{7,6},{8,11},{9,8},{10,9... | collective-permute-start | bytes 786440 | tf_op jit(solution)/shard_map/ppermute | solution.py:210
  92.6 28.5 %collective-permute-start.4 = (bf16[128,1024]{1,0:T(8,128)(2,1)S(1)}, bf16[128,1024]{1,0:T(8,128)(2,1)}, u32[]{:S(2)}, u32[]{:S(2)}) collective-permute-start(bf16[128,1024]{1,0:T(8,128)(2,1)S(1)} %get-tuple-element.10), channel_id=1, source_target_pairs={{0,1},{1,2},{2,3},{3,0},{4,5},{5,6},{6,7},{7,4},{8,9},{9,10},{10,1... | collective-permute-start | bytes 786440 | tf_op jit(solution)/shard_map/ppermute | solution.py:210
  111.0 0.8 copy-start.1
  116.5 19.4 %all-to-all-start.1 = ((bf16[4,256,512]{2,1,0:T(8,128)(2,1)}), bf16[4,256,512]{2,1,0:T(8,128)(2,1)S(1)}, u32[]{:S(2)}, u32[]{:S(2)}) async-start(bf16[4,256,512]{2,1,0:T(8,128)(2,1)} %partial.1), calls=%async_computation.1 | async-start | bytes 2097152 | tf_op jit(solution)/shard_map/all_to_all | solution.py:221
  122.3 18.2 %collective-permute-start.7 = (bf16[4,128,1024]{2,1,0:T(8,128)(2,1)S(1)}, bf16[4,128,1024]{2,1,0:T(8,128)(2,1)S(1)}, u32[]{:S(2)}, u32[]{:S(2)}) collective-permute-start(bf16[4,128,1024]{2,1,0:T(8,128)(2,1)S(1)} %pad_maximum_fusion.1.own_ref), channel_id=1, source_target_pairs={{0,4},{4,0},{8,12},{12,8},{16,20},{20,16},{24,28},{28,24},{32,36},... | collective-permute-start | bytes 3145736 | tf_op jit(solution)/shard_map/ppermute | solution.py:213
  136.9 11.9 %all-to-all-start.2 = ((bf16[4,2,256,128]{3,2,1,0:T(8,128)(2,1)}), bf16[4,2,256,128]{3,2,1,0:T(8,128)(2,1)S(1)}, u32[]{:S(2)}, u32[]{:S(2)}) async-start(bf16[4,2,256,128]{3,2,1,0:T(8,128)(2,1)} %act.1), calls=%async_computation.2 | async-start | bytes 1048576 | tf_op jit(solution)/shard_map/all_to_all | solution.py:221
  140.5 75.5 %copy-start = (f32[256,16]{1,0:T(8,128)S(1)}, f32[256,16]{1,0:T(8,128)}, u32[]{:S(2)}) copy-start(f32[256,16]{1,0:T(8,128)} %get-tuple-element.8.weight_ref) | copy-start | bytes 49156
